TPU v7x, 32 devices: a whole 2x2x4 slice. The times are simulated.
32 devices in a mesh: fsdp: 32 (over z, y, x, core).
Axes of the slice: x: 2, y: 2, z: 4, core: 2. Of those that a mesh axis runs over, the one named last changes fastest.
Arguments:
- tokens: bfloat16 [8192, 2048], P('fsdp'), may hold values from -6 to 6
- attention_gain: bfloat16 [2048], replicated, may hold values from 0.099609375 to 1.8984375
- feedforward_gain: bfloat16 [2048], replicated, may hold values from 0.099609375 to 1.8984375
- joined_projection: bfloat16 [4096, 2048], P('fsdp'), may hold values from -0.125 to 0.125
- output_projection: bfloat16 [2048, 2048], P('fsdp'), may hold values from -0.75 to 0.75
- gate_weight: bfloat16 [8192, 2048], P('fsdp'), may hold values from -0.125 to 0.125
- up_weight: bfloat16 [8192, 2048], P('fsdp'), may hold values from -0.125 to 0.125
- down_weight: bfloat16 [8192, 2048], P('fsdp'), may hold values from -0.0625 to 0.0625
- joined_adapter_input: bfloat16 [2048, 128], P('fsdp'), may hold values from -0.125 to 0.125
- joined_adapter_output: bfloat16 [4096, 128], P('fsdp'), may hold values from -1.5 to 1.5
- output_adapter_input: bfloat16 [2048, 128], P('fsdp'), may hold values from -0.75 to 0.75
- output_adapter_output: bfloat16 [2048, 128], P('fsdp'), may hold values from -1.5 to 1.5
- gate_adapter_input: bfloat16 [2048, 128], P('fsdp'), may hold values from -0.125 to 0.125
- gate_adapter_output: bfloat16 [8192, 128], P('fsdp'), may hold values from -1.5 to 1.5
- upward_adapter_input: bfloat16 [2048, 128], P('fsdp'), may hold values from -0.125 to 0.125
- upward_adapter_output: bfloat16 [8192, 128], P('fsdp'), may hold values from -1.5 to 1.5
- down_adapter_input: bfloat16 [8192, 128], P('fsdp'), may hold values from -0.0625 to 0.0625
- down_adapter_output: bfloat16 [2048, 128], P('fsdp'), may hold values from -1.5 to 1.5
- lengths: int32 [15], replicated, may hold values from 128 to 1024, as said below
- adapter_set: int32 [15], replicated, may hold values from 0 to 7
- cotangent: bfloat16 [8192, 2048], P('fsdp'), may hold values from -6 to 6
Outputs:
- layer_output: bfloat16 [8192, 2048], P('fsdp')
- grad_tokens: float32 [8192, 2048], P('fsdp')
- grad_joined_entry: float32 [2048, 128], P('fsdp')
- grad_joined_exit: float32 [4096, 128], P('fsdp')
- grad_output_entry: float32 [2048, 128], P('fsdp')
- grad_output_exit: float32 [2048, 128], P('fsdp')
- grad_gate_entry: float32 [2048, 128], P('fsdp')
- grad_gate_exit: float32 [8192, 128], P('fsdp')
- grad_up_entry: float32 [2048, 128], P('fsdp')
- grad_up_exit: float32 [8192, 128], P('fsdp')
- grad_down_entry: float32 [8192, 128], P('fsdp')
- grad_down_exit: float32 [2048, 128], P('fsdp')
Inputs may be any that keep to these rules, and one draw needn't show every extreme that they name: `lengths`: the sequences lie end to end in stream order and fill all 8192 tokens; one sequence has exactly 1024 tokens and one exactly 128.
All inputs are finite; a program needn't handle non-finite values.
Results may differ from a plain program's by a relative error of at most 0.017.
Values may be sent and summed in bfloat16 or wider, within the bound.
A program may use at most 384 MiB of HBM per device.

v0:
```python
import math

import jax
import jax.numpy as jnp
from jax import lax
from jax.sharding import PartitionSpec as P

HEADS = 16
KV_HEADS = 8
HEAD_WIDTH = 128
ADAPTER_RANK = 16
REACH = 4


EPSILON = 1e-05
ADAPTER_SCALE = 0.5
ROTARY_BASE = 1000000.0
MASKED = -1e30


def shifted(value, axis, steps):
    count = lax.axis_size(axis)
    leading, last = (max(0, -steps), min(count, count - steps))
    return lax.ppermute(value, axis, [(source, source + steps) for source in range(leading, last)])


def project(left, right):
    return lax.dot_general(
        left, right, (((1,), (1,)), ((), ())), preferred_element_type=jnp.float32
    )


def product(left, right):
    return jnp.dot(left, right, preferred_element_type=jnp.float32)


def contract_rows(left, right):
    return lax.dot_general(
        left, right, (((0,), (0,)), ((), ())), preferred_element_type=jnp.float32
    )


def sequence_info(lengths, adapter_set, first, number):
    ends = jnp.cumsum(lengths)
    starts = ends - lengths
    index = first + lax.iota(jnp.int32, number)
    member = (index[:, None] >= starts[None, :]) & (index[:, None] < ends[None, :])
    labels = lax.iota(jnp.int32, lengths.shape[0]) + 1
    sequence = jnp.sum(jnp.where(member, labels[None, :], 0), axis=1) - 1
    begin = jnp.sum(jnp.where(member, starts[None, :], 0), axis=1)
    chosen = jnp.sum(jnp.where(member, adapter_set[None, :], 0), axis=1)
    return (sequence, index - begin, chosen)


def adapter_mask(chosen, columns):
    column_set = lax.broadcasted_iota(jnp.int32, (1, columns), 1) // ADAPTER_RANK
    return column_set == chosen[:, None]


def masked(values, select):
    return jnp.where(select, values, 0.0).astype(jnp.bfloat16)


def rotary_tables(position):
    half = HEAD_WIDTH // 2
    inverse = jnp.exp(lax.iota(jnp.float32, half) * (-2.0 * math.log(ROTARY_BASE) / HEAD_WIDTH))
    angles = position.astype(jnp.float32)[:, None] * inverse[None, :]
    return (jnp.cos(angles)[:, None, :], jnp.sin(angles)[:, None, :])


def rotate(values, cosine, sine):
    half = values.shape[-1] // 2
    first_half = values[..., :half]
    second_half = values[..., half:]
    return jnp.concatenate(
        [first_half * cosine - second_half * sine, second_half * cosine + first_half * sine],
        axis=-1,
    )


def unrotate(values, cosine, sine):
    half = values.shape[-1] // 2
    first_half = values[..., :half]
    second_half = values[..., half:]
    return jnp.concatenate(
        [first_half * cosine + second_half * sine, second_half * cosine - first_half * sine],
        axis=-1,
    )


def norm_forward(values, gain):
    scale = lax.rsqrt(jnp.mean(values * values, axis=-1, keepdims=True) + EPSILON)
    unit = values * scale
    return (unit * gain, unit, scale)


def norm_backward(grad, unit, scale, gain):
    weighted = grad * gain
    return scale * (weighted - unit * jnp.mean(weighted * unit, axis=-1, keepdims=True))


def head_forward(query_head, key_head, value_head, allowed):
    scale = HEAD_WIDTH ** (-0.5)
    scores = (
        jnp.einsum("gqd,kd->gqk", query_head, key_head, preferred_element_type=jnp.float32) * scale
    )
    scores = jnp.where(allowed[None], scores, MASKED)
    top = jnp.max(scores, axis=-1, keepdims=True)
    weights = jnp.exp(scores - top)
    total = jnp.sum(weights, axis=-1, keepdims=True)
    probs = (weights / total).astype(jnp.bfloat16)
    result = jnp.einsum("gqk,kd->gqd", probs, value_head, preferred_element_type=jnp.float32)
    return (result, (top + jnp.log(total))[..., 0])


def head_backward(query_head, key_head, value_head, log_total, grad_head, allowed):
    scale = HEAD_WIDTH ** (-0.5)
    scores = (
        jnp.einsum("gqd,kd->gqk", query_head, key_head, preferred_element_type=jnp.float32) * scale
    )
    scores = jnp.where(allowed[None], scores, MASKED)
    probs = jnp.exp(scores - log_total[..., None])
    probs_back = jnp.einsum(
        "gqd,kd->gqk", grad_head, value_head, preferred_element_type=jnp.float32
    )
    center = jnp.sum(probs_back * probs, axis=-1, keepdims=True)
    score_back = (probs * (probs_back - center)).astype(jnp.bfloat16)
    query_back = (
        jnp.einsum("gqk,kd->gqd", score_back, key_head, preferred_element_type=jnp.float32) * scale
    )
    key_back = (
        jnp.einsum("gqk,gqd->kd", score_back, query_head, preferred_element_type=jnp.float32)
        * scale
    )
    value_back = jnp.einsum(
        "gqk,gqd->kd", probs.astype(jnp.bfloat16), grad_head, preferred_element_type=jnp.float32
    )
    return (query_back, key_back, value_back)


def per_device(
    tokens,
    attention_gain,
    feedforward_gain,
    joined_projection,
    output_projection,
    gate_weight,
    up_weight,
    down_weight,
    joined_adapter_input,
    joined_adapter_output,
    output_adapter_input,
    output_adapter_output,
    gate_adapter_input,
    gate_adapter_output,
    upward_adapter_input,
    upward_adapter_output,
    down_adapter_input,
    down_adapter_output,
    lengths,
    adapter_set,
    cotangent,
):
    number = tokens.shape[0]
    columns = joined_adapter_input.shape[1]
    attend_width = HEADS * HEAD_WIDTH
    kv_width = KV_HEADS * HEAD_WIDTH
    group = HEADS // KV_HEADS
    first = lax.axis_index("fsdp") * number
    sequence, position, chosen = sequence_info(lengths, adapter_set, first, number)
    select = adapter_mask(chosen, columns)
    cosine, sine = rotary_tables(position)
    inputs = tokens.astype(jnp.float32)
    gain_one = attention_gain.astype(jnp.float32)
    gain_two = feedforward_gain.astype(jnp.float32)
    attn_pieces = (
        joined_projection,
        output_projection,
        joined_adapter_input,
        joined_adapter_output,
        output_adapter_input,
        output_adapter_output,
        gate_adapter_input,
        upward_adapter_input,
        down_adapter_output,
    )
    attn_whole = (
        lax.all_gather(attn_pieces[0], "fsdp", axis=0, tiled=True),
        lax.all_gather(attn_pieces[1], "fsdp", axis=0, tiled=True),
        lax.all_gather(attn_pieces[2], "fsdp", axis=0, tiled=True),
        lax.all_gather(attn_pieces[3], "fsdp", axis=0, tiled=True),
        lax.all_gather(attn_pieces[4], "fsdp", axis=0, tiled=True),
        lax.all_gather(attn_pieces[5], "fsdp", axis=0, tiled=True),
        lax.all_gather(attn_pieces[6], "fsdp", axis=0, tiled=True),
        lax.all_gather(attn_pieces[7], "fsdp", axis=0, tiled=True),
        lax.all_gather(attn_pieces[8], "fsdp", axis=0, tiled=True),
    )
    (
        full_joined,
        full_output,
        full_f_entry,
        full_f_exit,
        full_o_entry,
        full_o_exit,
        full_g_entry,
        full_u_entry,
        full_d_exit,
    ) = attn_whole
    normed_one, unit_one, scale_one = norm_forward(inputs, gain_one)
    normed_one = normed_one.astype(jnp.bfloat16)
    joined_low = masked(product(normed_one, full_f_entry), select)
    projected = project(normed_one, full_joined) + ADAPTER_SCALE * project(joined_low, full_f_exit)
    query = rotate(
        projected[:, :attend_width].reshape(number, HEADS, HEAD_WIDTH), cosine, sine
    ).astype(jnp.bfloat16)
    key = rotate(
        projected[:, attend_width : attend_width + kv_width].reshape(number, KV_HEADS, HEAD_WIDTH),
        cosine,
        sine,
    ).astype(jnp.bfloat16)
    value = projected[:, attend_width + kv_width :].astype(jnp.bfloat16)
    pair = jnp.stack([key.reshape(number, kv_width), value], axis=0)
    earlier = []
    for back in range(REACH, 0, -1):
        earlier.append(shifted(pair, "fsdp", back))
    context = jnp.concatenate(earlier + [pair], axis=1)
    context_key = context[0].reshape(-1, KV_HEADS, HEAD_WIDTH).transpose(1, 0, 2)
    context_value = context[1].reshape(-1, KV_HEADS, HEAD_WIDTH).transpose(1, 0, 2)
    key_first = first - REACH * number
    key_sequence, unused_position, unused_set = sequence_info(
        lengths, adapter_set, key_first, (REACH + 1) * number
    )
    key_index = key_first + lax.iota(jnp.int32, (REACH + 1) * number)
    query_index = first + lax.iota(jnp.int32, number)
    allowed = (sequence[:, None] == key_sequence[None, :]) & (
        key_index[None, :] <= query_index[:, None]
    )
    query_heads = query.reshape(number, KV_HEADS, group, HEAD_WIDTH).transpose(1, 2, 0, 3)
    head_results, log_total = lax.map(
        lambda parts: head_forward(parts[0], parts[1], parts[2], allowed),
        (query_heads, context_key, context_value),
    )
    attended = head_results.transpose(2, 0, 1, 3).reshape(number, attend_width).astype(jnp.bfloat16)
    output_low = masked(product(attended, full_o_entry), select)
    branch = project(attended, full_output) + ADAPTER_SCALE * project(output_low, full_o_exit)
    hidden_one = inputs + branch
    normed_two, unit_two, scale_two = norm_forward(hidden_one, gain_two)
    normed_two = normed_two.astype(jnp.bfloat16)
    gate_low = masked(product(normed_two, full_g_entry), select)
    up_low = masked(product(normed_two, full_u_entry), select)
    feed_pieces = (
        gate_weight,
        up_weight,
        down_weight,
        gate_adapter_output,
        upward_adapter_output,
        down_adapter_input,
    )
    piece_gate = lax.all_gather(feed_pieces[0], "fsdp", axis=0, tiled=True)
    piece_up = lax.all_gather(feed_pieces[1], "fsdp", axis=0, tiled=True)
    piece_down = lax.all_gather(feed_pieces[2], "fsdp", axis=0, tiled=True)
    piece_g_exit = lax.all_gather(feed_pieces[3], "fsdp", axis=0, tiled=True)
    piece_u_exit = lax.all_gather(feed_pieces[4], "fsdp", axis=0, tiled=True)
    piece_d_entry = lax.all_gather(feed_pieces[5], "fsdp", axis=0, tiled=True)
    gate = project(normed_two, piece_gate) + ADAPTER_SCALE * project(gate_low, piece_g_exit)
    upward = project(normed_two, piece_up) + ADAPTER_SCALE * project(up_low, piece_u_exit)
    hidden = (gate * jax.nn.sigmoid(gate) * upward).astype(jnp.bfloat16)
    feed_gate_all = gate
    feed_up_all = upward
    down_sum = product(hidden, piece_d_entry)
    mixed = product(hidden, piece_down)
    down_low = masked(down_sum, select)
    mixed = mixed + ADAPTER_SCALE * project(down_low, full_d_exit)
    layer_output = (hidden_one + mixed).astype(jnp.bfloat16)
    back_whole = (
        lax.all_gather(attn_pieces[0], "fsdp", axis=0, tiled=True),
        lax.all_gather(attn_pieces[1], "fsdp", axis=0, tiled=True),
        lax.all_gather(attn_pieces[2], "fsdp", axis=0, tiled=True),
        lax.all_gather(attn_pieces[3], "fsdp", axis=0, tiled=True),
        lax.all_gather(attn_pieces[4], "fsdp", axis=0, tiled=True),
        lax.all_gather(attn_pieces[5], "fsdp", axis=0, tiled=True),
        lax.all_gather(attn_pieces[6], "fsdp", axis=0, tiled=True),
        lax.all_gather(attn_pieces[7], "fsdp", axis=0, tiled=True),
        lax.all_gather(attn_pieces[8], "fsdp", axis=0, tiled=True),
    )
    (
        full_joined,
        full_output,
        full_f_entry,
        full_f_exit,
        full_o_entry,
        full_o_exit,
        full_g_entry,
        full_u_entry,
        full_d_exit,
    ) = back_whole
    grad_d_exit = ADAPTER_SCALE * contract_rows(cotangent, down_low)
    down_back = masked(ADAPTER_SCALE * product(cotangent, full_d_exit), select)
    piece_gate = lax.all_gather(feed_pieces[0], "fsdp", axis=0, tiled=True)
    piece_up = lax.all_gather(feed_pieces[1], "fsdp", axis=0, tiled=True)
    piece_down = lax.all_gather(feed_pieces[2], "fsdp", axis=0, tiled=True)
    piece_g_exit = lax.all_gather(feed_pieces[3], "fsdp", axis=0, tiled=True)
    piece_u_exit = lax.all_gather(feed_pieces[4], "fsdp", axis=0, tiled=True)
    piece_d_entry = lax.all_gather(feed_pieces[5], "fsdp", axis=0, tiled=True)
    gate = feed_gate_all
    upward = feed_up_all
    sigma = jax.nn.sigmoid(gate)
    activated = gate * sigma
    hidden = (activated * upward).astype(jnp.bfloat16)
    hidden_back = project(cotangent, piece_down) + project(down_back, piece_d_entry)
    gate_back = (hidden_back * upward * sigma * (1.0 + gate * (1.0 - sigma))).astype(jnp.bfloat16)
    up_back = (hidden_back * activated).astype(jnp.bfloat16)
    normed_back = product(gate_back, piece_gate) + product(up_back, piece_up)
    gate_sum = ADAPTER_SCALE * product(gate_back, piece_g_exit)
    up_sum = ADAPTER_SCALE * product(up_back, piece_u_exit)
    grad_g_exit = ADAPTER_SCALE * contract_rows(gate_back, gate_low)
    grad_u_exit = ADAPTER_SCALE * contract_rows(up_back, up_low)
    grad_d_entry = contract_rows(hidden, down_back)
    feed_back = (normed_back, gate_sum, up_sum, grad_g_exit, grad_u_exit, grad_d_entry)
    normed_two_back, gate_sum, up_sum, grad_g_exit, grad_u_exit, grad_d_entry = feed_back
    gate_low_back = masked(gate_sum, select)
    up_low_back = masked(up_sum, select)
    normed_two_back = (
        normed_two_back + project(gate_low_back, full_g_entry) + project(up_low_back, full_u_entry)
    )
    grad_g_entry = contract_rows(normed_two, gate_low_back)
    grad_u_entry = contract_rows(normed_two, up_low_back)
    hidden_back_one = cotangent.astype(jnp.float32) + norm_backward(
        normed_two_back, unit_two, scale_two, gain_two
    )
    branch_back = hidden_back_one.astype(jnp.bfloat16)
    grad_o_exit = ADAPTER_SCALE * contract_rows(branch_back, output_low)
    output_low_back = masked(ADAPTER_SCALE * product(branch_back, full_o_exit), select)
    grad_o_entry = contract_rows(attended, output_low_back)
    attended_back = (
        product(branch_back, full_output) + project(output_low_back, full_o_entry)
    ).astype(jnp.bfloat16)
    grad_heads = attended_back.reshape(number, KV_HEADS, group, HEAD_WIDTH).transpose(1, 2, 0, 3)
    query_back, key_back, value_back = lax.map(
        lambda parts: head_backward(parts[0], parts[1], parts[2], parts[3], parts[4], allowed),
        (query_heads, context_key, context_value, log_total, grad_heads),
    )
    query_back = query_back.transpose(2, 0, 1, 3).reshape(number, HEADS, HEAD_WIDTH)
    key_blocks = key_back.transpose(1, 0, 2).reshape(REACH + 1, number, kv_width)
    value_blocks = value_back.transpose(1, 0, 2).reshape(REACH + 1, number, kv_width)
    pair_back = jnp.stack([key_blocks[REACH], value_blocks[REACH]], axis=0)
    for back in range(REACH, 0, -1):
        slot = REACH - back
        outgoing = jnp.stack([key_blocks[slot], value_blocks[slot]], axis=0)
        pair_back = pair_back + shifted(outgoing.astype(jnp.bfloat16), "fsdp", -back).astype(
            outgoing.dtype
        )
    query_plain = unrotate(query_back, cosine, sine).reshape(number, attend_width)
    key_plain = unrotate(pair_back[0].reshape(number, KV_HEADS, HEAD_WIDTH), cosine, sine).reshape(
        number, kv_width
    )
    joined_back = jnp.concatenate([query_plain, key_plain, pair_back[1]], axis=1).astype(
        jnp.bfloat16
    )
    grad_f_exit = ADAPTER_SCALE * contract_rows(joined_back, joined_low)
    joined_low_back = masked(ADAPTER_SCALE * product(joined_back, full_f_exit), select)
    grad_f_entry = contract_rows(normed_one, joined_low_back)
    normed_one_back = product(joined_back, full_joined) + project(joined_low_back, full_f_entry)
    grad_tokens = hidden_back_one + norm_backward(normed_one_back, unit_one, scale_one, gain_one)
    grads = (
        grad_f_entry,
        grad_f_exit,
        grad_o_entry,
        grad_o_exit,
        grad_g_entry,
        grad_g_exit,
        grad_u_entry,
        grad_u_exit,
        grad_d_entry,
        grad_d_exit,
    )
    shards = (
        lax.psum_scatter(grads[0], "fsdp", scatter_dimension=0, tiled=True),
        lax.psum_scatter(grads[1], "fsdp", scatter_dimension=0, tiled=True),
        lax.psum_scatter(grads[2], "fsdp", scatter_dimension=0, tiled=True),
        lax.psum_scatter(grads[3], "fsdp", scatter_dimension=0, tiled=True),
        lax.psum_scatter(grads[4], "fsdp", scatter_dimension=0, tiled=True),
        lax.psum_scatter(grads[5], "fsdp", scatter_dimension=0, tiled=True),
        lax.psum_scatter(grads[6], "fsdp", scatter_dimension=0, tiled=True),
        lax.psum_scatter(grads[7], "fsdp", scatter_dimension=0, tiled=True),
        lax.psum_scatter(grads[8], "fsdp", scatter_dimension=0, tiled=True),
        lax.psum_scatter(grads[9], "fsdp", scatter_dimension=0, tiled=True),
    )
    return (
        layer_output,
        grad_tokens,
        shards[0],
        shards[1],
        shards[2],
        shards[3],
        shards[4],
        shards[5],
        shards[6],
        shards[7],
        shards[8],
        shards[9],
    )


def solution(mesh):
    placed = (
        P("fsdp", None),
        P(),
        P(),
        P("fsdp", None),
        P("fsdp", None),
        P("fsdp", None),
        P("fsdp", None),
        P("fsdp", None),
        P("fsdp", None),
        P("fsdp", None),
        P("fsdp", None),
        P("fsdp", None),
        P("fsdp", None),
        P("fsdp", None),
        P("fsdp", None),
        P("fsdp", None),
        P("fsdp", None),
        P("fsdp", None),
        P(),
        P(),
        P("fsdp", None),
    )
    return jax.shard_map(
        per_device,
        mesh=mesh,
        in_specs=placed,
        out_specs=(
            P("fsdp", None),
            P("fsdp", None),
            P("fsdp", None),
            P("fsdp", None),
            P("fsdp", None),
            P("fsdp", None),
            P("fsdp", None),
            P("fsdp", None),
            P("fsdp", None),
            P("fsdp", None),
            P("fsdp", None),
            P("fsdp", None),
        ),
        check_vma=False,
    )
```

profile of v0, /device:TPU:0, one launch (start us, length us, event | category | flops | bytes accessed | tf_op | source)
XLA Modules:
  0.0 2568.7 jit_solution(15834907596622316026)
XLA Ops:
  14.1 46.9 %all_gather.61 = bf16[2048,128]{1,0:T(8,128)(2,1)S(1)} all-gather(bf16[64,128]{1,0:T(8,128)(2,1)S(1)} %copy-done.50), channel_id=1, replica_groups=mesh['fsdp'=32] {'fsdp'}, dimensions={0}, use_global_device_ids=true | all-gather | bytes 540672 | tf_op jit(solution)/shard_map/all_gather | solution.py:190
  61.1 41.1 %all_gather.64 = bf16[2048,128]{1,0:T(8,128)(2,1)S(1)} all-gather(bf16[64,128]{1,0:T(8,128)(2,1)S(1)} %copy-done.51), channel_id=1, replica_groups=mesh['fsdp'=32] {'fsdp'}, dimensions={0}, use_global_device_ids=true | all-gather | bytes 540672 | tf_op jit(solution)/shard_map/all_gather | solution.py:192
  102.2 44.5 %all_gather.65 = bf16[2048,128]{1,0:T(8,128)(2,1)} all-gather(bf16[64,128]{1,0:T(8,128)(2,1)S(1)} %copy-done.52), channel_id=1, replica_groups=mesh['fsdp'=32] {'fsdp'}, dimensions={0}, use_global_device_ids=true | all-gather | bytes 540672 | tf_op jit(solution)/shard_map/all_gather | solution.py:193
  146.7 41.4 %all_gather.70 = bf16[2048,128]{1,0:T(8,128)(2,1)} all-gather(bf16[64,128]{1,0:T(8,128)(2,1)S(1)} %copy-done.53), channel_id=1, replica_groups=mesh['fsdp'=32] {'fsdp'}, dimensions={0}, use_global_device_ids=true | all-gather | bytes 540672 | tf_op jit(solution)/shard_map/all_gather | solution.py:195
  188.0 42.6 %all_gather.67 = bf16[2048,128]{1,0:T(8,128)(2,1)} all-gather(bf16[64,128]{1,0:T(8,128)(2,1)S(1)} %copy-done.54), channel_id=1, replica_groups=mesh['fsdp'=32] {'fsdp'}, dimensions={0}, use_global_device_ids=true | all-gather | bytes 540672 | tf_op jit(solution)/shard_map/all_gather | solution.py:194
  230.7 41.6 %all_gather.74 = bf16[2048,128]{1,0:T(8,128)(2,1)S(1)} all-gather(bf16[64,128]{1,0:T(8,128)(2,1)S(1)} %copy-done.55), channel_id=1, replica_groups=mesh['fsdp'=32] {'fsdp'}, dimensions={0}, use_global_device_ids=true | all-gather | bytes 540672 | tf_op jit(solution)/shard_map/all_gather | solution.py:196
  274.7 10.3 fusion.96
  306.0 59.9 %collective-permute-done = bf16[2,256,1024]{2,1,0:T(8,128)(2,1)} collective-permute-done((bf16[2,256,1024]{2,1,0:T(8,128)(2,1)}, bf16[2,256,1024]{2,1,0:T(8,128)(2,1)}, u32[]{:S(2)}, u32[]{:S(2)}) %collective-permute-start) | collective-permute-done | bytes 1048608 | tf_op jit(solution)/shard_map/ppermute | solution.py:24
  376.1 40.5 %while.28 = (s32[]{:T(128)}, bf16[8,2,256,128]{2,3,1,0:T(8,128)(2,1)}, f32[8,2,256]{2,1,0:T(2,128)S(1)}, bf16[8,2,256,128]{3,2,1,0:T(8,128)(2,1)S(1)}, bf16[8,12...) while((s32[]{:T(128)}, ...), condition=%wide.region_9.10_spmd.clone, body=%wide.region_6.9_spmd.clone.sunk | while | flops 341769728 | bytes 9599089 | solution.py:239
  428.0 109.1 %all-gather.20.cloned.1.call-done = bf16[8192,2048]{1,0:T(8,128)(2,1)} async-done(((bf16[256,2048]{1,0:T(8,128)(2,1)}), bf16[8192,2048]{1,0:T(8,128)(2,1)}) %all-gather.20.cloned.1.call-update) | async-done | bytes 33554448 | tf_op jit(solution)/shard_map/all_gather | solution.py:260
  537.0 17.6 fusion.105
  554.6 39.5 %all-gather.22.cloned.1.call-done = bf16[8192,128]{1,0:T(8,128)(2,1)} async-done(((bf16[256,128]{1,0:T(8,128)(2,1)}), bf16[8192,128]{1,0:T(8,128)(2,1)}) %all-gather.22.cloned.1.call-update) | async-done | bytes 2097168 | tf_op jit(solution)/shard_map/all_gather | solution.py:263
  602.7 187.2 %all-gather.16.cloned.1.call-done = bf16[8192,2048]{1,0:T(8,128)(2,1)} async-done(((bf16[256,2048]{1,0:T(8,128)(2,1)}), bf16[8192,2048]{1,0:T(8,128)(2,1)}) %all-gather.16.cloned.1.call-update) | async-done | bytes 33554448 | tf_op jit(solution)/shard_map/all_gather | solution.py:259
  789.9 17.8 fusion.104
  807.7 39.5 %all-gather.18.cloned.1.call-done = bf16[8192,128]{1,0:T(8,128)(2,1)} async-done(((bf16[256,128]{1,0:T(8,128)(2,1)}), bf16[8192,128]{1,0:T(8,128)(2,1)}) %all-gather.18.cloned.1.call-update) | async-done | bytes 2097168 | tf_op jit(solution)/shard_map/all_gather | solution.py:262
  855.9 187.2 %all-gather.24.cloned.1.call-done = bf16[8192,2048]{1,0:T(8,128)(2,1)} async-done(((bf16[256,2048]{1,0:T(8,128)(2,1)}), bf16[8192,2048]{1,0:T(8,128)(2,1)}) %all-gather.24.cloned.1.call-update) | async-done | bytes 33554448 | tf_op jit(solution)/shard_map/all_gather | solution.py:261
  1043.1 18.5 fusion.107
  1061.6 38.7 %all-gather.26.cloned.1.call-done = bf16[8192,128]{1,0:T(8,128)(2,1)} async-done(((bf16[256,128]{1,0:T(8,128)(2,1)}), bf16[8192,128]{1,0:T(8,128)(2,1)}) %all-gather.26.cloned.1.call-update) | async-done | bytes 2097168 | tf_op jit(solution)/shard_map/all_gather | solution.py:264
  1100.3 13.7 multiply_convert_fusion.1
  1114.0 18.8 fusion.108
  1136.3 17.8 convolution_add_fusion.5
  1175.5 115.9 %while.29 = (s32[]{:T(128)}, f32[8,2,256,128]{3,2,1,0:T(8,128)}, f32[8,1280,128]{1,2,0:T(8,128)}, f32[8,1280,128]{1,2,0:T(8,128)}, bf16[8,2,256,128]{3,2,1,0:T(8...) while((s32[]{:T(128)}, f32[8,2,256,128]{3,2,1,0:T(8,128)}, ...), condition=%wide.region_14.15_spmd.clone, body=%wide.region_12.14_spmd.clone.sunk | while | flops 845970944 | bytes 31288484 | solution.py:339
  1373.3 16.4 fusion.106
  1402.8 50.8 %reduce-scatter.19.cloned.1.call-done = f32[64,128]{1,0:T(8,128)} async-done(((f32[2048,128]{1,0:T(8,128)}), f32[64,128]{1,0:T(8,128)}) %reduce-scatter.19.cloned.1.call-update) | async-done | bytes 32784 | tf_op jit(solution)/shard_map/reduce_scatter | solution.py:381
  1453.7 140.3 %reduce-scatter.21.cloned.1.call-done = f32[64,128]{1,0:T(8,128)} async-done(((f32[2048,128]{1,0:T(8,128)}), f32[64,128]{1,0:T(8,128)}) %reduce-scatter.21.cloned.1.call-update) | async-done | bytes 32784 | tf_op jit(solution)/shard_map/reduce_scatter | solution.py:382
  1594.0 135.4 %reduce-scatter.25.cloned.1.call-done = f32[64,128]{1,0:T(8,128)} async-done(((f32[2048,128]{1,0:T(8,128)}), f32[64,128]{1,0:T(8,128)}) %reduce-scatter.25.cloned.1.call-update) | async-done | bytes 32784 | tf_op jit(solution)/shard_map/reduce_scatter | solution.py:384
  1729.4 135.2 %reduce-scatter.31.cloned.1.call-done = f32[64,128]{1,0:T(8,128)} async-done(((f32[2048,128]{1,0:T(8,128)}), f32[64,128]{1,0:T(8,128)}) %reduce-scatter.31.cloned.1.call-update) | async-done | bytes 32784
  1864.6 135.1 %reduce-scatter.13.cloned.1.call-done = f32[64,128]{1,0:T(8,128)} async-done(((f32[2048,128]{1,0:T(8,128)}), f32[64,128]{1,0:T(8,128)}) %reduce-scatter.13.cloned.1.call-update) | async-done | bytes 32784 | tf_op jit(solution)/shard_map/reduce_scatter | solution.py:378
  1999.7 137.0 %reduce-scatter.15.cloned.1.call-done = f32[128,128]{1,0:T(8,128)} async-done(((f32[4096,128]{1,0:T(8,128)}), f32[128,128]{1,0:T(8,128)}) %reduce-scatter.15.cloned.1.call-update) | async-done | bytes 65552 | tf_op jit(solution)/shard_map/reduce_scatter | solution.py:379
  2136.7 141.7 %reduce-scatter.23.cloned.1.call-done = f32[256,128]{1,0:T(8,128)} async-done(((f32[8192,128]{1,0:T(8,128)}), f32[256,128]{1,0:T(8,128)}) %reduce-scatter.23.cloned.1.call-update) | async-done | bytes 131088 | tf_op jit(solution)/shard_map/reduce_scatter | solution.py:383
  2278.4 141.6 %reduce-scatter.27.cloned.1.call-done = f32[256,128]{1,0:T(8,128)} async-done(((f32[8192,128]{1,0:T(8,128)}), f32[256,128]{1,0:T(8,128)}) %reduce-scatter.27.cloned.1.call-update) | async-done | bytes 131088 | tf_op jit(solution)/shard_map/reduce_scatter | solution.py:385
  2420.0 141.7 %reduce-scatter.29.cloned.1.call-done = f32[256,128]{1,0:T(8,128)} async-done(((f32[8192,128]{1,0:T(8,128)}), f32[256,128]{1,0:T(8,128)}) %reduce-scatter.29.cloned.1.call-update) | async-done | bytes 131088 | tf_op jit(solution)/shard_map/reduce_scatter | solution.py:386
  (424 shorter events, 343.4 us)
Async XLA Ops:
  7.2 267.5 %all-gather.10.cloned.1.call-start = ((), (), s32[]{:S(2)}) async-start(), calls=%async_computation.10 | async-start | bytes 17301504 | tf_op jit(solution)/shard_map/all_gather | solution.py:188
  8.0 277.0 %all-gather.12.cloned.1.call-start = ((), (), s32[]{:S(2)}) async-start(), calls=%async_computation.11 | async-start | bytes 1081344 | tf_op jit(solution)/shard_map/all_gather | solution.py:191
  8.7 410.0 %all-gather.14.cloned.1.call-start = ((), (), s32[]{:S(2)}) async-start(), calls=%async_computation.12 | async-start | bytes 8650752 | tf_op jit(solution)/shard_map/all_gather | solution.py:189
  9.5 527.6 %all-gather.20.cloned.1.call-start = ((), (), s32[]{:S(2)}) async-start(), calls=%async_computation.15 | async-start | bytes 34603008 | tf_op jit(solution)/shard_map/all_gather | solution.py:260
  10.0 584.1 %all-gather.22.cloned.1.call-start = ((), (), s32[]{:S(2)}) async-start(), calls=%async_computation.16 | async-start | bytes 2162688 | tf_op jit(solution)/shard_map/all_gather | solution.py:263
  10.6 779.2 %all-gather.16.cloned.1.call-start = ((), (), s32[]{:S(2)}) async-start(), calls=%async_computation.13 | async-start | bytes 34603008 | tf_op jit(solution)/shard_map/all_gather | solution.py:259
  11.2 835.9 %all-gather.18.cloned.1.call-start = ((), (), s32[]{:S(2)}) async-start(), calls=%async_computation.14 | async-start | bytes 2162688 | tf_op jit(solution)/shard_map/all_gather | solution.py:262
  12.0 261.1 %copy-start.12 = (bf16[256,2048]{1,0:T(8,128)(2,1)S(1)}, bf16[256,2048]{1,0:T(8,128)(2,1)}, u32[]{:S(2)}) copy-start(bf16[256,2048]{1,0:T(8,128)(2,1)} %param.45) | copy-start | bytes 3145732
  12.0 1031.1 %all-gather.24.cloned.1.call-start = ((), (), s32[]{:S(2)}) async-start(), calls=%async_computation.17 | async-start | bytes 34603008 | tf_op jit(solution)/shard_map/all_gather | solution.py:261
  12.8 1087.6 %all-gather.26.cloned.1.call-start = ((), (), s32[]{:S(2)}) async-start(), calls=%async_computation.18 | async-start | bytes 2162688 | tf_op jit(solution)/shard_map/all_gather | solution.py:264
  13.5 1389.3 %reduce-scatter.17.cloned.1.call-start = ((), (), s32[]{:S(2)}) async-start(), calls=%async_computation.21 | async-start | bytes 1081344 | tf_op jit(solution)/shard_map/reduce_scatter | solution.py:380
  102.2 314.4 %copy-start.21 = (bf16[2048,128]{1,0:T(8,128)(2,1)}, bf16[2048,128]{1,0:T(8,128)(2,1)S(1)}, u32[]{:S(2)}) copy-start(bf16[2048,128]{1,0:T(8,128)(2,1)S(1)} %all_gather.64) | copy-start | bytes 1572868
  292.7 73.3 %collective-permute-start = (bf16[2,256,1024]{2,1,0:T(8,128)(2,1)}, bf16[2,256,1024]{2,1,0:T(8,128)(2,1)}, u32[]{:S(2)}, u32[]{:S(2)}) collective-permute-start(bf16[2,256,1024]{2,1,0:T(8,128)(2,1)} %pad_maximum_fusion.1), channel_id=1, source_target_pairs={{0,4},{1,5},{2,6},{3,7},{4,8},{5,9},{6,10},{7,11},{8,12},{9,13},{1... | collective-permute-start | bytes 3145736 | tf_op jit(solution)/shard_map/ppermute | solution.py:24
  295.1 72.1 %collective-permute-start.1 = (bf16[2,256,1024]{2,1,0:T(8,128)(2,1)}, bf16[2,256,1024]{2,1,0:T(8,128)(2,1)}, u32[]{:S(2)}, u32[]{:S(2)}) collective-permute-start(bf16[2,256,1024]{2,1,0:T(8,128)(2,1)} %pad_maximum_fusion.1), channel_id=1, source_target_pairs={{0,3},{1,4},{2,5},{3,6},{4,7},{5,8},{6,9},{7,10},{8,11},{9,12},{10... | collective-permute-start | bytes 3145736 | tf_op jit(solution)/shard_map/ppermute | solution.py:24
  298.3 70.3 %collective-permute-start.2 = (bf16[2,256,1024]{2,1,0:T(8,128)(2,1)}, bf16[2,256,1024]{2,1,0:T(8,128)(2,1)S(1)}, u32[]{:S(2)}, u32[]{:S(2)}) collective-permute-start(bf16[2,256,1024]{2,1,0:T(8,128)(2,1)} %pad_maximum_fusion.1), channel_id=1, source_target_pairs={{0,2},{1,3},{2,4},{3,5},{4,6},{5,7},{6,8},{7,9},{8,10},{9,11},{10,... | collective-permute-start | bytes 3145736 | tf_op jit(solution)/shard_map/ppermute | solution.py:24
  299.7 69.0 %collective-permute-start.3 = (bf16[2,256,1024]{2,1,0:T(8,128)(2,1)}, bf16[2,256,1024]{2,1,0:T(8,128)(2,1)S(1)}, u32[]{:S(2)}, u32[]{:S(2)}) collective-permute-start(bf16[2,256,1024]{2,1,0:T(8,128)(2,1)} %pad_maximum_fusion.1), channel_id=1, source_target_pairs={{0,1},{1,2},{2,3},{3,4},{4,5},{5,6},{6,7},{7,8},{8,9},{9,10},{10,1... | collective-permute-start | bytes 3145736 | tf_op jit(solution)/shard_map/ppermute | solution.py:24
  425.6 732.9 %copy-start.1 = (f32[256,2048]{1,0:T(8,128)}, f32[256,2048]{1,0:T(8,128)S(1)}, u32[]{:S(2)}) copy-start(f32[256,2048]{1,0:T(8,128)S(1)} %get-tuple-element.296) | copy-start | bytes 6291460
  427.0 747.0 %copy-start.6 = (bf16[256,2048]{1,0:T(8,128)(2,1)}, bf16[256,2048]{1,0:T(8,128)(2,1)S(1)}, u32[]{:S(2)}) copy-start(bf16[256,2048]{1,0:T(8,128)(2,1)S(1)} %multiply_convert_fusion.4) | copy-start | bytes 3145732
  428.0 419.2 %copy-start.40 = (bf16[256,128]{1,0:T(8,128)(2,1)}, bf16[256,128]{1,0:T(8,128)(2,1)S(1)}, u32[]{:S(2)}) copy-start(bf16[256,128]{1,0:T(8,128)(2,1)S(1)} %fusion.78) | copy-start | bytes 196612
  1164.0 289.6 %reduce-scatter.19.cloned.1.call-start = ((), (), s32[]{:S(2)}) async-start(), calls=%async_computation.22 | async-start | bytes 1081344 | tf_op jit(solution)/shard_map/reduce_scatter | solution.py:381
  1165.6 428.4 %reduce-scatter.21.cloned.1.call-start = ((), (), s32[]{:S(2)}) async-start(), calls=%async_computation.23 | async-start | bytes 1081344 | tf_op jit(solution)/shard_map/reduce_scatter | solution.py:382
  1175.4 554.0 %reduce-scatter.25.cloned.1.call-start = ((), (), s32[]{:S(2)}) async-start(), calls=%async_computation.25 | async-start | bytes 1081344 | tf_op jit(solution)/shard_map/reduce_scatter | solution.py:384
  1297.2 567.4 %reduce-scatter.31.cloned.1.call-start = ((), (), s32[]{:S(2)}) async-start(), calls=%async_computation.28 | async-start | bytes 1081344
  1301.4 28.5 %collective-permute-start.4 = (bf16[2,256,1024]{1,2,0:T(8,128)(2,1)}, bf16[2,256,1024]{1,2,0:T(8,128)(2,1)}, u32[]{:S(2)}, u32[]{:S(2)}) collective-permute-start(bf16[2,256,1024]{1,2,0:T(8,128)(2,1)} %pad_maximum_fusion.3), channel_id=1, source_target_pairs={{4,0},{5,1},{6,2},{7,3},{8,4},{9,5},{10,6},{11,7},{12,8},{13,9},{1... | collective-permute-start | bytes 3145736 | tf_op jit(solution)/shard_map/ppermute | solution.py:24
  1303.8 27.5 %collective-permute-start.5 = (bf16[2,256,1024]{1,2,0:T(8,128)(2,1)}, bf16[2,256,1024]{1,2,0:T(8,128)(2,1)}, u32[]{:S(2)}, u32[]{:S(2)}) collective-permute-start(bf16[2,256,1024]{1,2,0:T(8,128)(2,1)} %pad_maximum_fusion.4), channel_id=1, source_target_pairs={{3,0},{4,1},{5,2},{6,3},{7,4},{8,5},{9,6},{10,7},{11,8},{12,9},{13... | collective-permute-start | bytes 3145736 | tf_op jit(solution)/shard_map/ppermute | solution.py:24
  1306.4 30.7 %collective-permute-start.6 = (bf16[2,256,1024]{1,2,0:T(8,128)(2,1)}, bf16[2,256,1024]{1,2,0:T(8,128)(2,1)}, u32[]{:S(2)}, u32[]{:S(2)}) collective-permute-start(bf16[2,256,1024]{1,2,0:T(8,128)(2,1)} %pad_maximum_fusion.5), channel_id=1, source_target_pairs={{2,0},{3,1},{4,2},{5,3},{6,4},{7,5},{8,6},{9,7},{10,8},{11,9},{12,... | collective-permute-start | bytes 3145736 | tf_op jit(solution)/shard_map/ppermute | solution.py:24
  1308.7 28.3 %collective-permute-start.7 = (bf16[2,256,1024]{1,2,0:T(8,128)(2,1)}, bf16[2,256,1024]{1,2,0:T(8,128)(2,1)}, u32[]{:S(2)}, u32[]{:S(2)}) collective-permute-start(bf16[2,256,1024]{1,2,0:T(8,128)(2,1)} %pad_maximum_fusion.6), channel_id=1, source_target_pairs={{1,0},{2,1},{3,2},{4,3},{5,4},{6,5},{7,6},{8,7},{9,8},{10,9},{11,1... | collective-permute-start | bytes 3145736 | tf_op jit(solution)/shard_map/ppermute | solution.py:24
  1313.0 686.7 %reduce-scatter.13.cloned.1.call-start = ((), (), s32[]{:S(2)}) async-start(), calls=%async_computation.19 | async-start | bytes 1081344 | tf_op jit(solution)/shard_map/reduce_scatter | solution.py:378
  1351.8 785.0 %reduce-scatter.15.cloned.1.call-start = ((), (), s32[]{:S(2)}) async-start(), calls=%async_computation.20 | async-start | bytes 2162688 | tf_op jit(solution)/shard_map/reduce_scatter | solution.py:379
  1355.0 923.4 %reduce-scatter.23.cloned.1.call-start = ((), (), s32[]{:S(2)}) async-start(), calls=%async_computation.24 | async-start | bytes 4325376 | tf_op jit(solution)/shard_map/reduce_scatter | solution.py:383
  1360.6 1059.4 %reduce-scatter.27.cloned.1.call-start = ((), (), s32[]{:S(2)}) async-start(), calls=%async_computation.26 | async-start | bytes 4325376 | tf_op jit(solution)/shard_map/reduce_scatter | solution.py:385
  1366.9 1194.8 %reduce-scatter.29.cloned.1.call-start = ((), (), s32[]{:S(2)}) async-start(), calls=%async_computation.27 | async-start | bytes 4325376 | tf_op jit(solution)/shard_map/reduce_scatter | solution.py:386
  (64 other events, 2384.6 us)
Sparse Core Ops, SparseCore 0:
  10.9 124.5 all-gather.9
  138.3 53.0 all-gather.11
  194.3 79.2 all-gather.13
  276.3 260.7 all-gather.19
  539.7 54.3 all-gather.21
  596.8 192.9 all-gather.15
  792.7 54.3 all-gather.17
  850.0 192.9 all-gather.23
  1045.9 54.3 all-gather.25
  1164.2 135.3 reduce-scatter.16
  1302.4 151.2 reduce-scatter.18
  1456.4 137.5 reduce-scatter.20
  1596.8 132.5 reduce-scatter.24
  1732.1 132.4 reduce-scatter.30
  1867.2 132.4 reduce-scatter.12
  2002.4 134.2 reduce-scatter.14
  2139.4 138.9 reduce-scatter.22
  2281.1 138.8 reduce-scatter.26
  2422.8 138.8 reduce-scatter.28
where the time goes:
time: 2580 us; the launch traced here: 2570 us
  waiting for transfers between devices  1840 us (71%)
  matrix products  331 us (13%)
  blocking collectives  258 us (10%)
  local copies, waits for them, and re-layouts  68.6 us (3%)
  other arithmetic  37 us (1%)
    all_gather x1, waiting for transfers between devices, per_device(): piece_down = lax.all_gather(feed_pieces[2], 'fsdp', axis=0, tiled=True)  187 us
    all_gather x1, waiting for transfers between devices, per_device(): piece_gate = lax.all_gather(feed_pieces[0], 'fsdp', axis=0, tiled=True)  187 us
    reduce_scatter x1, waiting for transfers between devices, per_device(): lax.psum_scatter(grads[5], 'fsdp', scatter_dimension=0, tiled=True)  142 us
    reduce_scatter x1, waiting for transfers between devices, per_device(): lax.psum_scatter(grads[8], 'fsdp', scatter_dimension=0, tiled=True)  142 us
    reduce_scatter x1, waiting for transfers between devices, per_device(): lax.psum_scatter(grads[7], 'fsdp', scatter_dimension=0, tiled=True)  142 us
    unnamed x20, waiting for transfers between devices  141 us
    reduce_scatter x1, waiting for transfers between devices, per_device(): lax.psum_scatter(grads[4], 'fsdp', scatter_dimension=0, tiled=True)  140 us
    reduce_scatter x1, waiting for transfers between devices, per_device(): lax.psum_scatter(grads[1], 'fsdp', scatter_dimension=0, tiled=True)  137 us
  transfers between devices with their start and end apart: 27, of which 19 were waited for; matrix products, arithmetic and copies ran while one was open for 14% of the time, Pallas kernels for 0%

commit v1 on v0

v1 whole, which is shorter than its diff:
```python
import functools
import math

import jax
import jax.numpy as jnp
from jax import lax
from jax.experimental import pallas as pl
from jax.experimental.pallas import tpu as pltpu
from jax.sharding import PartitionSpec as P

HEADS = 16
KV_HEADS = 8
HEAD_WIDTH = 128
ADAPTER_RANK = 16
REACH = 4

EPSILON = 1e-05
ADAPTER_SCALE = 0.5
ROTARY_BASE = 1000000.0
MASKED = -1e30
MESH = pl.DeviceIdType.MESH
AXIS = "fsdp"
VMEM_LIMIT = 60 * 1024 * 1024


def shifted(value, steps):
    count = lax.axis_size(AXIS)
    leading, last = (max(0, -steps), min(count, count - steps))
    return lax.ppermute(value, AXIS, [(source, source + steps) for source in range(leading, last)])


def swapped(value, bit):
    count = lax.axis_size(AXIS)
    return lax.ppermute(value, AXIS, [(source, source ^ bit) for source in range(count)])


def project(left, right):
    return lax.dot_general(
        left, right, (((1,), (1,)), ((), ())), preferred_element_type=jnp.float32
    )


def product(left, right):
    return jnp.dot(left, right, preferred_element_type=jnp.float32)


def contract_rows(left, right):
    return lax.dot_general(
        left, right, (((0,), (0,)), ((), ())), preferred_element_type=jnp.float32
    )


def sequence_info(lengths, adapter_set, index):
    ends = jnp.cumsum(lengths)
    starts = ends - lengths
    member = (index[:, None] >= starts[None, :]) & (index[:, None] < ends[None, :])
    labels = lax.iota(jnp.int32, lengths.shape[0]) + 1
    sequence = jnp.sum(jnp.where(member, labels[None, :], 0), axis=1) - 1
    begin = jnp.sum(jnp.where(member, starts[None, :], 0), axis=1)
    chosen = jnp.sum(jnp.where(member, adapter_set[None, :], 0), axis=1)
    return (sequence, index - begin, chosen)


def adapter_mask(chosen, columns):
    column_set = lax.broadcasted_iota(jnp.int32, (1, columns), 1) // ADAPTER_RANK
    return column_set == chosen[:, None]


def masked(values, select):
    return jnp.where(select, values, 0.0).astype(jnp.bfloat16)


def rotary_tables(position):
    half = HEAD_WIDTH // 2
    inverse = jnp.exp(lax.iota(jnp.float32, half) * (-2.0 * math.log(ROTARY_BASE) / HEAD_WIDTH))
    angles = position.astype(jnp.float32)[:, None] * inverse[None, :]
    cosine, sine = jnp.cos(angles), jnp.sin(angles)
    return (
        jnp.concatenate([cosine, cosine], axis=1),
        jnp.concatenate([-sine, sine], axis=1),
    )


def norm_forward(values, gain):
    scale = lax.rsqrt(jnp.mean(values * values, axis=-1, keepdims=True) + EPSILON)
    unit = values * scale
    return (unit * gain, unit, scale)


def norm_backward(grad, unit, scale, gain):
    weighted = grad * gain
    return scale * (weighted - unit * jnp.mean(weighted * unit, axis=-1, keepdims=True))


def partner_of(me, bit):
    return me + bit - 2 * bit * ((me // bit) % 2)


def peer_of(me, mask):
    bit = 1
    while bit <= mask:
        if mask & bit:
            me = partner_of(me, bit)
        bit *= 2
    return me


def enter(me, bits):
    barrier = pltpu.get_barrier_semaphore()
    for bit in bits:
        pl.semaphore_signal(
            barrier, inc=1, device_id=(partner_of(me, bit),), device_id_type=MESH
        )
    pl.semaphore_wait(barrier, len(bits))


def gather_kernel(parts, count, *refs):
    ins, outs = refs[:count], refs[count : 2 * count]
    send, recv, local = refs[2 * count :]
    me = lax.axis_index(AXIS)
    enter(me, sorted({bit for part in parts for bit in part[3]}))
    kept = []
    for a in range(count):
        rows = ins[a].shape[0]
        own = pltpu.make_async_copy(
            ins[a], outs[a].at[pl.ds(pl.multiple_of(me * rows, rows), rows)], local.at[a]
        )
        own.start()
        kept.append(own)

    def block(p, mask):
        a, first, number, _ = parts[p]
        rows = ins[a].shape[0]
        start = pl.multiple_of(peer_of(me, mask) * rows + first, 8)
        return outs[a].at[pl.ds(start, number)]

    def copy(p, mask, bit):
        a, first, number, _ = parts[p]
        source = ins[a].at[pl.ds(first, number)] if mask == 0 else block(p, mask)
        return pltpu.make_async_remote_copy(
            src_ref=source,
            dst_ref=block(p, mask),
            send_sem=send.at[p, mask + bit],
            recv_sem=recv.at[p, mask + bit],
            device_id=(partner_of(me, bit),),
            device_id_type=MESH,
        )

    def arrive(p, mask, bit):
        pltpu.make_async_remote_copy(
            src_ref=block(p, mask),
            dst_ref=block(p, mask),
            send_sem=send.at[p, mask],
            recv_sem=recv.at[p, mask],
            device_id=(partner_of(me, bit),),
            device_id_type=MESH,
        ).wait_recv()

    sends, arrivals = [], []
    for p, (_, _, _, order) in enumerate(parts):
        for level, bit in enumerate(order):
            first = copy(p, 0, bit)
            first.start()
            sends.append(first)
            held = [0]
            for earlier in order[:level]:
                held = held + [mask + earlier for mask in held]
            for place, mask in enumerate(held):
                arrivals.append(((level, place, p), p, mask + bit, bit, order[level + 1 :]))
    arrivals.sort(key=lambda entry: entry[0])
    for _, p, mask, bit, later in arrivals:
        arrive(p, mask, bit)
        for following in later:
            onward = copy(p, mask, following)
            onward.start()
            sends.append(onward)
    for sent in sends:
        sent.wait_send()
    for own in kept:
        own.wait()


def gather_rows(arrays, parts, members, collective_id):
    count = len(arrays)
    moved = sum(a.size * 2 for a in arrays) * (members - 1)
    return pl.pallas_call(
        functools.partial(gather_kernel, parts, count),
        out_shape=[
            jax.ShapeDtypeStruct((members * a.shape[0], a.shape[1]), a.dtype) for a in arrays
        ],
        in_specs=[pl.BlockSpec(memory_space=pl.ANY)] * count,
        out_specs=[pl.BlockSpec(memory_space=pl.ANY)] * count,
        scratch_shapes=[
            pltpu.SemaphoreType.DMA((len(parts), members)),
            pltpu.SemaphoreType.DMA((len(parts), members)),
            pltpu.SemaphoreType.DMA((count,)),
        ],
        compiler_params=pltpu.CompilerParams(
            collective_id=collective_id, has_side_effects=True
        ),
        cost_estimate=pl.CostEstimate(flops=0, bytes_accessed=moved * 2, transcendentals=0),
        name="gather_rows",
    )(*arrays)


def reduce_kernel(order, members, in_ref, out_ref, total, outgoing, incoming, send, recv):
    me = lax.axis_index(AXIS)
    rows = out_ref.shape[0]
    enter(me, sorted(order))
    for mask in range(members):
        start = pl.multiple_of(peer_of(me, mask) * rows, 8)
        total[mask] = in_ref[pl.ds(start, rows), :]
    live = list(range(members))
    for bit in order:
        leaving = [mask for mask in live if mask & bit]
        live = [mask for mask in live if not mask & bit]
        copies = []
        for mask in leaving:
            outgoing[mask] = total[mask].astype(jnp.bfloat16)
            copy = pltpu.make_async_remote_copy(
                src_ref=outgoing.at[mask],
                dst_ref=incoming.at[mask],
                send_sem=send.at[mask],
                recv_sem=recv.at[mask],
                device_id=(partner_of(me, bit),),
                device_id_type=MESH,
            )
            copy.start()
            copies.append((mask, copy))
        for mask, copy in copies:
            copy.wait_recv()
            total[mask - bit] = total[mask - bit] + incoming[mask].astype(jnp.float32)
        for mask, copy in copies:
            copy.wait_send()
    out_ref[...] = total[0]


def reduce_rows(value, order, members, collective_id):
    rows, columns = value.shape[0] // members, value.shape[1]
    return pl.pallas_call(
        functools.partial(reduce_kernel, order, members),
        out_shape=jax.ShapeDtypeStruct((rows, columns), jnp.float32),
        in_specs=[pl.BlockSpec(memory_space=pltpu.VMEM)],
        out_specs=pl.BlockSpec(memory_space=pltpu.VMEM),
        scratch_shapes=[
            pltpu.VMEM((members, rows, columns), jnp.float32),
            pltpu.VMEM((members, rows, columns), jnp.bfloat16),
            pltpu.VMEM((members, rows, columns), jnp.bfloat16),
            pltpu.SemaphoreType.DMA((members,)),
            pltpu.SemaphoreType.DMA((members,)),
        ],
        compiler_params=pltpu.CompilerParams(
            collective_id=collective_id, has_side_effects=True, vmem_limit_bytes=VMEM_LIMIT
        ),
        name="reduce_rows",
    )(value)


def joined_kernel(turned, x_ref, w_ref, cos_ref, sin_ref, query_ref, pair_ref):
    step = pl.program_id(0)
    values = project(x_ref[...], w_ref[...])
    cosine, sine = cos_ref[...], sin_ref[...]
    heads = values.shape[1] // HEAD_WIDTH
    turn = step < turned
    pieces = []
    for h in range(heads):
        head = values[:, h * HEAD_WIDTH : (h + 1) * HEAD_WIDTH]
        rotated = head * cosine + pltpu.roll(head, HEAD_WIDTH // 2, 1) * sine
        pieces.append(jnp.where(turn, rotated, head).astype(jnp.bfloat16))
    result = jnp.concatenate(pieces, axis=1)
    half = pl.num_programs(0) // 2

    @pl.when(step < half)
    def _():
        query_ref[...] = result

    @pl.when(step >= half)
    def _():
        pair_ref[...] = result


def joined_heads(x, weight, cosine, sine):
    number, depth = x.shape
    tile = 512
    steps = weight.shape[0] // tile
    half = steps // 2
    turned = (HEADS + KV_HEADS) * HEAD_WIDTH // tile
    wide = half * tile
    return pl.pallas_call(
        functools.partial(joined_kernel, turned),
        out_shape=[jax.ShapeDtypeStruct((number, wide), jnp.bfloat16)] * 2,
        grid=(steps,),
        in_specs=[
            pl.BlockSpec((number, depth), lambda j: (0, 0), pipeline_mode=pl.Buffered(1)),
            pl.BlockSpec((tile, depth), lambda j: (j, 0)),
            pl.BlockSpec((number, HEAD_WIDTH), lambda j: (0, 0)),
            pl.BlockSpec((number, HEAD_WIDTH), lambda j: (0, 0)),
        ],
        out_specs=[
            pl.BlockSpec((number, tile), lambda j: (0, jnp.minimum(j, half - 1))),
            pl.BlockSpec((number, tile), lambda j: (0, jnp.maximum(j - half, 0))),
        ],
        compiler_params=pltpu.CompilerParams(vmem_limit_bytes=VMEM_LIMIT),
        cost_estimate=pl.CostEstimate(
            flops=2 * number * depth * weight.shape[0],
            bytes_accessed=2 * weight.size + 4 * x.size,
            transcendentals=0,
        ),
        name="joined_heads",
    )(x, weight, cosine, sine)


def make_bias(first, query_seq, key_seq, bias_ref):
    number, keys = bias_ref.shape
    row = lax.broadcasted_iota(jnp.int32, (number, keys), 0) + (keys - number)
    column = lax.broadcasted_iota(jnp.int32, (number, keys), 1)
    allowed = (query_seq == key_seq) & (column <= row)
    bias_ref[...] = jnp.where(allowed, 0.0, MASKED)


def softmax_of(query, keys, bias):
    scale = HEAD_WIDTH ** (-0.5)
    scores = jnp.concatenate([project(query, key) for key in keys], axis=1) * scale + bias
    top = jnp.max(scores, axis=-1, keepdims=True)
    weights = jnp.exp(scores - top)
    return weights * (1.0 / jnp.sum(weights, axis=-1, keepdims=True))


def attend_kernel(blocks, *refs):
    q_ref = refs[0]
    k_refs = refs[1 : 1 + blocks]
    v_refs = refs[1 + blocks : 1 + 2 * blocks]
    qs_ref, ks_ref, out_ref, bias_ref = refs[1 + 2 * blocks :]

    @pl.when(pl.program_id(0) == 0)
    def _():
        make_bias(0, qs_ref[...], ks_ref[...], bias_ref)

    keys = [ref[...] for ref in k_refs]
    number = keys[0].shape[0]
    for g in range(HEADS // KV_HEADS):
        columns = slice(g * HEAD_WIDTH, (g + 1) * HEAD_WIDTH)
        probs = softmax_of(q_ref[:, columns], keys, bias_ref[...]).astype(jnp.bfloat16)
        result = product(probs[:, :number], v_refs[0][...])
        for b in range(1, blocks):
            result += product(probs[:, b * number : (b + 1) * number], v_refs[b][...])
        out_ref[:, columns] = result.astype(jnp.bfloat16)


def attend(query, pairs, query_seq, key_seq):
    number, blocks = query.shape[0], len(pairs)
    group = HEADS // KV_HEADS
    keys = blocks * number
    key_spec = pl.BlockSpec((number, HEAD_WIDTH), lambda j: (0, j))
    value_spec = pl.BlockSpec((number, HEAD_WIDTH), lambda j: (0, KV_HEADS + j))
    wide_spec = pl.BlockSpec((number, group * HEAD_WIDTH), lambda j: (0, j))
    return pl.pallas_call(
        functools.partial(attend_kernel, blocks),
        out_shape=jax.ShapeDtypeStruct(query.shape, jnp.bfloat16),
        grid=(KV_HEADS,),
        in_specs=[wide_spec]
        + [key_spec] * blocks
        + [value_spec] * blocks
        + [
            pl.BlockSpec((number, 1), lambda j: (0, 0)),
            pl.BlockSpec((1, keys), lambda j: (0, 0)),
        ],
        out_specs=wide_spec,
        scratch_shapes=[pltpu.VMEM((number, keys), jnp.float32)],
        compiler_params=pltpu.CompilerParams(vmem_limit_bytes=VMEM_LIMIT),
        cost_estimate=pl.CostEstimate(
            flops=4 * HEADS * number * keys * HEAD_WIDTH,
            bytes_accessed=4 * query.size + 2 * sum(p.size for p in pairs),
            transcendentals=HEADS * number * keys,
        ),
        name="attend",
    )(query, *pairs, *pairs, query_seq, key_seq)


def attend_back_kernel(blocks, *refs):
    q_ref, g_ref = refs[:2]
    k_refs = refs[2 : 2 + blocks]
    v_refs = refs[2 + blocks : 2 + 2 * blocks]
    qs_ref, ks_ref, cos_ref, sin_ref = refs[2 + 2 * blocks : 6 + 2 * blocks]
    dq_ref, own_ref, away_ref, bias_ref = refs[6 + 2 * blocks :]

    @pl.when(pl.program_id(0) == 0)
    def _():
        make_bias(0, qs_ref[...], ks_ref[...], bias_ref)

    scale = HEAD_WIDTH ** (-0.5)
    keys = [ref[...] for ref in k_refs]
    number = keys[0].shape[0]
    key_back = [None] * blocks
    value_back = [None] * blocks
    for g in range(HEADS // KV_HEADS):
        columns = slice(g * HEAD_WIDTH, (g + 1) * HEAD_WIDTH)
        query, grad = q_ref[:, columns], g_ref[:, columns]
        probs = softmax_of(query, keys, bias_ref[...])
        back = jnp.concatenate([project(grad, ref[...]) for ref in v_refs], axis=1)
        center = jnp.sum(back * probs, axis=-1, keepdims=True)
        score_back = (probs * (back - center)).astype(jnp.bfloat16)
        probs = probs.astype(jnp.bfloat16)
        total = None
        for b in range(blocks):
            rows = slice(b * number, (b + 1) * number)
            part = product(score_back[:, rows], keys[b])
            total = part if total is None else total + part
            to_key = contract_rows(score_back[:, rows], query)
            to_value = contract_rows(probs[:, rows], grad)
            key_back[b] = to_key if g == 0 else key_back[b] + to_key
            value_back[b] = to_value if g == 0 else value_back[b] + to_value
        total = total * scale
        turned = total * cos_ref[...] - pltpu.roll(total, HEAD_WIDTH // 2, 1) * sin_ref[...]
        dq_ref[:, columns] = turned.astype(jnp.bfloat16)
    for b in range(blocks - 1):
        away_ref[b, 0] = (key_back[b] * scale).astype(jnp.bfloat16)
        away_ref[b, 1] = value_back[b].astype(jnp.bfloat16)
    own_ref[0] = key_back[blocks - 1] * scale
    own_ref[1] = value_back[blocks - 1]


def attend_back(query, grad, pairs, query_seq, key_seq, cosine, sine):
    number, blocks = query.shape[0], len(pairs)
    group = HEADS // KV_HEADS
    keys = blocks * number
    wide = KV_HEADS * HEAD_WIDTH
    key_spec = pl.BlockSpec((number, HEAD_WIDTH), lambda j: (0, j))
    value_spec = pl.BlockSpec((number, HEAD_WIDTH), lambda j: (0, KV_HEADS + j))
    wide_spec = pl.BlockSpec((number, group * HEAD_WIDTH), lambda j: (0, j))
    fixed = pl.BlockSpec((number, HEAD_WIDTH), lambda j: (0, 0))
    return pl.pallas_call(
        functools.partial(attend_back_kernel, blocks),
        out_shape=[
            jax.ShapeDtypeStruct(query.shape, jnp.bfloat16),
            jax.ShapeDtypeStruct((2, number, wide), jnp.float32),
            jax.ShapeDtypeStruct((blocks - 1, 2, number, wide), jnp.bfloat16),
        ],
        grid=(KV_HEADS,),
        in_specs=[wide_spec, wide_spec]
        + [key_spec] * blocks
        + [value_spec] * blocks
        + [
            pl.BlockSpec((number, 1), lambda j: (0, 0)),
            pl.BlockSpec((1, keys), lambda j: (0, 0)),
            fixed,
            fixed,
        ],
        out_specs=[
            wide_spec,
            pl.BlockSpec((2, number, HEAD_WIDTH), lambda j: (0, 0, j)),
            pl.BlockSpec((blocks - 1, 2, number, HEAD_WIDTH), lambda j: (0, 0, 0, j)),
        ],
        scratch_shapes=[pltpu.VMEM((number, keys), jnp.float32)],
        compiler_params=pltpu.CompilerParams(vmem_limit_bytes=VMEM_LIMIT),
        cost_estimate=pl.CostEstimate(
            flops=10 * HEADS * number * keys * HEAD_WIDTH,
            bytes_accessed=6 * query.size + 8 * sum(p.size for p in pairs),
            transcendentals=HEADS * number * keys,
        ),
        name="attend_back",
    )(query, grad, *pairs, *pairs, query_seq, key_seq, cosine, sine)


def feed_kernel(
    width, tile, x_ref, c_ref, gl_ref, ul_ref, db_ref, w_ref,
    mixed_ref, back_ref, grads_ref, mixed_acc, back_acc, grad_acc,
):
    step, last = pl.program_id(0), pl.num_programs(0) - 1
    rows, columns = x_ref.shape[0], gl_ref.shape[1]
    hid = w_ref.shape[0] // 3
    wg, wu, wd = (w_ref.at[pl.ds(i * hid, hid)] for i in range(3))
    main, side = slice(0, width), slice(width, width + columns)

    @pl.when(step == 0)
    def _():
        mixed_acc[...] = jnp.zeros_like(mixed_acc)
        back_acc[...] = jnp.zeros_like(back_acc)

    grad_acc[...] = jnp.zeros_like(grad_acc)

    @pl.loop(0, rows // tile)
    def _(i):
        at = pl.ds(pl.multiple_of(i * tile, tile), tile)
        x, cot = x_ref[at, :], c_ref[at, :]
        gl, ul, db = gl_ref[at, :], ul_ref[at, :], db_ref[at, :]
        gate = project(x, wg[:, main]) + project(gl, wg[:, side])
        up = project(x, wu[:, main]) + project(ul, wu[:, side])
        back = project(cot, wd[:, main]) + project(db, wd[:, side])
        sigma = 1.0 / (1.0 + jnp.exp(-gate))
        active = gate * sigma
        hidden = (active * up).astype(jnp.bfloat16)
        gate_back = (back * up * sigma * (1.0 + gate * (1.0 - sigma))).astype(jnp.bfloat16)
        up_back = (back * active).astype(jnp.bfloat16)
        mixed_acc[at, :] += product(hidden, wd[...])
        back_acc[at, main] += product(gate_back, wg[:, main]) + product(up_back, wu[:, main])
        back_acc[at, side] += product(gate_back, wg[:, side])
        back_acc[at, width + columns : width + 2 * columns] += product(up_back, wu[:, side])
        grad_acc[:, :columns] += contract_rows(gate_back, gl)
        grad_acc[:, columns : 2 * columns] += contract_rows(up_back, ul)
        grad_acc[:, 2 * columns :] += contract_rows(hidden, db)

    grads_ref[...] = grad_acc[...].astype(grads_ref.dtype)

    @pl.when(step == last)
    def _():
        mixed_ref[...] = mixed_acc[...].astype(mixed_ref.dtype)
        back_ref[...] = back_acc[...].astype(back_ref.dtype)


def feed(x, cot, gate_low, up_low, down_back, weights, shard):
    rows, width = x.shape
    columns = gate_low.shape[1]
    steps = weights.shape[0] // (3 * shard)
    tile = 256
    one = pl.Buffered(1)
    whole = lambda j: (0, 0)
    return pl.pallas_call(
        functools.partial(feed_kernel, width, tile),
        out_shape=[
            jax.ShapeDtypeStruct((rows, width + columns), jnp.bfloat16),
            jax.ShapeDtypeStruct((rows, width + 2 * columns), jnp.bfloat16),
            jax.ShapeDtypeStruct((steps * shard, 3 * columns), jnp.bfloat16),
        ],
        grid=(steps,),
        in_specs=[
            pl.BlockSpec((rows, width), whole, pipeline_mode=one),
            pl.BlockSpec((rows, width), whole, pipeline_mode=one),
            pl.BlockSpec((rows, columns), whole, pipeline_mode=one),
            pl.BlockSpec((rows, columns), whole, pipeline_mode=one),
            pl.BlockSpec((rows, columns), whole, pipeline_mode=one),
            pl.BlockSpec((3 * shard, width + columns), lambda j: (j, 0)),
        ],
        out_specs=[
            pl.BlockSpec((rows, width + columns), whole, pipeline_mode=one),
            pl.BlockSpec((rows, width + 2 * columns), whole, pipeline_mode=one),
            pl.BlockSpec((shard, 3 * columns), lambda j: (j, 0)),
        ],
        scratch_shapes=[
            pltpu.VMEM((rows, width + columns), jnp.float32),
            pltpu.VMEM((rows, width + 2 * columns), jnp.float32),
            pltpu.VMEM((shard, 3 * columns), jnp.float32),
        ],
        compiler_params=pltpu.CompilerParams(vmem_limit_bytes=VMEM_LIMIT),
        cost_estimate=pl.CostEstimate(
            flops=4 * rows * weights.size,
            bytes_accessed=2 * weights.size + 8 * x.size,
            transcendentals=rows * steps * shard,
        ),
        name="feed",
    )(x, cot, gate_low, up_low, down_back, weights)


def per_device(
    tokens,
    attention_gain,
    feedforward_gain,
    joined_projection,
    output_projection,
    gate_weight,
    up_weight,
    down_weight,
    joined_adapter_input,
    joined_adapter_output,
    output_adapter_input,
    output_adapter_output,
    gate_adapter_input,
    gate_adapter_output,
    upward_adapter_input,
    upward_adapter_output,
    down_adapter_input,
    down_adapter_output,
    lengths,
    adapter_set,
    cotangent,
):
    number, width = tokens.shape
    columns = joined_adapter_input.shape[1]
    devices = lax.axis_size(AXIS)
    kv_width = KV_HEADS * HEAD_WIDTH
    shard = gate_weight.shape[0]
    near, far = 1, devices // 4
    highest = devices // 2
    middle = [1 << i for i in range(1, devices.bit_length()) if (1 << i) < far]
    me = lax.axis_index(AXIS)
    first = me * number

    joined_shard = jnp.concatenate([joined_projection, joined_adapter_output], axis=1)
    output_shard = jnp.concatenate([output_projection, output_adapter_output], axis=1)
    entry_shard = jnp.concatenate(
        [output_adapter_input, gate_adapter_input, upward_adapter_input, down_adapter_output],
        axis=1,
    )
    feed_shard = jnp.concatenate(
        [
            jnp.concatenate([gate_weight, gate_adapter_output], axis=1),
            jnp.concatenate([up_weight, upward_adapter_output], axis=1),
            jnp.concatenate([down_weight, down_adapter_input], axis=1),
        ],
        axis=0,
    )
    up_order = tuple([highest, far] + middle + [near])
    down_order = tuple([highest, far] + middle[::-1] + [near])
    rows = joined_shard.shape[0]
    full_joined, full_f_entry = gather_rows(
        [joined_shard, joined_adapter_input],
        (
            (0, 0, rows // 2, up_order),
            (0, rows // 2, rows // 2, down_order),
            (1, 0, joined_adapter_input.shape[0], up_order),
        ),
        devices,
        1,
    )
    full_output = lax.all_gather(output_shard, AXIS, axis=0, tiled=True)
    full_entry = lax.all_gather(entry_shard, AXIS, axis=0, tiled=True)
    full_o_entry = full_entry[:, :columns]
    full_gu_entry = full_entry[:, columns : 3 * columns]
    full_d_exit = full_entry[:, 3 * columns :]
    groups, seen = [], set()
    for device in range(devices):
        if device not in seen:
            members = [device]
            for bit in middle + [highest]:
                members = members + [m ^ bit for m in members]
            groups.append(sorted(members))
            seen.update(members)
    full_feed = lax.all_gather(
        feed_shard, AXIS, axis=0, tiled=True, axis_index_groups=groups
    )

    offsets = lax.iota(jnp.int32, number)
    blocks = [me, me ^ near, me ^ far, me ^ far ^ near]
    index = jnp.concatenate([b * number + offsets for b in blocks])
    all_sequence, all_position, all_chosen = sequence_info(lengths, adapter_set, index)
    all_select = adapter_mask(all_chosen, columns)
    select = all_select[:number]
    cosine, sine = rotary_tables(all_position[:number])
    key_index = first - REACH * number + lax.iota(jnp.int32, (REACH + 1) * number)
    key_sequence, _, _ = sequence_info(lengths, adapter_set, key_index)
    query_seq = all_sequence[:number][:, None]
    key_seq = key_sequence[None, :]

    inputs = tokens.astype(jnp.float32)
    gain_one = attention_gain.astype(jnp.float32)
    gain_two = feedforward_gain.astype(jnp.float32)

    def group_rows(value):
        beside = swapped(value, near)
        across = swapped(value, far)
        return jnp.concatenate([value, beside, across, swapped(across, near)], axis=0)

    group_cot = group_rows(cotangent)

    normed_one, unit_one, scale_one = norm_forward(inputs, gain_one)
    normed_one = normed_one.astype(jnp.bfloat16)
    joined_low = masked(product(normed_one, full_f_entry), select)
    half_low = joined_low * ADAPTER_SCALE
    query, pair = joined_heads(
        jnp.concatenate([normed_one, half_low], axis=1), full_joined, cosine, sine
    )
    pairs = [shifted(pair, back) for back in range(REACH, 0, -1)] + [pair]
    attended = attend(query, pairs, query_seq, key_seq)
    output_low = masked(product(attended, full_o_entry), select)
    branch = project(
        jnp.concatenate([attended, output_low * ADAPTER_SCALE], axis=1), full_output
    )
    hidden_one = inputs + branch

    normed_two, unit_two, scale_two = norm_forward(hidden_one, gain_two)
    normed_two = normed_two.astype(jnp.bfloat16)
    group_normed = group_rows(normed_two)
    lows = masked(
        product(group_normed, full_gu_entry), jnp.concatenate([all_select, all_select], axis=1)
    )
    gate_low, up_low = lows[:, :columns], lows[:, columns:]
    down_back = masked(ADAPTER_SCALE * product(group_cot, full_d_exit), all_select)
    mixed_parts, back_parts, feed_grads = feed(
        group_normed,
        group_cot,
        gate_low * ADAPTER_SCALE,
        up_low * ADAPTER_SCALE,
        down_back,
        full_feed,
        shard,
    )

    def group_sum(parts):
        own, beside = parts[:number], parts[number : 2 * number]
        across, corner = parts[2 * number : 3 * number], parts[3 * number :]
        wide = jnp.float32
        far_sum = across.astype(wide) + swapped(corner, near).astype(wide)
        near_sum = own.astype(wide) + swapped(beside, near).astype(wide)
        return near_sum + swapped(far_sum.astype(jnp.bfloat16), far).astype(wide)

    back_sum = group_sum(back_parts)
    mixed_sum = group_sum(mixed_parts)
    low_back = masked(
        ADAPTER_SCALE * back_sum[:, width:], jnp.concatenate([select, select], axis=1)
    )
    normed_two_back = back_sum[:, :width] + project(low_back, full_gu_entry)
    hidden_back_one = cotangent.astype(jnp.float32) + norm_backward(
        normed_two_back, unit_two, scale_two, gain_two
    )
    branch_back = hidden_back_one.astype(jnp.bfloat16)

    down_low = masked(mixed_sum[:, width:], select)
    mixed = mixed_sum[:, :width] + ADAPTER_SCALE * project(down_low, full_d_exit)
    layer_output = (hidden_one + mixed).astype(jnp.bfloat16)

    through = product(branch_back, full_output)
    output_low_back = masked(ADAPTER_SCALE * through[:, width:], select)
    attended_back = (through[:, :width] + project(output_low_back, full_o_entry)).astype(
        jnp.bfloat16
    )
    query_back, own_back, away_back = attend_back(
        query, attended_back, pairs, query_seq, key_seq, cosine, sine
    )
    pair_back = own_back
    for back in range(REACH, 0, -1):
        pair_back = pair_back + shifted(away_back[REACH - back], -back).astype(jnp.float32)
    half = HEAD_WIDTH // 2
    key_back = pair_back[0].reshape(number, KV_HEADS, HEAD_WIDTH)
    rolled = jnp.concatenate([key_back[..., half:], key_back[..., :half]], axis=-1)
    key_back = key_back * cosine[:, None, :] - rolled * sine[:, None, :]
    joined_back = jnp.concatenate(
        [
            query_back,
            key_back.reshape(number, kv_width).astype(jnp.bfloat16),
            pair_back[1].astype(jnp.bfloat16),
        ],
        axis=1,
    )
    inward = product(joined_back, full_joined)
    joined_low_back = masked(ADAPTER_SCALE * inward[:, width:], select)
    normed_one_back = inward[:, :width] + project(joined_low_back, full_f_entry)
    grad_tokens = hidden_back_one + norm_backward(normed_one_back, unit_one, scale_one, gain_one)

    feed_rows = lax.psum_scatter(
        feed_grads, AXIS, scatter_dimension=0, tiled=True, axis_index_groups=groups
    ).astype(jnp.float32)
    early = jnp.concatenate(
        [
            contract_rows(attended, output_low_back),
            ADAPTER_SCALE * contract_rows(branch_back, output_low),
            contract_rows(normed_two, low_back),
            ADAPTER_SCALE * contract_rows(cotangent, down_low),
        ],
        axis=1,
    )
    late_exit = contract_rows(joined_back, half_low)
    late_entry = contract_rows(normed_one, joined_low_back)
    per_exit, per_entry = late_exit.shape[0] // devices, late_entry.shape[0] // devices
    late = jnp.concatenate(
        [
            late_exit.reshape(devices, per_exit, columns),
            late_entry.reshape(devices, per_entry, columns),
            early.reshape(devices, per_entry, 5, columns)
            .transpose(0, 2, 1, 3)
            .reshape(devices, 5 * per_entry, columns),
        ],
        axis=1,
    ).reshape(-1, columns)
    mine = reduce_rows(late, (near,) + tuple(middle) + (far, highest), devices, 2)

    def piece(at):
        return mine[per_exit + at * per_entry : per_exit + (at + 1) * per_entry]

    return (
        layer_output,
        grad_tokens,
        piece(0),
        mine[:per_exit],
        piece(1),
        piece(2),
        piece(3),
        feed_rows[:, :columns],
        piece(4),
        feed_rows[:, columns : 2 * columns],
        feed_rows[:, 2 * columns :],
        piece(5),
    )


def solution(mesh):
    split, copied = P(AXIS, None), P()
    placed = (split, copied, copied) + (split,) * 15 + (copied, copied, split)
    return jax.shard_map(
        per_device, mesh=mesh, in_specs=placed, out_specs=(split,) * 12, check_vma=False
    )
```

time: 2580 us -> 970 us (0.38)
  waiting for transfers between devices: 1840 us -> 410 us
  Pallas kernels: 0 us -> 350 us
  matrix products: 331 us -> 39.3 us
  blocking collectives: 258 us -> 0 us
  starting transfers between devices: 15.7 us -> 64.7 us
    reduce_scatter x9 -> x1, waiting for transfers between devices: 1020 us -> 0.01 us  [per_device(): lax.psum_scatter(feed_grads, AXIS, scatter_dimension=0, tiled=True, axis_...]
    pallas_call x0 -> x6, Pallas kernels: none -> 350 us  [the longest x1 111 us: reduce_rows(): pl.pallas_call(functools.partial(reduce_kernel, order, members), out_shap...]
    all_gather x9 -> x3, waiting for transfers between devices: 601 us -> 270 us  [the longest x1 270 us: per_device(): lax.all_gather(feed_shard, AXIS, axis=0, tiled=True, axis_index_groups=gr...]
    all_gather x6 -> x0, blocking collectives: 258 us -> none  [the longest x1 46.9 us: per_device(): lax.all_gather(attn_pieces[2], 'fsdp', axis=0, tiled=True)]
    unnamed x20 -> x4, waiting for transfers between devices: 141 us -> 0.07 us
    dot_general x56 -> x0, matrix products: 110 us -> none  [the longest x8 20.6 us: head_backward(): jnp.einsum('gqk,kd->gqd', score_back, key_head, preferred_element_type=jn...]
    dot_general x15 -> x5, matrix products: 111 us -> 13.8 us  [project(): lax.dot_general(left, right, (((1,), (1,)), ((), ())), preferred_element_...]
    ppermute x8 -> x20, waiting for transfers between devices: 75.5 us -> 140 us  [the longest x12 75.5 us: swapped(): lax.ppermute(value, AXIS, [(source, source ^ bit) for source in range(cou...]
  transfers between devices with their start and end apart: 27 -> 24, of which waited for: 19 -> 5; matrix products, arithmetic and copies ran while one was open for 14% -> 9% of each run, Pallas kernels for 0% -> 16%
where the time goes in v1:
time: 970 us; the launch traced here: 964 us
  waiting for transfers between devices  410 us (42%)
  Pallas kernels  350 us (36%)
  starting transfers between devices  64.7 us (7%)
  local copies, waits for them, and re-layouts  46.9 us (5%)
  matrix products  39.3 us (4%)
  other arithmetic  38.9 us (4%)
  between operations  15 us (2%)
    all_gather x1, waiting for transfers between devices, per_device(): lax.all_gather(feed_shard, AXIS, axis=0, tiled=True, axis_index_groups=gr...  270 us
    pallas_call x1, Pallas kernels, reduce_rows(): pl.pallas_call(functools.partial(reduce_kernel, order, members), out_shap...  111 us
    pallas_call x1, Pallas kernels, gather_rows(): pl.pallas_call(functools.partial(gather_kernel, parts, count), out_shape=...  100 us
    pallas_call x1, Pallas kernels, feed(): pl.pallas_call(functools.partial(feed_kernel, width, tile), out_shape=[ja...  81.4 us
    ppermute x12, waiting for transfers between devices, swapped(): lax.ppermute(value, AXIS, [(source, source ^ bit) for source in range(cou...  75.5 us
    ppermute x8, waiting for transfers between devices, shifted(): lax.ppermute(value, AXIS, [(source, source + steps) for source in range(l...  64.6 us
    ppermute x12, starting transfers between devices, swapped(): lax.ppermute(value, AXIS, [(source, source ^ bit) for source in range(cou...  45.7 us
    pallas_call x1, Pallas kernels, attend_back(): pl.pallas_call(functools.partial(attend_back_kernel, blocks), out_shape=[...  26.5 us
  transfers between devices with their start and end apart: 24, of which 5 were waited for; matrix products, arithmetic and copies ran while one was open for 9% of the time, Pallas kernels for 16%

profile of v1, /device:TPU:0, one launch (start us, length us, event | category | flops | bytes accessed | tf_op | source)
XLA Modules:
  0.0 964.4 jit_solution(13339453030401324532)
XLA Ops:
  10.5 4.9 maximum_maximum_fusion
  17.3 100.2 %gather_rows.1 = (bf16[4096,2176]{1,0:T(8,128)(2,1)}, bf16[2048,128]{1,0:T(8,128)(2,1)}) custom-call(bf16[128,2176]{1,0:T(8,128)(2,1)} %pad_maximum_fusion.7.refs_0_, bf16[64,128]{1,0:T(8,128)(2,1)} %refs_1_.1), custom_call_target="tpu_custom_call" | custom-call | bytes 35553280 | tf_op jit(solution)/shard_map/gather_rows/pallas_call | solution.py:186
  122.3 14.0 %joined_heads.1 = (bf16[256,2048]{1,0:T(8,128)(2,1)}, bf16[256,2048]{1,0:T(8,128)(2,1)}) custom-call(bf16[256,2176]{1,0:T(8,128)(2,1)} %pad_maximum_fusion.4.x_ref, bf16[4096,2176]{1,0:T(8,128)(2,1)} %get-tuple-element.23.w_ref, f32[256,128]{1,0:T(8,128)} %pad_maximum_fusion.9.cos_ref.refs_14_, f32[256,128]{1,0:T(8,128)} %pad_maximum_fusion.10.sin_ref.refs_15_), custom_call_target="tpu_custom_call" | custom-call | flops 4563402752 | bytes 20054016 | tf_op jit(solution)/shard_map/joined_heads/pallas_call | solution.py:289
  138.4 5.3 collective-permute-start.1
  143.7 2.4 collective-permute-start.2
  146.1 3.7 collective-permute-start.3
  151.4 64.6 %collective-permute-done.refs_1_.refs_6_.refs_2_.refs_7_ = bf16[256,2048]{1,0:T(8,128)(2,1)S(1)} collective-permute-done((bf16[256,2048]{1,0:T(8,128)(2,1)}, bf16[256,2048]{1,0:T(8,128)(2,1)S(1)}, u32[]{:S(2)}, u32[]{:S(2)}) %collective-permute-start) | collective-permute-done | bytes 1048608 | tf_op jit(solution)/shard_map/ppermute | solution.py:29
  217.3 16.6 %attend.1 = bf16[256,2048]{1,0:T(8,128)(2,1)} custom-call(bf16[256,2048]{1,0:T(8,128)(2,1)} %get-tuple-element.24.refs_0_, bf16[256,2048]{1,0:T(8,128)(2,1)} %copy-done.6, bf16[256,2048]{1,0:T(8,128)(2,1)} %copy-done.7, bf16[256,2048]{1,0:T(8,128)(2,1)} %collective-permute-done.2.refs_3_.refs_8_.refs_4_.refs_9_, ...), custom_call_target="tpu_custom_call" | custom-call | flops 2684354560 | bytes 7340032 | tf_op jit(solution)/shard_map/attend/pallas_call | solution.py:357
  236.0 7.8 multiply_reduce_fusion.1
  244.1 42.2 %collective-permute-start.5 = (bf16[256,2048]{1,0:T(8,128)(2,1)S(1)}, bf16[256,2048]{1,0:T(8,128)(2,1)S(1)}, u32[]{:S(2)}, u32[]{:S(2)}) collective-permute-start(bf16[256,2048]{1,0:T(8,128)(2,1)S(1)} %multiply_convert_fusion), channel_id=1, source_target_pairs={{0,8},{1,9},{2,10},{3,11},{4,12},{5,13},{6,14},{7,15},{8,0},{9,1},... | collective-permute-start | bytes 3145736 | tf_op jit(solution)/shard_map/ppermute | solution.py:34
  288.2 24.0 %collective-permute-done.5 = bf16[256,2048]{1,0:T(8,128)(2,1)S(1)} collective-permute-done((bf16[256,2048]{1,0:T(8,128)(2,1)S(1)}, bf16[256,2048]{1,0:T(8,128)(2,1)S(1)}, u32[]{:S(2)}, u32[]{:S(2)}) %collective-permute-start.5) | collective-permute-done | bytes 1048608 | tf_op jit(solution)/shard_map/ppermute | solution.py:34
  319.8 269.5 %all-gather.8.cloned.1.call-done.w_ref = bf16[6144,2176]{1,0:T(8,128)(2,1)} async-done(((bf16[768,2176]{1,0:T(8,128)(2,1)}), bf16[6144,2176]{1,0:T(8,128)(2,1)}) %all-gather.8.cloned.1.call-update) | async-done | bytes 26738704 | tf_op jit(solution)/shard_map/all_gather | solution.py:628
  589.3 81.4 %feed.1 = (bf16[1024,2176]{1,0:T(8,128)(2,1)}, bf16[1024,2304]{1,0:T(8,128)(2,1)}, bf16[2048,384]{1,0:T(8,128)(2,1)}) custom-call(bf16[1024,2048]{1,0:T(8,128)(2,1)} %copy-done.10, bf16[1024,2048]{1,0:T(8,128)(2,1)} %copy-done.19, bf16[1024,128]{1,0:T(8,128)(2,1)} %get-tuple-element.46.gl_ref, bf16[1024,128]{1,0:T(8,128)(2,1)} %get-tuple-element.45.ul_ref, ...), custom_call_target="tpu_custom_call" | custom-call | flops 54760833024 | bytes 43515904 | tf_op jit(solution)/shard_map/feed/pallas_call | solution.py:518
  670.7 2.7 fusion.72
  673.4 3.2 fusion.71
  677.1 2.5 add_convert_fusion.1
  684.0 29.0 %collective-permute-done.12 = bf16[256,2176]{1,0:T(8,128)(2,1)} collective-permute-done((bf16[256,2176]{1,0:T(8,128)(2,1)}, bf16[256,2176]{1,0:T(8,128)(2,1)}, u32[]{:S(2)}, u32[]{:S(2)}) %collective-permute-start.12) | collective-permute-done | bytes 1114144 | tf_op jit(solution)/shard_map/ppermute | solution.py:34
  713.0 2.3 convert_add_fusion.2
  715.3 2.7 fusion.5
  719.5 22.5 %collective-permute-done.15 = bf16[256,2304]{1,0:T(8,128)(2,1)S(1)} collective-permute-done((bf16[256,2304]{1,0:T(8,128)(2,1)S(1)}, bf16[256,2304]{1,0:T(8,128)(2,1)S(1)}, u32[]{:S(2)}, u32[]{:S(2)}) %collective-permute-start.15) | collective-permute-done | bytes 1179680 | tf_op jit(solution)/shard_map/ppermute | solution.py:34
  747.3 2.6 fusion.34
  752.8 26.5 %attend_back.1 = (bf16[256,2048]{1,0:T(8,128)(2,1)}, f32[2,256,1024]{2,1,0:T(8,128)}, bf16[4,2,256,1024]{3,2,1,0:T(8,128)(2,1)}) custom-call(bf16[256,2048]{1,0:T(8,128)(2,1)} %get-tuple-element.24.refs_0_, bf16[256,2048]{1,0:T(8,128)(2,1)} %fusion.4.refs_1_, bf16[256,2048]{1,0:T(8,128)(2,1)} %copy-done.6, bf16[256,2048]{1,0:T(8,128)(2,1)} %copy-done.7, ...), custom_call_target="tpu_custom_call" | custom-call | flops 6710886400 | bytes 24117248 | tf_op jit(solution)/shard_map/attend_back/pallas_call | solution.py:432
  779.3 4.7 slice_bitcast_fusion.3
  792.5 3.0 pad_maximum_fusion.1
  795.5 5.9 copy.51
  801.5 7.4 reshape.165
  808.8 6.8 copy.52
  817.3 3.7 convert_add_fusion.3
  824.7 10.1 %fusion.31 = f32[256,2176]{1,0:T(8,128)S(1)} fusion(bf16[4096,2176]{1,0:T(8,128)(2,1)} %get-tuple-element.23.w_ref, bf16[256,1024]{1,0:T(8,128)(2,1)S(1)} %fusion.32, bf16[256,1024]{1,0:T(8,128)(2,1)S(1)} %fusion.24, bf16[256,2048]{1,0:T(8,128)(2,1)S(1)} %copy-done.31), kind=kOutput, calls=%fused_computation.67 | convolution fusion | flops 4569694208 | bytes 22151168 | tf_op jit(solution)/shard_map/dot_general | solution.py:44
  835.3 3.7 pad_maximum_fusion
  839.0 111.2 %reduce_rows.1 = f32[512,128]{1,0:T(8,128)} custom-call(f32[16384,128]{1,0:T(8,128)} %bitcast.52), custom_call_target="tpu_custom_call" | custom-call | tf_op jit(solution)/shard_map/reduce_rows/pallas_call | solution.py:240
  953.2 2.3 fusion.7
  (186 shorter events, 60.0 us)
Async XLA Ops:
  7.2 226.8 %all-gather.4.cloned.1.call-start = ((), (), s32[]{:S(2)}) async-start(), calls=%async_computation.1 | async-start | bytes 2162688 | tf_op jit(solution)/shard_map/all_gather | solution.py:616
  8.7 227.4 %all-gather.6.cloned.1.call-start = ((), (), s32[]{:S(2)}) async-start(), calls=%async_computation.2 | async-start | bytes 9191424 | tf_op jit(solution)/shard_map/all_gather | solution.py:615
  10.4 578.9 %all-gather.8.cloned.1.call-start = ((), (), s32[]{:S(2)}) async-start(), calls=%async_computation.3 | async-start | bytes 30081024 | tf_op jit(solution)/shard_map/all_gather | solution.py:628
  15.4 102.2 %copy-start.29 = (s32[15]{0:T(128)S(1)}, s32[15]{0:T(128)}, u32[]{:S(2)}) copy-start(s32[15]{0:T(128)} %param.40) | copy-start | bytes 184
  15.5 104.4 %copy-start.2 = (bf16[256,2048]{1,0:T(8,128)(2,1)S(1)}, bf16[256,2048]{1,0:T(8,128)(2,1)}, u32[]{:S(2)}) copy-start(bf16[256,2048]{1,0:T(8,128)(2,1)} %param.21) | copy-start | bytes 3145732
  15.5 800.1 %reduce-scatter.2.cloned.1.call-start = ((), (), s32[]{:S(2)}) async-start(), calls=%async_computation.4 | async-start | bytes 1769472 | tf_op jit(solution)/shard_map/reduce_scatter | solution.py:739
  16.1 104.6 %copy-start.20 = (f32[2048]{0:T(1024)}, f32[2048]{0:T(1024)S(1)}, u32[]{:S(2)}) copy-start(f32[2048]{0:T(1024)S(1)} %convert_element_type.113) | copy-start | bytes 24580
  136.3 79.7 %collective-permute-start = (bf16[256,2048]{1,0:T(8,128)(2,1)}, bf16[256,2048]{1,0:T(8,128)(2,1)S(1)}, u32[]{:S(2)}, u32[]{:S(2)}) collective-permute-start(bf16[256,2048]{1,0:T(8,128)(2,1)} %get-tuple-element.25.refs_5_.refs_10_.refs_6_.refs_11_), channel_id=1, source_target_pairs={{0,4},{1,5},{2,6},{3,7},{4,8},{5,9},{6,10},{7,11},{8,12},{9,13},{1... | collective-permute-start | bytes 3145736 | tf_op jit(solution)/shard_map/ppermute | solution.py:29
  138.4 77.6 %collective-permute-start.1 = (bf16[256,2048]{1,0:T(8,128)(2,1)}, bf16[256,2048]{1,0:T(8,128)(2,1)S(1)}, u32[]{:S(2)}, u32[]{:S(2)}) collective-permute-start(bf16[256,2048]{1,0:T(8,128)(2,1)} %get-tuple-element.25.refs_5_.refs_10_.refs_6_.refs_11_), channel_id=1, source_target_pairs={{0,3},{1,4},{2,5},{3,6},{4,7},{5,8},{6,9},{7,10},{8,11},{9,12},{10... | collective-permute-start | bytes 3145736 | tf_op jit(solution)/shard_map/ppermute | solution.py:29
  143.7 72.3 %collective-permute-start.2 = (bf16[256,2048]{1,0:T(8,128)(2,1)}, bf16[256,2048]{1,0:T(8,128)(2,1)}, u32[]{:S(2)}, u32[]{:S(2)}) collective-permute-start(bf16[256,2048]{1,0:T(8,128)(2,1)} %get-tuple-element.25.refs_5_.refs_10_.refs_6_.refs_11_), channel_id=1, source_target_pairs={{0,2},{1,3},{2,4},{3,5},{4,6},{5,7},{6,8},{7,9},{8,10},{9,11},{10,... | collective-permute-start | bytes 3145736 | tf_op jit(solution)/shard_map/ppermute | solution.py:29
  146.1 69.9 %collective-permute-start.3 = (bf16[256,2048]{1,0:T(8,128)(2,1)}, bf16[256,2048]{1,0:T(8,128)(2,1)}, u32[]{:S(2)}, u32[]{:S(2)}) collective-permute-start(bf16[256,2048]{1,0:T(8,128)(2,1)} %get-tuple-element.25.refs_5_.refs_10_.refs_6_.refs_11_), channel_id=1, source_target_pairs={{0,1},{1,2},{2,3},{3,4},{4,5},{5,6},{6,7},{7,8},{8,9},{9,10},{10,1... | collective-permute-start | bytes 3145736 | tf_op jit(solution)/shard_map/ppermute | solution.py:29
  149.8 136.5 %collective-permute-start.8 = (bf16[256,2048]{1,0:T(8,128)(2,1)}, bf16[256,2048]{1,0:T(8,128)(2,1)}, u32[]{:S(2)}, u32[]{:S(2)}) collective-permute-start(bf16[256,2048]{1,0:T(8,128)(2,1)} %param.41), channel_id=1, source_target_pairs={{0,8},{1,9},{2,10},{3,11},{4,12},{5,13},{6,14},{7,15},{8,0},{9,1},... | collective-permute-start | bytes 3145736 | tf_op jit(solution)/shard_map/ppermute | solution.py:34
  244.1 72.2 %copy-start.4 = (bf16[256,2048]{1,0:T(8,128)(2,1)}, bf16[256,2048]{1,0:T(8,128)(2,1)S(1)}, u32[]{:S(2)}) copy-start(bf16[256,2048]{1,0:T(8,128)(2,1)S(1)} %multiply_convert_fusion) | copy-start | bytes 3145732
  244.1 68.1 %collective-permute-start.5 = (bf16[256,2048]{1,0:T(8,128)(2,1)S(1)}, bf16[256,2048]{1,0:T(8,128)(2,1)S(1)}, u32[]{:S(2)}, u32[]{:S(2)}) collective-permute-start(bf16[256,2048]{1,0:T(8,128)(2,1)S(1)} %multiply_convert_fusion), channel_id=1, source_target_pairs={{0,8},{1,9},{2,10},{3,11},{4,12},{5,13},{6,14},{7,15},{8,0},{9,1},... | collective-permute-start | bytes 3145736 | tf_op jit(solution)/shard_map/ppermute | solution.py:34
  286.3 25.9 %collective-permute-start.7 = (bf16[256,2048]{1,0:T(8,128)(2,1)}, bf16[256,2048]{1,0:T(8,128)(2,1)S(1)}, u32[]{:S(2)}, u32[]{:S(2)}) collective-permute-start(bf16[256,2048]{1,0:T(8,128)(2,1)} %param.41), channel_id=1, source_target_pairs={{0,1},{1,0},{2,3},{3,2},{4,5},{5,4},{6,7},{7,6},{8,9},{9,8},{10,11... | collective-permute-start | bytes 3145736 | tf_op jit(solution)/shard_map/ppermute | solution.py:34
  286.3 27.5 %collective-permute-start.9 = (bf16[256,2048]{1,0:T(8,128)(2,1)}, bf16[256,2048]{1,0:T(8,128)(2,1)S(1)}, u32[]{:S(2)}, u32[]{:S(2)}) collective-permute-start(bf16[256,2048]{1,0:T(8,128)(2,1)} %collective-permute-done.8), channel_id=1, source_target_pairs={{0,1},{1,0},{2,3},{3,2},{4,5},{5,4},{6,7},{7,6},{8,9},{9,8},{10,11... | collective-permute-start | bytes 3145736 | tf_op jit(solution)/shard_map/ppermute | solution.py:34
  288.1 28.1 %collective-permute-start.4 = (bf16[256,2048]{1,0:T(8,128)(2,1)S(1)}, bf16[256,2048]{1,0:T(8,128)(2,1)S(1)}, u32[]{:S(2)}, u32[]{:S(2)}) collective-permute-start(bf16[256,2048]{1,0:T(8,128)(2,1)S(1)} %multiply_convert_fusion), channel_id=1, source_target_pairs={{0,1},{1,0},{2,3},{3,2},{4,5},{5,4},{6,7},{7,6},{8,9},{9,8},{10,11... | collective-permute-start | bytes 3145736 | tf_op jit(solution)/shard_map/ppermute | solution.py:34
  312.2 4.0 collective-permute-start.6
  673.4 3.7 collective-permute-start.11
  676.6 3.7 collective-permute-start.14
  677.1 6.9 collective-permute-start.10
  679.7 33.4 %collective-permute-start.12 = (bf16[256,2176]{1,0:T(8,128)(2,1)}, bf16[256,2176]{1,0:T(8,128)(2,1)}, u32[]{:S(2)}, u32[]{:S(2)}) collective-permute-start(bf16[256,2176]{1,0:T(8,128)(2,1)} %add_convert_fusion.1), channel_id=1, source_target_pairs={{0,8},{1,9},{2,10},{3,11},{4,12},{5,13},{6,14},{7,15},{8,0},{9,1},... | collective-permute-start | bytes 3342344 | tf_op jit(solution)/shard_map/ppermute | solution.py:34
  679.7 39.8 %collective-permute-start.13 = (bf16[256,2304]{1,0:T(8,128)(2,1)}, bf16[256,2304]{1,0:T(8,128)(2,1)}, u32[]{:S(2)}, u32[]{:S(2)}) collective-permute-start(bf16[256,2304]{1,0:T(8,128)(2,1)} %get-tuple-element.35), channel_id=1, source_target_pairs={{0,1},{1,0},{2,3},{3,2},{4,5},{5,4},{6,7},{7,6},{8,9},{9,8},{10,11... | collective-permute-start | bytes 3538952 | tf_op jit(solution)/shard_map/ppermute | solution.py:34
  682.2 59.8 %collective-permute-start.15 = (bf16[256,2304]{1,0:T(8,128)(2,1)S(1)}, bf16[256,2304]{1,0:T(8,128)(2,1)S(1)}, u32[]{:S(2)}, u32[]{:S(2)}) collective-permute-start(bf16[256,2304]{1,0:T(8,128)(2,1)S(1)} %add_convert_fusion), channel_id=1, source_target_pairs={{0,8},{1,9},{2,10},{3,11},{4,12},{5,13},{6,14},{7,15},{8,0},{9,1},... | collective-permute-start | bytes 3538952 | tf_op jit(solution)/shard_map/ppermute | solution.py:34
  784.0 33.3 %collective-permute-start.16 = (bf16[2,256,1024]{2,1,0:T(8,128)(2,1)}, bf16[2,256,1024]{2,1,0:T(8,128)(2,1)}, u32[]{:S(2)}, u32[]{:S(2)}) collective-permute-start(bf16[2,256,1024]{2,1,0:T(8,128)(2,1)} %get-tuple-element.39), channel_id=1, source_target_pairs={{4,0},{5,1},{6,2},{7,3},{8,4},{9,5},{10,6},{11,7},{12,8},{13,9},{1... | collective-permute-start | bytes 3145736 | tf_op jit(solution)/shard_map/ppermute | solution.py:29
  785.4 31.9 %collective-permute-start.17 = (bf16[2,256,1024]{2,1,0:T(8,128)(2,1)}, bf16[2,256,1024]{2,1,0:T(8,128)(2,1)}, u32[]{:S(2)}, u32[]{:S(2)}) collective-permute-start(bf16[2,256,1024]{2,1,0:T(8,128)(2,1)} %get-tuple-element.42), channel_id=1, source_target_pairs={{3,0},{4,1},{5,2},{6,3},{7,4},{8,5},{9,6},{10,7},{11,8},{12,9},{13... | collective-permute-start | bytes 3145736 | tf_op jit(solution)/shard_map/ppermute | solution.py:29
  786.7 30.6 %collective-permute-start.18 = (bf16[2,256,1024]{2,1,0:T(8,128)(2,1)}, bf16[2,256,1024]{2,1,0:T(8,128)(2,1)}, u32[]{:S(2)}, u32[]{:S(2)}) collective-permute-start(bf16[2,256,1024]{2,1,0:T(8,128)(2,1)} %get-tuple-element.41), channel_id=1, source_target_pairs={{2,0},{3,1},{4,2},{5,3},{6,4},{7,5},{8,6},{9,7},{10,8},{11,9},{12,... | collective-permute-start | bytes 3145736 | tf_op jit(solution)/shard_map/ppermute | solution.py:29
  788.0 29.3 %collective-permute-start.19 = (bf16[2,256,1024]{2,1,0:T(8,128)(2,1)}, bf16[2,256,1024]{2,1,0:T(8,128)(2,1)}, u32[]{:S(2)}, u32[]{:S(2)}) collective-permute-start(bf16[2,256,1024]{2,1,0:T(8,128)(2,1)} %get-tuple-element.40), channel_id=1, source_target_pairs={{1,0},{2,1},{3,2},{4,3},{5,4},{6,5},{7,6},{8,7},{9,8},{10,9},{11,1... | collective-permute-start | bytes 3145736 | tf_op jit(solution)/shard_map/ppermute | solution.py:29
  839.0 114.2 %copy-start.3 = (bf16[256,2048]{1,0:T(8,128)(2,1)S(1)}, bf16[256,2048]{1,0:T(8,128)(2,1)}, u32[]{:S(2)}) copy-start(bf16[256,2048]{1,0:T(8,128)(2,1)} %param.21) | copy-start | bytes 3145732
  839.0 114.2 %copy-start.17 = (bf16[2048,128]{1,0:T(8,128)(2,1)S(1)}, bf16[2048,128]{1,0:T(8,128)(2,1)}, u32[]{:S(2)}) copy-start(bf16[2048,128]{1,0:T(8,128)(2,1)} %get-tuple-element.22) | copy-start | bytes 1572868
  839.0 114.2 %copy-start.21 = (f32[2048]{0:T(1024)S(1)}, f32[2048]{0:T(1024)}, u32[]{:S(2)}) copy-start(f32[2048]{0:T(1024)} %copy-done.20) | copy-start | bytes 24580
  839.0 114.2 %copy-start.24 = (f32[256]{0:T(256)S(1)}, f32[256]{0:T(256)}, u32[]{:S(2)}) copy-start(f32[256]{0:T(256)} %copy-done.23) | copy-start | bytes 3076
  (29 other events, 162.3 us)
Sparse Core Ops, SparseCore 0:
  11.4 69.8 all-gather.3
  84.1 118.4 all-gather.5
  204.8 384.4 all-gather.7
  680.4 50.9 reduce-scatter.1

commit v2 on v1

v2 whole, which is shorter than its diff:
```python
import functools
import math

import jax
import jax.numpy as jnp
from jax import lax
from jax.experimental import pallas as pl
from jax.experimental.pallas import tpu as pltpu
from jax.sharding import PartitionSpec as P


HEADS = 16
KV_HEADS = 8
HEAD_WIDTH = 128
ADAPTER_RANK = 16
REACH = 4

EPSILON = 1e-05
ADAPTER_SCALE = 0.5
ROTARY_BASE = 1000000.0
MASKED = -1e30
MESH = pl.DeviceIdType.MESH
AXIS = "fsdp"
VMEM_LIMIT = 60 * 1024 * 1024


def swapped(value, bit):
    count = lax.axis_size(AXIS)
    return lax.ppermute(value, AXIS, [(source, source ^ bit) for source in range(count)])


def project(left, right):
    return lax.dot_general(
        left, right, (((1,), (1,)), ((), ())), preferred_element_type=jnp.float32
    )


def product(left, right):
    return jnp.dot(left, right, preferred_element_type=jnp.float32)


def contract_rows(left, right):
    return lax.dot_general(
        left, right, (((0,), (0,)), ((), ())), preferred_element_type=jnp.float32
    )


def sequence_info(lengths, adapter_set, index):
    ends = jnp.cumsum(lengths)
    starts = ends - lengths
    member = (index[:, None] >= starts[None, :]) & (index[:, None] < ends[None, :])
    labels = lax.iota(jnp.int32, lengths.shape[0]) + 1
    sequence = jnp.sum(jnp.where(member, labels[None, :], 0), axis=1) - 1
    begin = jnp.sum(jnp.where(member, starts[None, :], 0), axis=1)
    chosen = jnp.sum(jnp.where(member, adapter_set[None, :], 0), axis=1)
    return (sequence, index - begin, chosen)


def adapter_mask(chosen, columns):
    column_set = lax.broadcasted_iota(jnp.int32, (1, columns), 1) // ADAPTER_RANK
    return column_set == chosen[:, None]


def masked(values, select):
    return jnp.where(select, values, 0.0).astype(jnp.bfloat16)


def rotary_tables(position):
    half = HEAD_WIDTH // 2
    inverse = jnp.exp(lax.iota(jnp.float32, half) * (-2.0 * math.log(ROTARY_BASE) / HEAD_WIDTH))
    angles = position.astype(jnp.float32)[:, None] * inverse[None, :]
    cosine, sine = jnp.cos(angles), jnp.sin(angles)
    return (
        jnp.concatenate([cosine, cosine], axis=1),
        jnp.concatenate([-sine, sine], axis=1),
    )


def norm_forward(values, gain):
    scale = lax.rsqrt(jnp.mean(values * values, axis=-1, keepdims=True) + EPSILON)
    unit = values * scale
    return (unit * gain, unit, scale)


def norm_backward(grad, unit, scale, gain):
    weighted = grad * gain
    return scale * (weighted - unit * jnp.mean(weighted * unit, axis=-1, keepdims=True))


def partner_of(me, bit):
    return me + bit - 2 * bit * ((me // bit) % 2)


def peer_of(me, mask):
    bit = 1
    while bit <= mask:
        if mask & bit:
            me = partner_of(me, bit)
        bit *= 2
    return me


def enter(me, bits):
    barrier = pltpu.get_barrier_semaphore()
    for bit in bits:
        pl.semaphore_signal(
            barrier, inc=1, device_id=(partner_of(me, bit),), device_id_type=MESH
        )
    pl.semaphore_wait(barrier, len(bits))


def span(bits):
    held = [0]
    for bit in bits:
        held = held + [mask + bit for mask in held]
    return held


def gather_kernel(parts, slots, bits_moved, count, *refs):
    moved = len(bits_moved)
    ins, more = refs[:count], refs[count : count + (moved > 0)]
    outs = refs[count + len(more) : 2 * count + len(more)]
    away = refs[2 * count + len(more) : 2 * count + len(more) + moved]
    send, recv, local = refs[2 * count + len(more) + moved :]
    me = lax.axis_index(AXIS)
    enter(me, sorted({bit for part in parts for bit in part[3]}))

    def block(p, mask):
        a, first, number, _ = parts[p]
        rows = ins[a].shape[0]
        start = pl.multiple_of(peer_of(me, mask) % slots[a] * rows + first, 8)
        return outs[a].at[pl.ds(start, number)]

    def own(p):
        a, first, number, _ = parts[p]
        return ins[a].at[pl.ds(first, number)]

    def copy(p, mask, bit):
        return pltpu.make_async_remote_copy(
            src_ref=own(p) if mask == 0 else block(p, mask),
            dst_ref=block(p, mask),
            send_sem=send.at[p, mask + bit],
            recv_sem=recv.at[p, mask + bit],
            device_id=(partner_of(me, bit),),
            device_id_type=MESH,
        )

    def arrive(p, mask, bit):
        pltpu.make_async_remote_copy(
            src_ref=block(p, mask),
            dst_ref=block(p, mask),
            send_sem=send.at[p, mask],
            recv_sem=recv.at[p, mask],
            device_id=(partner_of(me, bit),),
            device_id_type=MESH,
        ).wait_recv()

    sends, arrivals = [], []
    for p, (_, _, _, order) in enumerate(parts):
        for level, bit in enumerate(order):
            first = copy(p, 0, bit)
            first.start()
            sends.append(first)
            for place, mask in enumerate(span(order[:level])):
                arrivals.append(((level, place, p), p, mask + bit, bit, order[level + 1 :]))
    kept = []
    for p in range(len(parts)):
        kept.append(pltpu.make_async_copy(own(p), block(p, 0), local.at[p]))
        kept[-1].start()
    arrivals.sort(key=lambda entry: entry[0])
    moves = [
        pltpu.make_async_remote_copy(
            src_ref=more[0],
            dst_ref=away[i],
            send_sem=send.at[len(parts), i],
            recv_sem=recv.at[len(parts), i],
            device_id=(partner_of(me, bit),),
            device_id_type=MESH,
        )
        for i, bit in enumerate(bits_moved)
    ]
    waiting = True
    for (level, _, _), p, mask, bit, later in arrivals:
        if waiting and level == 1:
            waiting = False
            for move in moves:
                move.start()
        arrive(p, mask, bit)
        for following in later:
            onward = copy(p, mask, following)
            onward.start()
            sends.append(onward)
    for move in moves:
        move.wait()
    for sent in sends:
        sent.wait_send()
    for copied in kept:
        copied.wait()


def gather_rows(arrays, parts, collective_id, slots, moved=None, bits_moved=()):
    count, devices = len(arrays), lax.axis_size(AXIS)
    shapes = [
        jax.ShapeDtypeStruct((times * a.shape[0], a.shape[1]), a.dtype)
        for a, times in zip(arrays, slots, strict=True)
    ]
    sent = 2 * sum(math.prod(shape.shape) for shape in shapes)
    if moved is not None:
        arrays = list(arrays) + [moved]
        shapes += [jax.ShapeDtypeStruct(moved.shape, moved.dtype)] * len(bits_moved)
    return pl.pallas_call(
        functools.partial(gather_kernel, parts, slots, bits_moved, count),
        out_shape=shapes,
        in_specs=[pl.BlockSpec(memory_space=pl.ANY)] * len(arrays),
        out_specs=[pl.BlockSpec(memory_space=pl.ANY)] * len(shapes),
        scratch_shapes=[
            pltpu.SemaphoreType.DMA((len(parts) + 1, devices)),
            pltpu.SemaphoreType.DMA((len(parts) + 1, devices)),
            pltpu.SemaphoreType.DMA((len(parts),)),
        ],
        compiler_params=pltpu.CompilerParams(
            collective_id=collective_id, has_side_effects=True
        ),
        cost_estimate=pl.CostEstimate(flops=0, bytes_accessed=8 * sent, transcendentals=0),
        name="gather_rows",
    )(*arrays)


class Halving:
    def __init__(self, me, parts, ins, outs, totals, outgoing, incoming, send, recv):
        self.me, self.parts, self.ins, self.outs = me, parts, ins, outs
        self.totals, self.outgoing, self.incoming = totals, outgoing, incoming
        self.send, self.recv = send, recv
        self.live = [sorted(span(part[4])) for part in parts]
        self.slots = [{mask: at for at, mask in enumerate(masks)} for masks in self.live]
        self.held = []
        for part, masks in zip(parts, self.live, strict=True):
            sent = part[4][0] if ins[part[5][0]].dtype == jnp.bfloat16 else 0
            kept = [mask for mask in masks if not mask & sent]
            self.held.append({mask: at for at, mask in enumerate(kept)})
        self.pending = [[] for _ in parts]
        self.every = []
        self.levels = max(len(part[4]) for part in parts)

    def given(self, p, mask):
        _, block, first, rows, _, places = self.parts[p]
        a, place = places
        if isinstance(place, int):
            start = pl.multiple_of(peer_of(self.me, mask) % place * block + first, 8)
        else:
            start = place[mask] * block + first
        return self.ins[a].at[pl.ds(start, rows)]

    def launch(self, p, level):
        bit = self.parts[p][4][level]
        leaving = [mask for mask in self.live[p] if mask & bit]
        self.live[p] = [mask for mask in self.live[p] if not mask & bit]
        for mask in leaving:
            at = self.slots[p][mask]
            source = self.given(p, mask) if level == 0 else None
            if source is None or source.dtype != jnp.bfloat16:
                place = self.held[p][mask]
                value = self.totals[p][place] if level else source[...]
                self.outgoing[p][place] = value.astype(jnp.bfloat16)
                source = self.outgoing[p].at[place]
            copy = pltpu.make_async_remote_copy(
                src_ref=source,
                dst_ref=self.incoming[p].at[at],
                send_sem=self.send.at[p, at],
                recv_sem=self.recv.at[p, at],
                device_id=(partner_of(self.me, bit),),
                device_id_type=MESH,
            )
            copy.start()
            self.pending[p].append((mask, bit, copy))
            self.every.append(copy)

    def begin(self):
        for p in range(len(self.parts)):
            self.launch(p, 0)

    def advance(self, level):
        for p in range(len(self.parts)):
            if level >= len(self.parts[p][4]):
                continue
            arrived, self.pending[p] = self.pending[p], []
            for mask, bit, copy in arrived:
                copy.wait_recv()
                onto, wide = self.held[p][mask - bit], jnp.float32
                if level:
                    held = self.totals[p][onto]
                else:
                    held = self.given(p, mask - bit)[...].astype(wide)
                came = self.incoming[p][self.slots[p][mask]].astype(wide)
                self.totals[p][onto] = held + came
            if level + 1 < len(self.parts[p][4]):
                self.launch(p, level + 1)

    def finish(self):
        for p, (a, _, first, rows, _, _) in enumerate(self.parts):
            self.outs[a][first : first + rows, :] = self.totals[p][0]
        for copy in self.every:
            copy.wait_send()


def reduce_kernel(parts, counts, *refs):
    inputs, outputs = counts
    number = len(parts)
    ins, outs = refs[:inputs], refs[inputs : inputs + outputs]
    rest = refs[inputs + outputs :]
    buffers = (rest[i * number : (i + 1) * number] for i in range(3))
    me = lax.axis_index(AXIS)
    enter(me, sorted({bit for part in parts for bit in part[4]}))
    halving = Halving(me, parts, ins, outs, *buffers, *rest[3 * number :])
    halving.begin()
    for level in range(halving.levels):
        halving.advance(level)
    halving.finish()


def reduce_plan(values, sums):
    parts, shapes, scratch = [], [], []
    for a, (places, orders) in enumerate(sums):
        members = 1 << len(orders[0])
        source = places[0]
        block = values[source].shape[0] // members
        columns = values[source].shape[1]
        shapes.append(jax.ShapeDtypeStruct((block, columns), jnp.float32))
        pieces = len(orders) if block % (16 * len(orders)) == 0 else 1
        rows = block // pieces
        for i in range(pieces):
            parts.append((a, block, i * rows, rows, orders[i], places))
            held = members // 2 if values[source].dtype == jnp.bfloat16 else members
            scratch.append(((held, rows, columns), (members, rows, columns)))
    most = max(shape[0] for _, shape in scratch)
    buffers = [pltpu.VMEM(shape, jnp.float32) for shape, _ in scratch]
    buffers += [pltpu.VMEM(shape, jnp.bfloat16) for shape, _ in scratch]
    buffers += [pltpu.VMEM(shape, jnp.bfloat16) for _, shape in scratch]
    buffers += [pltpu.SemaphoreType.DMA((len(parts), most))] * 2
    return tuple(parts), shapes, buffers


def reduce_rows(values, sums, collective_id):
    parts, shapes, buffers = reduce_plan(values, sums)
    sent = 2 * sum(value.size for value in values)
    return pl.pallas_call(
        functools.partial(reduce_kernel, parts, (len(values), len(sums))),
        out_shape=shapes,
        in_specs=[pl.BlockSpec(memory_space=pltpu.VMEM)] * len(values),
        out_specs=[pl.BlockSpec(memory_space=pltpu.VMEM)] * len(sums),
        scratch_shapes=buffers,
        compiler_params=pltpu.CompilerParams(
            collective_id=collective_id, has_side_effects=True, vmem_limit_bytes=VMEM_LIMIT
        ),
        cost_estimate=pl.CostEstimate(flops=0, bytes_accessed=16 * sent, transcendentals=0),
        name="reduce_rows",
    )(*values)


def greet(me, devices, steps, bits=(1,)):
    barrier = pltpu.get_barrier_semaphore()
    for bit in bits:
        pl.semaphore_signal(
            barrier, inc=1, device_id=(partner_of(me, bit),), device_id_type=MESH
        )
    for step in steps:
        for there in (me + step, me - step):
            pl.semaphore_signal(
                barrier, inc=1, device_id=((there + devices) % devices,), device_id_type=MESH
            )
    pl.semaphore_wait(barrier, len(bits) + 2 * len(steps))


def context_kernel(devices, pair_ref, out_ref, zero, send, recv, local):
    me = lax.axis_index(AXIS)
    greet(me, devices, (2, 4))
    even = me % 2 == 0
    partner = partner_of(me, 1)

    def copy(i, source, slot, there):
        return pltpu.make_async_remote_copy(
            src_ref=source,
            dst_ref=out_ref.at[slot],
            send_sem=send.at[i],
            recv_sem=recv.at[slot],
            device_id=(there,),
            device_id_type=MESH,
        )

    def arrive(slot):
        copy(0, out_ref.at[slot], slot, partner).wait_recv()

    two = copy(0, pair_ref, 2, (me + 2) % devices)
    four = copy(1, pair_ref, 0, (me + 4) % devices)
    own = copy(2, pair_ref, 3, partner)
    two_even = copy(3, out_ref.at[2], 1, partner)
    two_odd = copy(3, out_ref.at[2], 3, partner)
    four_odd = copy(2, out_ref.at[0], 1, partner)
    has_two, has_four = me >= 2, me >= 4

    @pl.when(me + 2 < devices)
    def _():
        two.start()

    @pl.when(me + 4 < devices)
    def _():
        four.start()

    @pl.when(even)
    def _():
        own.start()

    @pl.when(me < 4)
    def _():
        zero[...] = jnp.zeros_like(zero)
        pltpu.make_async_copy(zero, out_ref.at[0], local.at[0]).start()

    @pl.when(me < 2)
    def _():
        pltpu.make_async_copy(zero, out_ref.at[2], local.at[2]).start()

    lacks_three = me < 3
    lacks_one = me < 1

    @pl.when(lacks_three)
    def _():
        pltpu.make_async_copy(zero, out_ref.at[1], local.at[1]).start()

    @pl.when(lacks_one)
    def _():
        pltpu.make_async_copy(zero, out_ref.at[3], local.at[3]).start()

    @pl.when(has_two)
    def _():
        arrive(2)

    @pl.when(has_two & even)
    def _():
        two_even.start()

    @pl.when(has_two & (me % 2 == 1))
    def _():
        two_odd.start()

    @pl.when(has_four)
    def _():
        arrive(0)

    @pl.when(has_four & (me % 2 == 1))
    def _():
        four_odd.start()

    @pl.when(me >= 1)
    def _():
        arrive(3)

    @pl.when(me >= 3)
    def _():
        arrive(1)

    for lacks, slot in ((me < 4, 0), (me < 3, 1), (me < 2, 2), (me < 1, 3)):

        @pl.when(lacks)
        def _(slot=slot):
            pltpu.make_async_copy(zero, out_ref.at[slot], local.at[slot]).wait()

    @pl.when(me + 2 < devices)
    def _():
        two.wait_send()

    @pl.when(me + 4 < devices)
    def _():
        four.wait_send()

    @pl.when(even)
    def _():
        own.wait_send()

    @pl.when(has_two)
    def _():
        two_even.wait_send()

    @pl.when(has_four & (me % 2 == 1))
    def _():
        four_odd.wait_send()


def context_of(pair, collective_id):
    devices = lax.axis_size(AXIS)
    return pl.pallas_call(
        functools.partial(context_kernel, devices),
        out_shape=jax.ShapeDtypeStruct((REACH,) + pair.shape, pair.dtype),
        in_specs=[pl.BlockSpec(memory_space=pl.ANY)],
        out_specs=pl.BlockSpec(memory_space=pl.ANY),
        scratch_shapes=[
            pltpu.VMEM(pair.shape, pair.dtype),
            pltpu.SemaphoreType.DMA((REACH,)),
            pltpu.SemaphoreType.DMA((REACH,)),
            pltpu.SemaphoreType.DMA((REACH,)),
        ],
        compiler_params=pltpu.CompilerParams(
            collective_id=collective_id, has_side_effects=True, vmem_limit_bytes=VMEM_LIMIT
        ),
        cost_estimate=pl.CostEstimate(
            flops=0, bytes_accessed=64 * pair.size, transcendentals=0
        ),
        name="context",
    )(pair)


def context_back_kernel(devices, parts, away, own, mixed, *refs):
    out_ref, sum_ref, beside, going, coming, send, recv = refs[:7]
    number = len(parts)
    buffers = (refs[7 + i * number : 7 + (i + 1) * number] for i in range(3))
    me = lax.axis_index(AXIS)
    bits = sorted({bit for part in parts for bit in part[4]})
    greet(me, devices, (2, 4), bits)
    halving = Halving(me, parts, [mixed], [sum_ref], *buffers, *refs[7 + 3 * number :])
    even = me % 2 == 0
    partner = partner_of(me, 1)
    wide, narrow = jnp.float32, jnp.bfloat16

    def copy(i, h, source, target, there):
        return pltpu.make_async_remote_copy(
            src_ref=source,
            dst_ref=target,
            send_sem=send.at[h, i],
            recv_sem=recv.at[h, i],
            device_id=(there,),
            device_id_type=MESH,
        )

    shared = []
    for h in range(2):
        for i, slot in enumerate((3, 1)):
            shared.append(copy(i, h, away.at[slot, h], beside.at[i, h], partner))
            shared[-1].start()
    halving.begin()
    out_ref[...] = own[...]
    far = []
    for h in range(2):
        for i in range(2):
            shared[2 * h + i].wait_recv()
        one, three = beside[0, h].astype(wide), beside[1, h].astype(wide)
        going[0, h] = (away[2, h].astype(wide) + jnp.where(even, three, one)).astype(narrow)
        going[1, h] = (away[0, h].astype(wide) + jnp.where(even, 0.0, three)).astype(narrow)
        out_ref[h] += jnp.where(even, one, 0.0)
        for i, step in enumerate((2, 4)):
            move = copy(
                2 + i, h, going.at[i, h], coming.at[i, h], (me - step + devices) % devices
            )
            far.append((i, h, step, move))

            @pl.when(me >= step)
            def _(move=move):
                move.start()

    for level in range(halving.levels):
        halving.advance(level)
    for i, h, step, move in far:

        @pl.when(me + step < devices)
        def _(i=i, h=h, move=move):
            move.wait_recv()
            out_ref[h] += coming[i, h].astype(wide)

    halving.finish()
    for move in shared:
        move.wait_send()
    for i, h, step, move in far:

        @pl.when(me >= step)
        def _(move=move):
            move.wait_send()


def context_back(away, own, mixed, sums, collective_id):
    devices = lax.axis_size(AXIS)
    half = (2,) + own.shape
    parts, shapes, buffers = reduce_plan([mixed], sums)
    return pl.pallas_call(
        functools.partial(context_back_kernel, devices, parts),
        out_shape=[jax.ShapeDtypeStruct(own.shape, jnp.float32)] + shapes,
        in_specs=[pl.BlockSpec(memory_space=pltpu.VMEM)] * 3,
        out_specs=[pl.BlockSpec(memory_space=pltpu.VMEM)] * 2,
        scratch_shapes=[
            pltpu.VMEM(half, jnp.bfloat16),
            pltpu.VMEM(half, jnp.bfloat16),
            pltpu.VMEM(half, jnp.bfloat16),
            pltpu.SemaphoreType.DMA((2, 4)),
            pltpu.SemaphoreType.DMA((2, 4)),
        ]
        + buffers,
        compiler_params=pltpu.CompilerParams(
            collective_id=collective_id, has_side_effects=True, vmem_limit_bytes=VMEM_LIMIT
        ),
        cost_estimate=pl.CostEstimate(flops=0, bytes_accessed=64 * own.size, transcendentals=0),
        name="context_back",
    )(away, own, mixed)


def joined_kernel(turned, x_ref, w_ref, cos_ref, sin_ref, query_ref, pair_ref):
    step = pl.program_id(0)
    values = project(x_ref[...], w_ref[...])
    cosine, sine = cos_ref[...], sin_ref[...]
    heads = values.shape[1] // HEAD_WIDTH
    turn = step < turned
    pieces = []
    for h in range(heads):
        head = values[:, h * HEAD_WIDTH : (h + 1) * HEAD_WIDTH]
        rotated = head * cosine + pltpu.roll(head, HEAD_WIDTH // 2, 1) * sine
        pieces.append(jnp.where(turn, rotated, head).astype(jnp.bfloat16))
    result = jnp.concatenate(pieces, axis=1)
    half = pl.num_programs(0) // 2

    @pl.when(step < half)
    def _():
        query_ref[...] = result

    @pl.when(step >= half)
    def _():
        pair_ref[...] = result


def joined_heads(x, weight, cosine, sine):
    number, depth = x.shape
    tile = 512
    steps = weight.shape[0] // tile
    half = steps // 2
    turned = (HEADS + KV_HEADS) * HEAD_WIDTH // tile
    wide = half * tile
    return pl.pallas_call(
        functools.partial(joined_kernel, turned),
        out_shape=[jax.ShapeDtypeStruct((number, wide), jnp.bfloat16)] * 2,
        grid=(steps,),
        in_specs=[
            pl.BlockSpec((number, depth), lambda j: (0, 0), pipeline_mode=pl.Buffered(1)),
            pl.BlockSpec((tile, depth), lambda j: (j, 0)),
            pl.BlockSpec((number, HEAD_WIDTH), lambda j: (0, 0)),
            pl.BlockSpec((number, HEAD_WIDTH), lambda j: (0, 0)),
        ],
        out_specs=[
            pl.BlockSpec((number, tile), lambda j: (0, jnp.minimum(j, half - 1))),
            pl.BlockSpec((number, tile), lambda j: (0, jnp.maximum(j - half, 0))),
        ],
        compiler_params=pltpu.CompilerParams(vmem_limit_bytes=VMEM_LIMIT),
        cost_estimate=pl.CostEstimate(
            flops=2 * number * depth * weight.shape[0],
            bytes_accessed=2 * weight.size + 4 * x.size,
            transcendentals=0,
        ),
        name="joined_heads",
    )(x, weight, cosine, sine)


def make_bias(query_seq, key_seq, bias_ref):
    number, keys = bias_ref.shape
    row = lax.broadcasted_iota(jnp.int32, (number, keys), 0) + (keys - number)
    column = lax.broadcasted_iota(jnp.int32, (number, keys), 1)
    allowed = (query_seq == key_seq) & (column <= row)
    bias_ref[...] = jnp.where(allowed, 0.0, MASKED)


def softmax_of(query, keys, bias):
    scale = HEAD_WIDTH ** (-0.5)
    scores = jnp.concatenate([project(query, key) for key in keys], axis=1) * scale + bias
    top = jnp.max(scores, axis=-1, keepdims=True)
    weights = jnp.exp(scores - top)
    return weights * (1.0 / jnp.sum(weights, axis=-1, keepdims=True))


def attend_kernel(blocks, *refs):
    q_ref = refs[0]
    k_refs = refs[1 : 1 + blocks]
    v_refs = refs[1 + blocks : 1 + 2 * blocks]
    qs_ref, ks_ref, out_ref, bias_ref = refs[1 + 2 * blocks :]

    @pl.when(pl.program_id(0) == 0)
    def _():
        make_bias(qs_ref[...], ks_ref[...], bias_ref)

    keys = [ref[...] for ref in k_refs]
    number = keys[0].shape[0]
    for g in range(HEADS // KV_HEADS):
        columns = slice(g * HEAD_WIDTH, (g + 1) * HEAD_WIDTH)
        probs = softmax_of(q_ref[:, columns], keys, bias_ref[...]).astype(jnp.bfloat16)
        result = product(probs[:, :number], v_refs[0][...])
        for b in range(1, blocks):
            result += product(probs[:, b * number : (b + 1) * number], v_refs[b][...])
        out_ref[:, columns] = result.astype(jnp.bfloat16)


def context_specs(number, blocks):
    def at(b, shift):
        if b == blocks - 1:
            return pl.BlockSpec((number, HEAD_WIDTH), lambda j: (0, shift + j))
        return pl.BlockSpec((None, number, HEAD_WIDTH), lambda j: (b, 0, shift + j))

    return [at(b, 0) for b in range(blocks)] + [at(b, KV_HEADS) for b in range(blocks)]


def attend(query, context, pair, query_seq, key_seq):
    number, blocks = query.shape[0], context.shape[0] + 1
    pairs = [context] * (blocks - 1) + [pair]
    group = HEADS // KV_HEADS
    keys = blocks * number
    wide_spec = pl.BlockSpec((number, group * HEAD_WIDTH), lambda j: (0, j))
    return pl.pallas_call(
        functools.partial(attend_kernel, blocks),
        out_shape=jax.ShapeDtypeStruct(query.shape, jnp.bfloat16),
        grid=(KV_HEADS,),
        in_specs=[wide_spec]
        + context_specs(number, blocks)
        + [
            pl.BlockSpec((number, 1), lambda j: (0, 0)),
            pl.BlockSpec((1, keys), lambda j: (0, 0)),
        ],
        out_specs=wide_spec,
        scratch_shapes=[pltpu.VMEM((number, keys), jnp.float32)],
        compiler_params=pltpu.CompilerParams(vmem_limit_bytes=VMEM_LIMIT),
        cost_estimate=pl.CostEstimate(
            flops=4 * HEADS * number * keys * HEAD_WIDTH,
            bytes_accessed=4 * query.size + 2 * blocks * pair.size,
            transcendentals=HEADS * number * keys,
        ),
        name="attend",
    )(query, *pairs, *pairs, query_seq, key_seq)


def attend_back_kernel(blocks, *refs):
    q_ref, g_ref = refs[:2]
    k_refs = refs[2 : 2 + blocks]
    v_refs = refs[2 + blocks : 2 + 2 * blocks]
    qs_ref, ks_ref, cos_ref, sin_ref = refs[2 + 2 * blocks : 6 + 2 * blocks]
    dq_ref, own_ref, away_ref, bias_ref = refs[6 + 2 * blocks :]

    @pl.when(pl.program_id(0) == 0)
    def _():
        make_bias(qs_ref[...], ks_ref[...], bias_ref)

    scale = HEAD_WIDTH ** (-0.5)
    keys = [ref[...] for ref in k_refs]
    number = keys[0].shape[0]
    key_back = [None] * blocks
    value_back = [None] * blocks
    for g in range(HEADS // KV_HEADS):
        columns = slice(g * HEAD_WIDTH, (g + 1) * HEAD_WIDTH)
        query, grad = q_ref[:, columns], g_ref[:, columns]
        probs = softmax_of(query, keys, bias_ref[...])
        back = jnp.concatenate([project(grad, ref[...]) for ref in v_refs], axis=1)
        center = jnp.sum(back * probs, axis=-1, keepdims=True)
        score_back = (probs * (back - center)).astype(jnp.bfloat16)
        probs = probs.astype(jnp.bfloat16)
        total = None
        for b in range(blocks):
            rows = slice(b * number, (b + 1) * number)
            part = product(score_back[:, rows], keys[b])
            total = part if total is None else total + part
            to_key = contract_rows(score_back[:, rows], query)
            to_value = contract_rows(probs[:, rows], grad)
            key_back[b] = to_key if g == 0 else key_back[b] + to_key
            value_back[b] = to_value if g == 0 else value_back[b] + to_value
        total = total * scale
        turned = total * cos_ref[...] - pltpu.roll(total, HEAD_WIDTH // 2, 1) * sin_ref[...]
        dq_ref[:, columns] = turned.astype(jnp.bfloat16)
    for b in range(blocks - 1):
        away_ref[b, 0] = (key_back[b] * scale).astype(jnp.bfloat16)
        away_ref[b, 1] = value_back[b].astype(jnp.bfloat16)
    own_ref[0] = key_back[blocks - 1] * scale
    own_ref[1] = value_back[blocks - 1]


def attend_back(query, grad, context, pair, query_seq, key_seq, cosine, sine):
    number, blocks = query.shape[0], context.shape[0] + 1
    pairs = [context] * (blocks - 1) + [pair]
    group = HEADS // KV_HEADS
    keys = blocks * number
    wide = KV_HEADS * HEAD_WIDTH
    wide_spec = pl.BlockSpec((number, group * HEAD_WIDTH), lambda j: (0, j))
    fixed = pl.BlockSpec((number, HEAD_WIDTH), lambda j: (0, 0))
    return pl.pallas_call(
        functools.partial(attend_back_kernel, blocks),
        out_shape=[
            jax.ShapeDtypeStruct(query.shape, jnp.bfloat16),
            jax.ShapeDtypeStruct((2, number, wide), jnp.float32),
            jax.ShapeDtypeStruct((blocks - 1, 2, number, wide), jnp.bfloat16),
        ],
        grid=(KV_HEADS,),
        in_specs=[wide_spec, wide_spec]
        + context_specs(number, blocks)
        + [
            pl.BlockSpec((number, 1), lambda j: (0, 0)),
            pl.BlockSpec((1, keys), lambda j: (0, 0)),
            fixed,
            fixed,
        ],
        out_specs=[
            wide_spec,
            pl.BlockSpec((2, number, HEAD_WIDTH), lambda j: (0, 0, j)),
            pl.BlockSpec((blocks - 1, 2, number, HEAD_WIDTH), lambda j: (0, 0, 0, j)),
        ],
        scratch_shapes=[pltpu.VMEM((number, keys), jnp.float32)],
        compiler_params=pltpu.CompilerParams(vmem_limit_bytes=VMEM_LIMIT),
        cost_estimate=pl.CostEstimate(
            flops=10 * HEADS * number * keys * HEAD_WIDTH,
            bytes_accessed=6 * query.size + 8 * blocks * pair.size,
            transcendentals=HEADS * number * keys,
        ),
        name="attend_back",
    )(query, grad, *pairs, *pairs, query_seq, key_seq, cosine, sine)


def feed_kernel(pieces, joint, *refs):
    x_ref, c_ref, gl_ref, ul_ref, db_ref = refs[:5]
    w_refs = refs[5 : 5 + pieces]
    mixed_ref, back_ref, grads_ref, weights, mixed_acc, back_acc, arrival = refs[5 + pieces :]
    step = pl.program_id(0)
    width, columns = x_ref.shape[1], gl_ref.shape[1]
    rounds, hid = weights.shape[0], weights.shape[1] // 3
    height = hid // joint
    main, side = slice(0, width), slice(width, width + columns)

    def load(i, at, place):
        return [
            pltpu.make_async_copy(
                w_refs[i].at[pl.ds(j * height, height)],
                weights.at[at, pl.ds(j * hid + place * height, height)],
                arrival.at[at, place, j],
            )
            for j in range(3)
        ]

    @pl.when(step == 0)
    def _():
        for i in range(pieces):
            for copy in load(i, i // joint, i % joint):
                copy.start()
        grads_ref[...] = jnp.zeros_like(grads_ref)

    mixed_acc[...] = jnp.zeros_like(mixed_acc)
    back_acc[...] = jnp.zeros_like(back_acc)

    @pl.loop(0, rounds)
    def _(i):
        @pl.when(step == 0)
        def _():
            for place in range(joint):
                for copy in load(0, i, place):
                    copy.wait()

        wg, wu, wd = (weights.at[i, pl.ds(j * hid, hid)] for j in range(3))
        x, gl, ul, db = x_ref[...], gl_ref[...], ul_ref[...], db_ref[...]
        gate = project(x, wg[:, main]) + project(gl, wg[:, side])
        up = project(x, wu[:, main]) + project(ul, wu[:, side])
        back = project(c_ref[...], wd[:, main]) + project(db, wd[:, side])
        sigma = 1.0 / (1.0 + jnp.exp(-gate))
        active = gate * sigma
        hidden = (active * up).astype(jnp.bfloat16)
        gate_back = (back * up * sigma * (1.0 + gate * (1.0 - sigma))).astype(jnp.bfloat16)
        up_back = (back * active).astype(jnp.bfloat16)
        mixed_acc[...] += product(hidden, wd[...])
        back_acc[:, main] += product(gate_back, wg[:, main]) + product(up_back, wu[:, main])
        back_acc[:, side] += product(gate_back, wg[:, side])
        back_acc[:, width + columns :] += product(up_back, wu[:, side])
        at = pl.ds(pl.multiple_of(i * hid, hid), hid)
        grads_ref[at, :columns] += contract_rows(gate_back, gl)
        grads_ref[at, columns : 2 * columns] += contract_rows(up_back, ul)
        grads_ref[at, 2 * columns :] += contract_rows(hidden, db)

    mixed_ref[...] = mixed_acc[...].astype(jnp.bfloat16)
    back_ref[...] = back_acc[...].astype(jnp.bfloat16)


def feed(x, cot, gate_low, up_low, down_back, weights):
    (rows, width), columns = x.shape, gate_low.shape[1]
    pieces, height = len(weights), weights[0].shape[0] // 3
    hidden, tile = pieces * height, 256
    hid = min(512, hidden)
    row = lambda wide: pl.BlockSpec((tile, wide), lambda i: (i, 0))
    size = sum(w.size for w in weights)
    return pl.pallas_call(
        functools.partial(feed_kernel, pieces, hid // height),
        out_shape=[
            jax.ShapeDtypeStruct((rows, width + columns), jnp.bfloat16),
            jax.ShapeDtypeStruct((rows, width + 2 * columns), jnp.bfloat16),
            jax.ShapeDtypeStruct((hidden, 3 * columns), jnp.float32),
        ],
        grid=(rows // tile,),
        in_specs=[row(width)] * 2
        + [row(columns)] * 3
        + [pl.BlockSpec(memory_space=pl.ANY)] * pieces,
        out_specs=[
            row(width + columns),
            row(width + 2 * columns),
            pl.BlockSpec((hidden, 3 * columns), lambda i: (0, 0)),
        ],
        scratch_shapes=[
            pltpu.VMEM((hidden // hid, 3 * hid, width + columns), jnp.bfloat16),
            pltpu.VMEM((tile, width + columns), jnp.float32),
            pltpu.VMEM((tile, width + 2 * columns), jnp.float32),
            pltpu.SemaphoreType.DMA((hidden // hid, hid // height, 3)),
        ],
        compiler_params=pltpu.CompilerParams(vmem_limit_bytes=VMEM_LIMIT),
        cost_estimate=pl.CostEstimate(
            flops=4 * rows * size,
            bytes_accessed=2 * size + 14 * rows * width,
            transcendentals=rows * hidden,
        ),
        name="feed",
    )(x, cot, gate_low, up_low, down_back, *weights)


def layer(
    tokens,
    attention_gain,
    feedforward_gain,
    joined_projection,
    output_projection,
    gate_weight,
    up_weight,
    down_weight,
    joined_adapter_input,
    joined_adapter_output,
    output_adapter_input,
    output_adapter_output,
    gate_adapter_input,
    gate_adapter_output,
    upward_adapter_input,
    upward_adapter_output,
    down_adapter_input,
    down_adapter_output,
    lengths,
    adapter_set,
    cotangent,
):
    number, width = tokens.shape
    columns = joined_adapter_input.shape[1]
    devices = lax.axis_size(AXIS)
    kv_width = KV_HEADS * HEAD_WIDTH
    bits = [1 << i for i in range(devices.bit_length() - 1)]
    core, side, line = bits[:3]
    distant = bits[:2:-1]
    middle = bits[1:-2]
    me = lax.axis_index(AXIS)
    first = me * number

    joined_shard = jnp.concatenate([joined_projection, joined_adapter_output], axis=1)
    output_shard = jnp.concatenate([output_projection, output_adapter_output], axis=1)
    entry_shard = jnp.concatenate(
        [
            output_adapter_input,
            gate_adapter_input,
            upward_adapter_input,
            down_adapter_output,
            joined_adapter_input,
        ],
        axis=1,
    )
    half_shard = gate_weight.shape[0] // 2

    def feed_half(at):
        pairs = (
            (gate_weight, gate_adapter_output),
            (up_weight, upward_adapter_output),
            (down_weight, down_adapter_input),
        )
        cut = lambda value: value[at * half_shard : (at + 1) * half_shard]
        return jnp.concatenate(
            [jnp.concatenate([cut(left), cut(right)], axis=1) for left, right in pairs], axis=0
        )

    feed_first, feed_second = feed_half(0), feed_half(1)
    rows, output_rows, entry_rows = (
        value.shape[0] for value in (joined_shard, output_shard, entry_shard)
    )
    head = tuple(bits[:-3:-1])
    up_order, down_order = tuple(middle) + (core,), tuple(middle[::-1]) + (core,)
    full_joined, full_entry, full_output, *first_moved = gather_rows(
        [joined_shard, entry_shard, output_shard],
        (
            (0, 0, rows // 2, head + up_order),
            (0, rows // 2, rows // 2, head + down_order),
            (1, 0, entry_rows, head + up_order),
            (2, 0, output_rows // 2, head + down_order),
            (2, output_rows // 2, output_rows // 2, head + up_order),
        ),
        1,
        (devices,) * 3,
        feed_first,
        tuple(distant),
    )

    def spread(piece, moved):
        pieces = [piece]
        for bit, came in zip(distant, moved, strict=True):
            pieces.append(came)
            for held in pieces[1:-1]:
                pieces.append(swapped(held, bit))
        return pieces

    full_joined, *first_moved = lax.optimization_barrier((full_joined, *first_moved))
    first_pieces = spread(feed_first, first_moved)
    full_f_entry = full_entry[:, 4 * columns :]
    full_o_entry = full_entry[:, :columns]
    full_gu_entry = full_entry[:, columns : 3 * columns]
    full_d_exit = full_entry[:, 3 * columns : 4 * columns]

    members = 1 << 3
    place = me % members
    blocks = (me - place) * number
    index = blocks + lax.iota(jnp.int32, members * number)
    all_sequence, all_position, all_chosen = sequence_info(lengths, adapter_set, index)
    all_select = adapter_mask(all_chosen, columns)
    mine = lambda value: lax.dynamic_slice_in_dim(value, place * number, number, 0)
    select = mine(all_select)
    cosine, sine = rotary_tables(mine(all_position))
    key_index = first - REACH * number + lax.iota(jnp.int32, (REACH + 1) * number)
    key_sequence, _, _ = sequence_info(lengths, adapter_set, key_index)
    query_seq = mine(all_sequence)[:, None]
    key_seq = key_sequence[None, :]

    inputs = tokens.astype(jnp.float32)
    gain_one = attention_gain.astype(jnp.float32)
    gain_two = feedforward_gain.astype(jnp.float32)

    normed_one, unit_one, scale_one = norm_forward(inputs, gain_one)
    normed_one = normed_one.astype(jnp.bfloat16)
    joined_low = masked(product(normed_one, full_f_entry), select)
    half_low = joined_low * ADAPTER_SCALE
    query, pair = joined_heads(
        jnp.concatenate([normed_one, half_low], axis=1), full_joined, cosine, sine
    )
    context = context_of(pair, 4)
    context, feed_second = lax.optimization_barrier((context, feed_second))
    second_moved = []
    for bit in distant:
        second_moved.append(swapped(feed_second, bit))
    second_pieces = spread(feed_second, second_moved)
    attended = attend(query, context, pair, query_seq, key_seq)
    output_low = masked(product(attended, full_o_entry), select)
    branch = project(
        jnp.concatenate([attended, output_low * ADAPTER_SCALE], axis=1), full_output
    )
    hidden_one = inputs + branch

    normed_two, unit_two, scale_two = norm_forward(hidden_one, gain_two)
    normed_two = normed_two.astype(jnp.bfloat16)
    half_rows = number // 2
    up_group, down_group = (side, line, core), (line, side, core)
    group_normed, group_cot = gather_rows(
        [normed_two, cotangent],
        (
            (0, 0, half_rows, up_group),
            (0, half_rows, half_rows, down_group),
            (1, 0, half_rows, up_group),
            (1, half_rows, half_rows, down_group),
        ),
        5,
        (members, members),
    )
    both = jnp.concatenate([all_select, all_select], axis=1)
    lows = masked(product(group_normed, full_gu_entry), both) * ADAPTER_SCALE
    down_back = masked(ADAPTER_SCALE * product(group_cot, full_d_exit), all_select)
    mixed_parts, back_parts, feed_grads = feed(
        group_normed,
        group_cot,
        lows[:, :columns],
        lows[:, columns:],
        down_back,
        first_pieces + second_pieces,
    )
    up_sum, down_sum = (core, side, line), (core, line, side)
    (back_sum,) = reduce_rows([back_parts], [((0, members), (up_sum, down_sum) * 2)], 6)
    low_back = masked(
        ADAPTER_SCALE * back_sum[:, width:], jnp.concatenate([select, select], axis=1)
    )
    normed_two_back = back_sum[:, :width] + project(low_back, full_gu_entry)
    hidden_back_one = cotangent.astype(jnp.float32) + norm_backward(
        normed_two_back, unit_two, scale_two, gain_two
    )
    branch_back = hidden_back_one.astype(jnp.bfloat16)

    through = product(branch_back, full_output)
    output_low_back = masked(ADAPTER_SCALE * through[:, width:], select)
    attended_back = (through[:, :width] + project(output_low_back, full_o_entry)).astype(
        jnp.bfloat16
    )
    query_back, own_back, away = attend_back(
        query, attended_back, context, pair, query_seq, key_seq, cosine, sine
    )
    group_sums = ((0, members), (up_sum, down_sum))
    pair_back, mixed_sum = context_back(away, own_back, mixed_parts, [group_sums], 7)
    down_low = masked(mixed_sum[:, width:], select)
    mixed = mixed_sum[:, :width] + ADAPTER_SCALE * project(down_low, full_d_exit)
    layer_output = (hidden_one + mixed).astype(jnp.bfloat16)

    half = HEAD_WIDTH // 2
    key_back = pair_back[0].reshape(number, KV_HEADS, HEAD_WIDTH)
    rolled = jnp.concatenate([key_back[..., half:], key_back[..., :half]], axis=-1)
    key_back = key_back * cosine[:, None, :] - rolled * sine[:, None, :]
    joined_back = jnp.concatenate(
        [
            query_back,
            key_back.reshape(number, kv_width).astype(jnp.bfloat16),
            pair_back[1].astype(jnp.bfloat16),
        ],
        axis=1,
    )
    inward = product(joined_back, full_joined)
    joined_low_back = masked(ADAPTER_SCALE * inward[:, width:], select)
    normed_one_back = inward[:, :width] + project(joined_low_back, full_f_entry)
    grad_tokens = hidden_back_one + norm_backward(normed_one_back, unit_one, scale_one, gain_one)

    orders = ((core,) + tuple(middle) + head[::-1], (core,) + tuple(middle[::-1]) + head[::-1])
    low_grads = contract_rows(normed_two, low_back)
    totals = [
        contract_rows(attended, output_low_back),
        ADAPTER_SCALE * contract_rows(branch_back, output_low),
        low_grads[:, :columns],
        low_grads[:, columns:],
        ADAPTER_SCALE * contract_rows(cotangent, down_low),
        feed_grads,
        contract_rows(joined_back, half_low),
        contract_rows(normed_one, joined_low_back),
    ]
    sums = [((at, devices), orders) for at in range(len(totals))]
    blocks = len(first_pieces)
    feed_grads = feed_grads.reshape(2, blocks, half_shard, -1).transpose(1, 0, 2, 3)
    totals[5] = feed_grads.reshape(2 * blocks * half_shard, -1)
    sums[5] = ((5, {mask: at for at, mask in enumerate(span(distant))}), (tuple(distant[::-1]),))
    reduced = reduce_rows(totals, sums, 8)
    early, late = reduced[:6], (reduced[6], reduced[7])
    feed_rows = early[5]
    return (
        layer_output,
        grad_tokens,
        late[1],
        late[0],
        early[0],
        early[1],
        early[2],
        feed_rows[:, :columns],
        early[3],
        feed_rows[:, columns : 2 * columns],
        feed_rows[:, 2 * columns :],
        early[4],
    )


def solution(mesh):
    split, copied = P(AXIS, None), P()
    placed = (split, copied, copied) + (split,) * 15 + (copied, copied, split)
    return jax.shard_map(
        layer, mesh=mesh, in_specs=placed, out_specs=(split,) * 12, check_vma=False
    )
```

time: 970 us -> 761 us (0.78)
  waiting for transfers between devices: 410 us -> 25.9 us
  Pallas kernels: 350 us -> 613 us
  starting transfers between devices: 64.7 us -> 7.81 us
  local copies, waits for them, and re-layouts: 46.9 us -> 24.9 us
  matrix products: 39.3 us -> 59.3 us
  other arithmetic: 38.9 us -> 21.9 us
  between operations: 15 us -> 1.65 us
    all_gather x3 -> x0, waiting for transfers between devices: 270 us -> none  [the longest x1 270 us: per_device(): lax.all_gather(feed_shard, AXIS, axis=0, tiled=True, axis_index_groups=gr...]
    pallas_call x3 -> x7, Pallas kernels: 293 us -> 556 us  [the longest x2 236 us: gather_rows(): pl.pallas_call(functools.partial(gather_kernel, parts, slots, bits_moved,...]
    ppermute x8 -> x0, waiting for transfers between devices: 64.6 us -> none  [shifted(): lax.ppermute(value, AXIS, [(source, source + steps) for source in range(l...]
    ppermute x12 -> x4, waiting for transfers between devices: 75.5 us -> 25.9 us  [swapped(): lax.ppermute(value, AXIS, [(source, source ^ bit) for source in range(cou...]
    ppermute x12 -> x4, starting transfers between devices: 45.7 us -> 7.81 us  [swapped(): lax.ppermute(value, AXIS, [(source, source ^ bit) for source in range(cou...]
    ppermute x8 -> x0, starting transfers between devices: 18.8 us -> none  [shifted(): lax.ppermute(value, AXIS, [(source, source + steps) for source in range(l...]
    dot_general x6, matrix products: 18.4 us -> 31.1 us  [product(): return jnp.dot(left, right, preferred_element_type=jnp.float32)]
  transfers between devices with their start and end apart: 24 -> 4, of which waited for: 5 -> 1; matrix products, arithmetic and copies ran while one was open for 9% -> 3% of each run, Pallas kernels for 16% -> 15%
where the time goes in v2:
time: 761 us; the launch traced here: 754 us
  Pallas kernels  613 us (81%)
  matrix products  59.3 us (8%)
  waiting for transfers between devices  25.9 us (3%)
  local copies, waits for them, and re-layouts  24.9 us (3%)
  other arithmetic  21.9 us (3%)
  starting transfers between devices  7.81 us (1%)
    pallas_call x2, Pallas kernels, gather_rows(): pl.pallas_call(functools.partial(gather_kernel, parts, slots, bits_moved,...  236 us
    pallas_call x1, Pallas kernels, context_back(): pl.pallas_call(functools.partial(context_back_kernel, devices, parts), ou...  98.5 us
    pallas_call x2, Pallas kernels, reduce_rows(): pl.pallas_call(functools.partial(reduce_kernel, parts, (len(values), len(...  98.1 us
    pallas_call x1, Pallas kernels, feed(): pl.pallas_call(functools.partial(feed_kernel, pieces, hid // height), out...  76.1 us
    pallas_call x1, Pallas kernels, context_of(): pl.pallas_call(functools.partial(context_kernel, devices), out_shape=jax....  46.7 us
    dot_general x6, matrix products, product(): return jnp.dot(left, right, preferred_element_type=jnp.float32)  31.1 us
    pallas_call x1, Pallas kernels, attend_back(): pl.pallas_call(functools.partial(attend_back_kernel, blocks), out_shape=[...  27 us
    ppermute x4, waiting for transfers between devices, swapped(): lax.ppermute(value, AXIS, [(source, source ^ bit) for source in range(cou...  25.9 us
  transfers between devices with their start and end apart: 4, of which 1 were waited for; matrix products, arithmetic and copies ran while one was open for 3% of the time, Pallas kernels for 15%

profile of v2, /device:TPU:0, one launch (start us, length us, event | category | flops | bytes accessed | tf_op | source)
XLA Modules:
  0.0 754.2 jit_solution(7308329859371954142)
XLA Ops:
  13.5 5.3 maximum_maximum_fusion
  18.9 142.3 %gather_rows.2 = (bf16[4096,2176]{1,0:T(8,128)(2,1)}, bf16[2048,640]{1,0:T(8,128)(2,1)}, bf16[2048,2176]{1,0:T(8,128)(2,1)}, bf16[384,2176]{1,0:T(8,128)(2,1)}, bf16[384,2176]{1,0:T(8,128)(2,1)}) custom-call(bf16[128,2176]{1,0:T(8,128)(2,1)} %pad_maximum_fusion.4.refs_0_, bf16[64,640]{1,0:T(8,128)(2,1)} %copy-done.25, ...), custom_call_target="tpu_custom_call" | custom-call | bytes 234881024 | tf_op jit(solution)/shard_map/gather_rows/pallas_call | solution.py:211
  166.6 13.3 %joined_heads.1 = (bf16[256,2048]{1,0:T(8,128)(2,1)}, bf16[256,2048]{1,0:T(8,128)(2,1)}) custom-call(bf16[256,2176]{1,0:T(8,128)(2,1)} %pad_maximum_fusion.1.x_ref, bf16[4096,2176]{1,0:T(8,128)(2,1)} %get-tuple-element.46.w_ref, f32[256,128]{1,0:T(8,128)} %pad_maximum_fusion.6.cos_ref.refs_14_, f32[256,128]{1,0:T(8,128)} %pad_maximum_fusion.7.sin_ref.refs_15_), custom_call_target="tpu_custom_call" | custom-call | flops 4563402752 | bytes 20054016 | tf_op jit(solution)/shard_map/joined_heads/pallas_call | solution.py:632
  179.9 46.7 %context.1.refs_1_.refs_2_.refs_3_.refs_4_.refs_6_.refs_7_.refs_8_.refs_9_.refs_5_.refs_10_ = bf16[4,256,2048]{2,1,0:T(8,128)(2,1)} custom-call(bf16[256,2048]{1,0:T(8,128)(2,1)} %get-tuple-element.48.pair_ref.refs_5_.refs_10_.refs_6_.refs_11_), custom_call_target="tpu_custom_call" | custom-call | bytes 33554432 | tf_op jit(solution)/shard_map/context/pallas_call | solution.py:490
  226.7 2.3 collective-permute-start.1
  228.9 3.4 collective-permute-start.2
  234.0 16.6 %attend.1 = bf16[256,2048]{1,0:T(8,128)(2,1)} custom-call(bf16[256,2048]{1,0:T(8,128)(2,1)} %get-tuple-element.47.refs_0_, bf16[4,256,2048]{2,1,0:T(8,128)(2,1)} %context.1.refs_1_.refs_2_.refs_3_.refs_4_.refs_6_.refs_7_.refs_8_.refs_9_.refs_5_.refs_10_, ...), custom_call_target="tpu_custom_call" | custom-call | flops 2684354560 | bytes 7340032 | tf_op jit(solution)/shard_map/attend/pallas_call | solution.py:708
  250.6 2.4 broadcast_multiply_fusion
  253.0 5.6 multiply_reduce_fusion.1
  259.9 94.1 %gather_rows.3 = (bf16[2048,2048]{1,0:T(8,128)(2,1)}, bf16[2048,2048]{1,0:T(8,128)(2,1)}) custom-call(bf16[256,2048]{1,0:T(8,128)(2,1)} %multiply_convert_fusion.refs_0_, bf16[256,2048]{1,0:T(8,128)(2,1)} %refs_1_.1), custom_call_target="tpu_custom_call" | custom-call | bytes 134217728 | tf_op jit(solution)/shard_map/gather_rows/pallas_call | solution.py:211
  354.0 2.1 collective-permute-start.3
  356.1 6.2 fusion.6
  363.4 4.2 fusion.9.refs_4_
  367.6 25.9 %collective-permute-done.3.refs_12_ = bf16[384,2176]{1,0:T(8,128)(2,1)} collective-permute-done((bf16[384,2176]{1,0:T(8,128)(2,1)}, bf16[384,2176]{1,0:T(8,128)(2,1)}, u32[]{:S(2)}, u32[]{:S(2)}) %collective-permute-start.3) | collective-permute-done | bytes 1671200 | tf_op jit(solution)/shard_map/ppermute | solution.py:29
  393.5 76.1 %feed.1 = (bf16[2048,2176]{1,0:T(8,128)(2,1)}, bf16[2048,2304]{1,0:T(8,128)(2,1)}, f32[1024,384]{1,0:T(8,128)}) custom-call(bf16[2048,2048]{1,0:T(8,128)(2,1)} %get-tuple-element.51.refs_0_, bf16[2048,2048]{1,0:T(8,128)(2,1)} %get-tuple-element.52.refs_1_, bf16[2048,128]{1,0:T(8,128)(2,1)} %get-tuple-element.80.refs_2_, ...), custom_call_target="tpu_custom_call" | custom-call | flops 54760833024 | bytes 72089600 | tf_op jit(solution)/shard_map/feed/pallas_call | solution.py:881
  469.6 51.6 %reduce_rows.2 = f32[256,2304]{1,0:T(8,128)} custom-call(bf16[2048,2304]{1,0:T(8,128)(2,1)} %get-tuple-element.56.refs_0_), custom_call_target="tpu_custom_call" | custom-call | bytes 150994944 | tf_op jit(solution)/shard_map/reduce_rows/pallas_call | solution.py:346
  521.2 2.8 multiply_reduce_fusion
  524.5 6.9 fusion.32
  532.8 2.4 fusion.5.refs_1_
  535.2 27.0 %attend_back.1 = (bf16[256,2048]{1,0:T(8,128)(2,1)}, f32[2,256,1024]{2,1,0:T(8,128)}, bf16[4,2,256,1024]{3,2,1,0:T(8,128)(2,1)}) custom-call(bf16[256,2048]{1,0:T(8,128)(2,1)} %get-tuple-element.47.refs_0_, bf16[256,2048]{1,0:T(8,128)(2,1)} %fusion.5.refs_1_, ...), custom_call_target="tpu_custom_call" | custom-call | flops 6710886400 | bytes 24117248 | tf_op jit(solution)/shard_map/attend_back/pallas_call | solution.py:781
  562.2 98.5 %context_back.1 = (f32[2,256,1024]{2,1,0:T(8,128)}, f32[256,2176]{1,0:T(8,128)}) custom-call(bf16[4,2,256,1024]{3,2,1,0:T(8,128)(2,1)} %get-tuple-element.57.away, f32[2,256,1024]{2,1,0:T(8,128)} %get-tuple-element.58.own, bf16[2048,2176]{1,0:T(8,128)(2,1)} %get-tuple-element.59.mixed), custom_call_target="tpu_custom_call" | custom-call | bytes 33554432 | tf_op jit(solution)/shard_map/context_back/pallas_call | solution.py:581
  665.0 2.3 fusion.51.refs_0_
  670.6 2.1 fusion.28.refs_6_
  672.7 9.9 %fusion.29 = f32[256,2176]{1,0:T(8,128)S(1)} fusion(bf16[4096,2176]{1,0:T(8,128)(2,1)} %get-tuple-element.46.w_ref, bf16[256,1024]{1,0:T(8,128)(2,1)S(1)} %fusion.30, bf16[256,1024]{1,0:T(8,128)(2,1)S(1)} %fusion.22, bf16[256,2048]{1,0:T(8,128)(2,1)S(1)} %copy-done.62), kind=kOutput, calls=%fused_computation.54 | convolution fusion | flops 4569694208 | bytes 22151168 | tf_op jit(solution)/shard_map/dot_general | solution.py:39
  684.1 2.9 fusion.11
  687.0 2.4 fusion.7.refs_4_
  689.5 3.2 add_convert_fusion
  692.7 1.5 fusion.58
  695.1 1.5 convolution_multiply_fusion.3.refs_1_
  697.9 46.5 %reduce_rows.3 = (f32[64,128]{1,0:T(8,128)}, f32[64,128]{1,0:T(8,128)}, f32[64,128]{1,0:T(8,128)}, f32[64,128]{1,0:T(8,128)}, f32[64,128]{1,0:T(8,128)}, /*index...) custom-call(f32[2048,128]{1,0:T(8,128)} %fusion.51.refs_0_, f32[2048,128]{1,0:T(8,128)} %convolution_multiply_fusion.3.refs_1_, ...), custom_call_target="tpu_custom_call" | custom-call | bytes 79691776 | tf_op jit(solution)/shard_map/reduce_rows/pallas_call | solution.py:346
  744.4 1.8 fusion.64
  746.3 3.4 fusion.14
  (191 shorter events, 39.2 us)
Async XLA Ops:
  0.7 8.3 %copy-start.51 = (s32[15]{0:T(128)}, s32[15]{0:T(128)S(1)}, u32[]{:S(2)}) copy-start(s32[15]{0:T(128)S(1)} %iota_add_fusion.2) | copy-start | bytes 184
  2.5 6.5 copy-start.53
  3.2 5.8 copy-start.55
  5.7 4.7 copy-start.58
  5.7 5.1 copy-start.20
  5.7 5.1 copy-start.31
  5.7 6.0 copy-start.42
  5.7 6.0 copy-start.43
  5.7 6.0 copy-start.44
  5.7 6.0 copy-start.45
  5.8 6.6 copy-start.21
  5.8 6.6 copy-start.40
  9.0 4.1 copy-start.46
  13.4 149.2 %copy-start.7 = (bf16[256,2048]{1,0:T(8,128)(2,1)}, bf16[256,2048]{1,0:T(8,128)(2,1)S(1)}, u32[]{:S(2)}) copy-start(bf16[256,2048]{1,0:T(8,128)(2,1)S(1)} %fusion.10) | copy-start | bytes 3145732
  179.9 53.3 %copy-start.52 = (s32[15]{0:T(128)S(1)}, s32[15]{0:T(128)}, u32[]{:S(2)}) copy-start(s32[15]{0:T(128)} %copy-done.51) | copy-start | bytes 184
  179.9 53.3 %copy-start.54 = (s32[15,1]{0,1:T(1,128)S(1)}, s32[15,1]{0,1:T(1,128)}, u32[]{:S(2)}) copy-start(s32[15,1]{0,1:T(1,128)} %copy-done.53) | copy-start | bytes 184
  179.9 53.3 %copy-start.56 = (s32[15]{0:T(128)S(1)}, s32[15]{0:T(128)}, u32[]{:S(2)}) copy-start(s32[15]{0:T(128)} %copy-done.55) | copy-start | bytes 184
  226.7 127.3 %collective-permute-start.1 = (bf16[384,2176]{1,0:T(8,128)(2,1)}, bf16[384,2176]{1,0:T(8,128)(2,1)}, u32[]{:S(2)}, u32[]{:S(2)}) collective-permute-start(bf16[384,2176]{1,0:T(8,128)(2,1)} %get-tuple-element.55.refs_9_), channel_id=1, source_target_pairs={{0,16},{1,17},{2,18},{3,19},{4,20},{5,21},{6,22},{7,23},{8,24},{9,... | collective-permute-start | bytes 5013512 | tf_op jit(solution)/shard_map/ppermute | solution.py:29
  228.9 138.6 %collective-permute-start.2 = (bf16[384,2176]{1,0:T(8,128)(2,1)}, bf16[384,2176]{1,0:T(8,128)(2,1)}, u32[]{:S(2)}, u32[]{:S(2)}) collective-permute-start(bf16[384,2176]{1,0:T(8,128)(2,1)} %get-tuple-element.55.refs_9_), channel_id=1, source_target_pairs={{0,8},{1,9},{2,10},{3,11},{4,12},{5,13},{6,14},{7,15},{8,0},{9,1},... | collective-permute-start | bytes 5013512 | tf_op jit(solution)/shard_map/ppermute | solution.py:29
  232.4 135.2 %collective-permute-start = (bf16[384,2176]{1,0:T(8,128)(2,1)}, bf16[384,2176]{1,0:T(8,128)(2,1)}, u32[]{:S(2)}, u32[]{:S(2)}) collective-permute-start(bf16[384,2176]{1,0:T(8,128)(2,1)} %get-tuple-element.53.refs_6_), channel_id=1, source_target_pairs={{0,8},{1,9},{2,10},{3,11},{4,12},{5,13},{6,14},{7,15},{8,0},{9,1},... | collective-permute-start | bytes 5013512 | tf_op jit(solution)/shard_map/ppermute | solution.py:29
  234.0 19.0 %copy-start.50 = (bf16[2048]{0:T(1024)(128)(2,1)S(1)}, bf16[2048]{0:T(1024)(128)(2,1)}, u32[]{:S(2)}) copy-start(bf16[2048]{0:T(1024)(128)(2,1)} %param.23) | copy-start | bytes 12292
  354.0 39.5 %collective-permute-start.3 = (bf16[384,2176]{1,0:T(8,128)(2,1)}, bf16[384,2176]{1,0:T(8,128)(2,1)}, u32[]{:S(2)}, u32[]{:S(2)}) collective-permute-start(bf16[384,2176]{1,0:T(8,128)(2,1)} %collective-permute-done.1.refs_10_), channel_id=1, source_target_pairs={{0,8},{1,9},{2,10},{3,11},{4,12},{5,13},{6,14},{7,15},{8,0},{9,1},... | collective-permute-start | bytes 5013512 | tf_op jit(solution)/shard_map/ppermute | solution.py:29
  356.1 7.3 copy-start.61
  524.5 6.9 copy-start
  672.7 9.9 %copy-start.8 = (bf16[256,2048]{1,0:T(8,128)(2,1)S(1)}, bf16[256,2048]{1,0:T(8,128)(2,1)}, u32[]{:S(2)}) copy-start(bf16[256,2048]{1,0:T(8,128)(2,1)} %copy-done.7) | copy-start | bytes 3145732
  697.9 48.3 %copy-start.6 = (bf16[256,2048]{1,0:T(8,128)(2,1)S(1)}, bf16[256,2048]{1,0:T(8,128)(2,1)}, u32[]{:S(2)}) copy-start(bf16[256,2048]{1,0:T(8,128)(2,1)} %param.21) | copy-start | bytes 3145732
  746.2 4.1 copy-start.30
  746.2 4.8 copy-start.38
  746.2 5.4 copy-start.37
  746.2 6.0 copy-start.36
  746.3 6.6 copy-start.35
  746.3 7.2 copy-start.34
  (35 other events, 84.4 us)

commit v3 on v2

--- a/solution.py
+++ b/solution.py
@@ -116,12 +116,13 @@
     return held
 
 
-def gather_kernel(parts, slots, bits_moved, count, *refs):
-    moved = len(bits_moved)
-    ins, more = refs[:count], refs[count : count + (moved > 0)]
-    outs = refs[count + len(more) : 2 * count + len(more)]
-    away = refs[2 * count + len(more) : 2 * count + len(more) + moved]
-    send, recv, local = refs[2 * count + len(more) + moved :]
+def gather_kernel(parts, slots, bits_moved, shared, count, *refs):
+    extra = len(shared) or (len(bits_moved) > 0)
+    added = 1 if shared else len(bits_moved)
+    ins, more = refs[:count], refs[count : count + extra]
+    outs = refs[count + extra : 2 * count + extra]
+    away = refs[2 * count + extra : 2 * count + extra + added]
+    send, recv, local, *stage = refs[2 * count + extra + added :]
     me = lax.axis_index(AXIS)
     enter(me, sorted({bit for part in parts for bit in part[3]}))
 
@@ -163,10 +164,46 @@
             sends.append(first)
             for place, mask in enumerate(span(order[:level])):
                 arrivals.append(((level, place, p), p, mask + bit, bit, order[level + 1 :]))
-    kept = []
+    kept, exchanged = [], []
+
+    def keep(at, source, target):
+        inward = pltpu.make_async_copy(source, stage[at], local.at[0, at])
+        inward.start()
+        kept.append((inward, pltpu.make_async_copy(stage[at], target, local.at[1, at])))
+
+    def there(mask, first, rows):
+        height = away[0].shape[0] // slots[-1]
+        start = pl.multiple_of(peer_of(me, mask) % slots[-1] * height + first, 8)
+        return away[0].at[pl.ds(start, rows)]
+
+    def hand(at, source, target, bit):
+        return pltpu.make_async_remote_copy(
+            src_ref=source,
+            dst_ref=target,
+            send_sem=send.at[len(parts), at],
+            recv_sem=recv.at[len(parts), at],
+            device_id=(partner_of(me, bit),),
+            device_id_type=MESH,
+        )
+
+    crossed = []
+    for i, (mask, crossing) in enumerate(shared):
+        if crossing is not None:
+            first, rows, bit = crossing
+            crossed.append(
+                hand(8 + i, more[i].at[pl.ds(first, rows)], there(mask, first, rows), bit)
+            )
+            crossed[-1].start()
+    for i, (mask, _) in enumerate(shared):
+        rows = more[i].shape[0]
+        exchanged.append(hand(i, more[i], there(mask, 0, rows), 1))
+        exchanged[-1].start()
+        keep(len(parts) + i, more[i], there(mask, 0, rows))
     for p in range(len(parts)):
-        kept.append(pltpu.make_async_copy(own(p), block(p, 0), local.at[p]))
-        kept[-1].start()
+        keep(p, own(p), block(p, 0))
+    for inward, outward in kept:
+        inward.wait()
+        outward.start()
     arrivals.sort(key=lambda entry: entry[0])
     moves = [
         pltpu.make_async_remote_copy(
@@ -179,7 +216,7 @@
         )
         for i, bit in enumerate(bits_moved)
     ]
-    waiting = True
+    waiting = len(moves) > 0
     for (level, _, _), p, mask, bit, later in arrivals:
         if waiting and level == 1:
             waiting = False
@@ -190,34 +227,50 @@
             onward = copy(p, mask, following)
             onward.start()
             sends.append(onward)
-    for move in moves:
+    crossings = [entry for entry in enumerate(shared) if entry[1][1] is not None]
+    for (i, (mask, (first, rows, bit))), sent in zip(crossings, crossed, strict=True):
+        came = there(mask + bit, first, rows)
+        sent.wait_recv()
+        exchanged.append(hand(16 + i, came, came, 1))
+        exchanged[-1].start()
+    for move in moves + exchanged:
         move.wait()
+    for sent in crossed:
+        sent.wait_send()
     for sent in sends:
         sent.wait_send()
-    for copied in kept:
-        copied.wait()
-
-
-def gather_rows(arrays, parts, collective_id, slots, moved=None, bits_moved=()):
+    for _, outward in kept:
+        outward.wait()
+
+
+def gather_rows(arrays, parts, collective_id, slots, moved=None, bits_moved=(), shared=()):
     count, devices = len(arrays), lax.axis_size(AXIS)
     shapes = [
         jax.ShapeDtypeStruct((times * a.shape[0], a.shape[1]), a.dtype)
-        for a, times in zip(arrays, slots, strict=True)
+        for a, times in zip(arrays, slots)
     ]
     sent = 2 * sum(math.prod(shape.shape) for shape in shapes)
     if moved is not None:
         arrays = list(arrays) + [moved]
         shapes += [jax.ShapeDtypeStruct(moved.shape, moved.dtype)] * len(bits_moved)
+    if shared:
+        whole = shared[0][1]
+        arrays = list(arrays) + [value for _, value, _ in shared]
+        shape = (slots[-1] * whole.shape[0], whole.shape[1])
+        shapes.append(jax.ShapeDtypeStruct(shape, whole.dtype))
+    places = tuple((mask, crossing) for mask, _, crossing in shared)
     return pl.pallas_call(
-        functools.partial(gather_kernel, parts, slots, bits_moved, count),
+        functools.partial(gather_kernel, parts, slots, bits_moved, places, count),
         out_shape=shapes,
         in_specs=[pl.BlockSpec(memory_space=pl.ANY)] * len(arrays),
         out_specs=[pl.BlockSpec(memory_space=pl.ANY)] * len(shapes),
         scratch_shapes=[
             pltpu.SemaphoreType.DMA((len(parts) + 1, devices)),
             pltpu.SemaphoreType.DMA((len(parts) + 1, devices)),
-            pltpu.SemaphoreType.DMA((len(parts),)),
-        ],
+            pltpu.SemaphoreType.DMA((2, len(parts) + len(shared))),
+        ]
+        + [pltpu.VMEM((part[2], arrays[part[0]].shape[1]), arrays[part[0]].dtype) for part in parts]
+        + [pltpu.VMEM(value.shape, value.dtype) for _, value, _ in shared],
         compiler_params=pltpu.CompilerParams(
             collective_id=collective_id, has_side_effects=True
         ),
@@ -231,13 +284,6 @@
         self.me, self.parts, self.ins, self.outs = me, parts, ins, outs
         self.totals, self.outgoing, self.incoming = totals, outgoing, incoming
         self.send, self.recv = send, recv
-        self.live = [sorted(span(part[4])) for part in parts]
-        self.slots = [{mask: at for at, mask in enumerate(masks)} for masks in self.live]
-        self.held = []
-        for part, masks in zip(parts, self.live, strict=True):
-            sent = part[4][0] if ins[part[5][0]].dtype == jnp.bfloat16 else 0
-            kept = [mask for mask in masks if not mask & sent]
-            self.held.append({mask: at for at, mask in enumerate(kept)})
         self.pending = [[] for _ in parts]
         self.every = []
         self.levels = max(len(part[4]) for part in parts)
@@ -246,33 +292,42 @@
         _, block, first, rows, _, places = self.parts[p]
         a, place = places
         if isinstance(place, int):
-            start = pl.multiple_of(peer_of(self.me, mask) % place * block + first, 8)
+            at = peer_of(self.me, mask) % place
         else:
-            start = place[mask] * block + first
-        return self.ins[a].at[pl.ds(start, rows)]
+            at = dict(place)[mask]
+        return self.ins[a].at[pl.ds(pl.multiple_of(at * block + first, 8), rows)]
+
+    def masks(self, p):
+        return span(self.parts[p][4][:0:-1])
 
     def launch(self, p, level):
-        bit = self.parts[p][4][level]
-        leaving = [mask for mask in self.live[p] if mask & bit]
-        self.live[p] = [mask for mask in self.live[p] if not mask & bit]
-        for mask in leaving:
-            at = self.slots[p][mask]
-            source = self.given(p, mask) if level == 0 else None
-            if source is None or source.dtype != jnp.bfloat16:
-                place = self.held[p][mask]
-                value = self.totals[p][place] if level else source[...]
-                self.outgoing[p][place] = value.astype(jnp.bfloat16)
-                source = self.outgoing[p].at[place]
+        order = self.parts[p][4]
+        bit, half = order[level], 1 << (len(order) - 1 - level)
+        copies = []
+        if level:
+            self.outgoing[p][half : 2 * half] = self.totals[p][half : 2 * half].astype(jnp.bfloat16)
+            copies.append((self.outgoing[p].at[pl.ds(half, half)], half, half))
+        else:
+            for at, mask in enumerate(self.masks(p)):
+                source = self.given(p, mask + bit)
+                if source.dtype == jnp.bfloat16:
+                    copies.append((source, half + at, None))
+                else:
+                    self.outgoing[p][half + at] = source[...].astype(jnp.bfloat16)
+            if not copies:
+                copies.append((self.outgoing[p].at[pl.ds(half, half)], half, half))
+        for source, at, number in copies:
+            there = at if number is None else pl.ds(at, number)
             copy = pltpu.make_async_remote_copy(
                 src_ref=source,
-                dst_ref=self.incoming[p].at[at],
+                dst_ref=self.incoming[p].at[there],
                 send_sem=self.send.at[p, at],
                 recv_sem=self.recv.at[p, at],
                 device_id=(partner_of(self.me, bit),),
                 device_id_type=MESH,
             )
             copy.start()
-            self.pending[p].append((mask, bit, copy))
+            self.pending[p].append(copy)
             self.every.append(copy)
 
     def begin(self):
@@ -281,19 +336,21 @@
 
     def advance(self, level):
         for p in range(len(self.parts)):
-            if level >= len(self.parts[p][4]):
+            order = self.parts[p][4]
+            if level >= len(order):
                 continue
+            half, wide = 1 << (len(order) - 1 - level), jnp.float32
             arrived, self.pending[p] = self.pending[p], []
-            for mask, bit, copy in arrived:
+            for copy in arrived:
                 copy.wait_recv()
-                onto, wide = self.held[p][mask - bit], jnp.float32
-                if level:
-                    held = self.totals[p][onto]
-                else:
-                    held = self.given(p, mask - bit)[...].astype(wide)
-                came = self.incoming[p][self.slots[p][mask]].astype(wide)
-                self.totals[p][onto] = held + came
-            if level + 1 < len(self.parts[p][4]):
+            if level:
+                came = self.incoming[p][half : 2 * half].astype(wide)
+                self.totals[p][:half] = self.totals[p][:half] + came
+            else:
+                for at, mask in enumerate(self.masks(p)):
+                    came = self.incoming[p][half + at].astype(wide)
+                    self.totals[p][at] = self.given(p, mask)[...].astype(wide) + came
+            if level + 1 < len(order):
                 self.launch(p, level + 1)
 
     def finish(self):
@@ -326,16 +383,15 @@
         block = values[source].shape[0] // members
         columns = values[source].shape[1]
         shapes.append(jax.ShapeDtypeStruct((block, columns), jnp.float32))
-        pieces = len(orders) if block % (16 * len(orders)) == 0 else 1
+        pieces = len(orders) if block % (64 * len(orders)) == 0 else 1
         rows = block // pieces
         for i in range(pieces):
-            parts.append((a, block, i * rows, rows, orders[i], places))
-            held = members // 2 if values[source].dtype == jnp.bfloat16 else members
-            scratch.append(((held, rows, columns), (members, rows, columns)))
-    most = max(shape[0] for _, shape in scratch)
-    buffers = [pltpu.VMEM(shape, jnp.float32) for shape, _ in scratch]
-    buffers += [pltpu.VMEM(shape, jnp.bfloat16) for shape, _ in scratch]
-    buffers += [pltpu.VMEM(shape, jnp.bfloat16) for _, shape in scratch]
+            parts.append((a, block, i * rows, rows, orders[(a + i) % len(orders)], places))
+            out = members // 2 if values[source].dtype == jnp.bfloat16 else members
+            scratch.append([(n, rows, columns) for n in (members // 2, out, members)])
+    most = max(s[2][0] for s in scratch)
+    kinds = (jnp.float32, jnp.bfloat16, jnp.bfloat16)
+    buffers = [pltpu.VMEM(s[i], kinds[i]) for i in range(3) for s in scratch]
     buffers += [pltpu.SemaphoreType.DMA((len(parts), most))] * 2
     return tuple(parts), shapes, buffers
 
@@ -508,95 +564,105 @@
     )(pair)
 
 
-def context_back_kernel(devices, parts, away, own, mixed, *refs):
-    out_ref, sum_ref, beside, going, coming, send, recv = refs[:7]
+def context_back_kernel(devices, parts, counts, away, own, *refs):
+    inputs, outputs = counts
+    values, out_ref = refs[:inputs], refs[inputs]
+    sums = refs[inputs + 1 : inputs + 1 + outputs]
+    refs = refs[inputs + 1 + outputs :]
+    beside, going, coming, send, recv = refs[:5]
     number = len(parts)
-    buffers = (refs[7 + i * number : 7 + (i + 1) * number] for i in range(3))
+    buffers = (refs[5 + i * number : 5 + (i + 1) * number] for i in range(3))
     me = lax.axis_index(AXIS)
     bits = sorted({bit for part in parts for bit in part[4]})
     greet(me, devices, (2, 4), bits)
-    halving = Halving(me, parts, [mixed], [sum_ref], *buffers, *refs[7 + 3 * number :])
+    halving = Halving(me, parts, values, sums, *buffers, *refs[5 + 3 * number :])
     even = me % 2 == 0
     partner = partner_of(me, 1)
     wide, narrow = jnp.float32, jnp.bfloat16
 
-    def copy(i, h, source, target, there):
+    def copy(i, c, source, target, there):
         return pltpu.make_async_remote_copy(
             src_ref=source,
             dst_ref=target,
-            send_sem=send.at[h, i],
-            recv_sem=recv.at[h, i],
+            send_sem=send.at[c, i],
+            recv_sem=recv.at[c, i],
             device_id=(there,),
             device_id_type=MESH,
         )
 
+    pieces = own.shape[1] // 2
+    chunks = [(h, pl.ds(r * pieces, pieces), 2 * h + r) for h in range(2) for r in range(2)]
     shared = []
-    for h in range(2):
+    for h, rows, c in chunks:
         for i, slot in enumerate((3, 1)):
-            shared.append(copy(i, h, away.at[slot, h], beside.at[i, h], partner))
+            shared.append(copy(i, c, away.at[slot, h, rows], beside.at[i, h, rows], partner))
             shared[-1].start()
-    halving.begin()
     out_ref[...] = own[...]
     far = []
-    for h in range(2):
+    for h, rows, c in chunks:
         for i in range(2):
-            shared[2 * h + i].wait_recv()
-        one, three = beside[0, h].astype(wide), beside[1, h].astype(wide)
-        going[0, h] = (away[2, h].astype(wide) + jnp.where(even, three, one)).astype(narrow)
-        going[1, h] = (away[0, h].astype(wide) + jnp.where(even, 0.0, three)).astype(narrow)
-        out_ref[h] += jnp.where(even, one, 0.0)
+            shared[2 * c + i].wait_recv()
+        one, three = beside[0, h, rows].astype(wide), beside[1, h, rows].astype(wide)
+        first = away[2, h, rows].astype(wide) + jnp.where(even, three, one)
+        second = away[0, h, rows].astype(wide) + jnp.where(even, 0.0, three)
+        going[0, h, rows] = first.astype(narrow)
+        going[1, h, rows] = second.astype(narrow)
+        out_ref[h, rows] += jnp.where(even, one, 0.0)
         for i, step in enumerate((2, 4)):
             move = copy(
-                2 + i, h, going.at[i, h], coming.at[i, h], (me - step + devices) % devices
+                2 + i, c, going.at[i, h, rows], coming.at[i, h, rows],
+                (me - step + devices) % devices,
             )
-            far.append((i, h, step, move))
+            far.append((i, h, rows, step, move))
 
             @pl.when(me >= step)
             def _(move=move):
                 move.start()
 
+    halving.begin()
     for level in range(halving.levels):
         halving.advance(level)
-    for i, h, step, move in far:
+    for i, h, rows, step, move in far:
 
         @pl.when(me + step < devices)
-        def _(i=i, h=h, move=move):
+        def _(i=i, h=h, rows=rows, move=move):
             move.wait_recv()
-            out_ref[h] += coming[i, h].astype(wide)
+            out_ref[h, rows] += coming[i, h, rows].astype(wide)
 
     halving.finish()
     for move in shared:
         move.wait_send()
-    for i, h, step, move in far:
+    for _, _, _, step, move in far:
 
         @pl.when(me >= step)
         def _(move=move):
             move.wait_send()
 
 
-def context_back(away, own, mixed, sums, collective_id):
+def context_back(away, own, values, sums, collective_id):
     devices = lax.axis_size(AXIS)
     half = (2,) + own.shape
-    parts, shapes, buffers = reduce_plan([mixed], sums)
+    parts, shapes, buffers = reduce_plan(values, sums)
+    in_vmem = pl.BlockSpec(memory_space=pltpu.VMEM)
     return pl.pallas_call(
-        functools.partial(context_back_kernel, devices, parts),
+        functools.partial(context_back_kernel, devices, parts, (len(values), len(sums))),
         out_shape=[jax.ShapeDtypeStruct(own.shape, jnp.float32)] + shapes,
-        in_specs=[pl.BlockSpec(memory_space=pltpu.VMEM)] * 3,
-        out_specs=[pl.BlockSpec(memory_space=pltpu.VMEM)] * 2,
+        in_specs=[in_vmem] * (2 + len(values)),
+        out_specs=[in_vmem] * (1 + len(sums)),
         scratch_shapes=[
             pltpu.VMEM(half, jnp.bfloat16),
             pltpu.VMEM(half, jnp.bfloat16),
             pltpu.VMEM(half, jnp.bfloat16),
-            pltpu.SemaphoreType.DMA((2, 4)),
-            pltpu.SemaphoreType.DMA((2, 4)),
+            pltpu.SemaphoreType.DMA((4, 4)),
+            pltpu.SemaphoreType.DMA((4, 4)),
         ]
         + buffers,
         compiler_params=pltpu.CompilerParams(
-            collective_id=collective_id, has_side_effects=True, vmem_limit_bytes=VMEM_LIMIT
+            collective_id=collective_id, has_side_effects=True, vmem_limit_bytes=67043328
         ),
         cost_estimate=pl.CostEstimate(flops=0, bytes_accessed=64 * own.size, transcendentals=0),
         name="context_back",
-    )(away, own, mixed)
+    )(away, own, *values)
 
 
 def joined_kernel(turned, x_ref, w_ref, cos_ref, sin_ref, query_ref, pair_ref):
@@ -810,10 +876,11 @@
     )(query, grad, *pairs, *pairs, query_seq, key_seq, cosine, sine)
 
 
-def feed_kernel(pieces, joint, *refs):
-    x_ref, c_ref, gl_ref, ul_ref, db_ref = refs[:5]
-    w_refs = refs[5 : 5 + pieces]
-    mixed_ref, back_ref, grads_ref, weights, mixed_acc, back_acc, arrival = refs[5 + pieces :]
+def feed_kernel(pieces, joint, carried, *refs):
+    x_ref, c_ref, gl_ref, ul_ref = refs[:4]
+    w_refs, begun = refs[4 : 4 + pieces], refs[4 + pieces : 4 + pieces + carried]
+    outs = refs[4 + pieces + carried :]
+    mixed_ref, back_ref, grads_ref, weights, mixed_acc, back_acc, arrival = outs
     step = pl.program_id(0)
     width, columns = x_ref.shape[1], gl_ref.shape[1]
     rounds, hid = weights.shape[0], weights.shape[1] // 3
@@ -837,8 +904,8 @@
                 copy.start()
         grads_ref[...] = jnp.zeros_like(grads_ref)
 
-    mixed_acc[...] = jnp.zeros_like(mixed_acc)
-    back_acc[...] = jnp.zeros_like(back_acc)
+    for acc, start in zip((mixed_acc, back_acc), begun or (None, None), strict=True):
+        acc[...] = jnp.zeros_like(acc) if start is None else start[...].astype(jnp.float32)
 
     @pl.loop(0, rounds)
     def _(i):
@@ -849,10 +916,10 @@
                     copy.wait()
 
         wg, wu, wd = (weights.at[i, pl.ds(j * hid, hid)] for j in range(3))
-        x, gl, ul, db = x_ref[...], gl_ref[...], ul_ref[...], db_ref[...]
+        x, gl, ul = x_ref[...], gl_ref[...], ul_ref[...]
         gate = project(x, wg[:, main]) + project(gl, wg[:, side])
         up = project(x, wu[:, main]) + project(ul, wu[:, side])
-        back = project(c_ref[...], wd[:, main]) + project(db, wd[:, side])
+        back = project(c_ref[...], wd[...])
         sigma = 1.0 / (1.0 + jnp.exp(-gate))
         active = gate * sigma
         hidden = (active * up).astype(jnp.bfloat16)
@@ -865,13 +932,13 @@
         at = pl.ds(pl.multiple_of(i * hid, hid), hid)
         grads_ref[at, :columns] += contract_rows(gate_back, gl)
         grads_ref[at, columns : 2 * columns] += contract_rows(up_back, ul)
-        grads_ref[at, 2 * columns :] += contract_rows(hidden, db)
+        grads_ref[at, 2 * columns :] += contract_rows(hidden, c_ref[:, side])
 
     mixed_ref[...] = mixed_acc[...].astype(jnp.bfloat16)
     back_ref[...] = back_acc[...].astype(jnp.bfloat16)
 
 
-def feed(x, cot, gate_low, up_low, down_back, weights):
+def feed(x, cot, gate_low, up_low, weights, begun=()):
     (rows, width), columns = x.shape, gate_low.shape[1]
     pieces, height = len(weights), weights[0].shape[0] // 3
     hidden, tile = pieces * height, 256
@@ -879,16 +946,16 @@
     row = lambda wide: pl.BlockSpec((tile, wide), lambda i: (i, 0))
     size = sum(w.size for w in weights)
     return pl.pallas_call(
-        functools.partial(feed_kernel, pieces, hid // height),
+        functools.partial(feed_kernel, pieces, hid // height, len(begun)),
         out_shape=[
             jax.ShapeDtypeStruct((rows, width + columns), jnp.bfloat16),
             jax.ShapeDtypeStruct((rows, width + 2 * columns), jnp.bfloat16),
             jax.ShapeDtypeStruct((hidden, 3 * columns), jnp.float32),
         ],
         grid=(rows // tile,),
-        in_specs=[row(width)] * 2
-        + [row(columns)] * 3
-        + [pl.BlockSpec(memory_space=pl.ANY)] * pieces,
+        in_specs=[row(width), row(width + columns), row(columns), row(columns)]
+        + [pl.BlockSpec(memory_space=pl.ANY)] * pieces
+        + [row(value.shape[1]) for value in begun],
         out_specs=[
             row(width + columns),
             row(width + 2 * columns),
@@ -907,7 +974,7 @@
             transcendentals=rows * hidden,
         ),
         name="feed",
-    )(x, cot, gate_low, up_low, down_back, *weights)
+    )(x, cot, gate_low, up_low, *weights, *begun)
 
 
 def layer(
@@ -946,16 +1013,6 @@
 
     joined_shard = jnp.concatenate([joined_projection, joined_adapter_output], axis=1)
     output_shard = jnp.concatenate([output_projection, output_adapter_output], axis=1)
-    entry_shard = jnp.concatenate(
-        [
-            output_adapter_input,
-            gate_adapter_input,
-            upward_adapter_input,
-            down_adapter_output,
-            joined_adapter_input,
-        ],
-        axis=1,
-    )
     half_shard = gate_weight.shape[0] // 2
 
     def feed_half(at):
@@ -970,25 +1027,38 @@
         )
 
     feed_first, feed_second = feed_half(0), feed_half(1)
+    entries = [
+        joined_adapter_input,
+        output_adapter_input,
+        gate_adapter_input,
+        upward_adapter_input,
+        down_adapter_output,
+    ]
     rows, output_rows, entry_rows = (
-        value.shape[0] for value in (joined_shard, output_shard, entry_shard)
+        value.shape[0] for value in (joined_shard, output_shard, entries[0])
     )
     head = tuple(bits[:-3:-1])
     up_order, down_order = tuple(middle) + (core,), tuple(middle[::-1]) + (core,)
-    full_joined, full_entry, full_output, *first_moved = gather_rows(
-        [joined_shard, entry_shard, output_shard],
+    gathered = gather_rows(
+        [joined_shard, entries[0], output_shard] + entries[1:],
         (
             (0, 0, rows // 2, head + up_order),
             (0, rows // 2, rows // 2, head + down_order),
             (1, 0, entry_rows, head + up_order),
             (2, 0, output_rows // 2, head + down_order),
             (2, output_rows // 2, output_rows // 2, head + up_order),
+            (3, 0, entry_rows, head + down_order),
+            (4, 0, entry_rows, head + up_order),
+            (5, 0, entry_rows, head + down_order),
+            (6, 0, entry_rows, head + up_order),
         ),
         1,
-        (devices,) * 3,
+        (devices,) * 7,
         feed_first,
         tuple(distant),
     )
+    full_joined, full_f_entry, full_output, full_o_entry = gathered[:4]
+    full_g_entry, full_u_entry, full_d_exit, *first_moved = gathered[4:]
 
     def spread(piece, moved):
         pieces = [piece]
@@ -1000,10 +1070,6 @@
 
     full_joined, *first_moved = lax.optimization_barrier((full_joined, *first_moved))
     first_pieces = spread(feed_first, first_moved)
-    full_f_entry = full_entry[:, 4 * columns :]
-    full_o_entry = full_entry[:, :columns]
-    full_gu_entry = full_entry[:, columns : 3 * columns]
-    full_d_exit = full_entry[:, 3 * columns : 4 * columns]
 
     members = 1 << 3
     place = me % members
@@ -1023,6 +1089,11 @@
     gain_one = attention_gain.astype(jnp.float32)
     gain_two = feedforward_gain.astype(jnp.float32)
 
+    down_back = masked(ADAPTER_SCALE * product(cotangent, full_d_exit), select)
+    wide_cot = jnp.concatenate([cotangent, down_back], axis=1)
+    cot_side = swapped(wide_cot, side)
+    cot_line = swapped(wide_cot, line)
+
     normed_one, unit_one, scale_one = norm_forward(inputs, gain_one)
     normed_one = normed_one.astype(jnp.bfloat16)
     joined_low = masked(product(normed_one, full_f_entry), select)
@@ -1033,9 +1104,8 @@
     context = context_of(pair, 4)
     context, feed_second = lax.optimization_barrier((context, feed_second))
     second_moved = []
-    for bit in distant:
+    for bit in distant[1:]:
         second_moved.append(swapped(feed_second, bit))
-    second_pieces = spread(feed_second, second_moved)
     attended = attend(query, context, pair, query_seq, key_seq)
     output_low = masked(product(attended, full_o_entry), select)
     branch = project(
@@ -1045,36 +1115,36 @@
 
     normed_two, unit_two, scale_two = norm_forward(hidden_one, gain_two)
     normed_two = normed_two.astype(jnp.bfloat16)
+    normed_two, second = lax.optimization_barrier((normed_two, feed_second))
+    second_moved = [swapped(second, distant[0])] + second_moved
+    second_pieces = spread(feed_second, second_moved)
     half_rows = number // 2
     up_group, down_group = (side, line, core), (line, side, core)
     group_normed, group_cot = gather_rows(
-        [normed_two, cotangent],
-        (
-            (0, 0, half_rows, up_group),
-            (0, half_rows, half_rows, down_group),
-            (1, 0, half_rows, up_group),
-            (1, half_rows, half_rows, down_group),
+        [normed_two],
+        ((0, 0, half_rows, up_group), (0, half_rows, half_rows, down_group)),
+        5,
+        (members,),
+        shared=(
+            (0, wide_cot, None),
+            (side, cot_side, (0, half_rows, line)),
+            (line, cot_line, (half_rows, half_rows, side)),
         ),
-        5,
-        (members, members),
-    )
-    both = jnp.concatenate([all_select, all_select], axis=1)
-    lows = masked(product(group_normed, full_gu_entry), both) * ADAPTER_SCALE
-    down_back = masked(ADAPTER_SCALE * product(group_cot, full_d_exit), all_select)
-    mixed_parts, back_parts, feed_grads = feed(
-        group_normed,
-        group_cot,
-        lows[:, :columns],
-        lows[:, columns:],
-        down_back,
-        first_pieces + second_pieces,
-    )
+    )
+    gate_low = masked(product(group_normed, full_g_entry), all_select) * ADAPTER_SCALE
+    up_low = masked(product(group_normed, full_u_entry), all_select) * ADAPTER_SCALE
+    feeding = (group_normed, group_cot, gate_low, up_low)
+    *begun, first_grads = feed(*feeding, first_pieces)
+    mixed_parts, back_parts, second_grads = feed(*feeding, second_pieces, begun)
     up_sum, down_sum = (core, side, line), (core, line, side)
     (back_sum,) = reduce_rows([back_parts], [((0, members), (up_sum, down_sum) * 2)], 6)
-    low_back = masked(
-        ADAPTER_SCALE * back_sum[:, width:], jnp.concatenate([select, select], axis=1)
-    )
-    normed_two_back = back_sum[:, :width] + project(low_back, full_gu_entry)
+    gate_low_back = masked(ADAPTER_SCALE * back_sum[:, width : width + columns], select)
+    up_low_back = masked(ADAPTER_SCALE * back_sum[:, width + columns :], select)
+    normed_two_back = (
+        back_sum[:, :width]
+        + project(gate_low_back, full_g_entry)
+        + project(up_low_back, full_u_entry)
+    )
     hidden_back_one = cotangent.astype(jnp.float32) + norm_backward(
         normed_two_back, unit_two, scale_two, gain_two
     )
@@ -1088,8 +1158,25 @@
     query_back, own_back, away = attend_back(
         query, attended_back, context, pair, query_seq, key_seq, cosine, sine
     )
-    group_sums = ((0, members), (up_sum, down_sum))
-    pair_back, mixed_sum = context_back(away, own_back, mixed_parts, [group_sums], 7)
+    orders = ((core,) + tuple(middle) + head[::-1], (core,) + tuple(middle[::-1]) + head[::-1])
+    places = tuple((mask, at) for at, mask in enumerate(span(distant)))
+    pair_back, mixed_sum, *early = context_back(
+        away,
+        own_back,
+        [
+            mixed_parts,
+            first_grads,
+            second_grads,
+            contract_rows(attended, output_low_back),
+            ADAPTER_SCALE * contract_rows(branch_back, output_low),
+            contract_rows(normed_two, gate_low_back),
+            contract_rows(normed_two, up_low_back),
+        ],
+        [((0, members), (up_sum, down_sum))]
+        + [((at, places), (tuple(distant[::-1]),)) for at in (1, 2)]
+        + [((at, devices), orders) for at in (3, 4, 5, 6)],
+        7,
+    )
     down_low = masked(mixed_sum[:, width:], select)
     mixed = mixed_sum[:, :width] + ADAPTER_SCALE * project(down_low, full_d_exit)
     layer_output = (hidden_one + mixed).astype(jnp.bfloat16)
@@ -1111,39 +1198,29 @@
     normed_one_back = inward[:, :width] + project(joined_low_back, full_f_entry)
     grad_tokens = hidden_back_one + norm_backward(normed_one_back, unit_one, scale_one, gain_one)
 
-    orders = ((core,) + tuple(middle) + head[::-1], (core,) + tuple(middle[::-1]) + head[::-1])
-    low_grads = contract_rows(normed_two, low_back)
     totals = [
-        contract_rows(attended, output_low_back),
-        ADAPTER_SCALE * contract_rows(branch_back, output_low),
-        low_grads[:, :columns],
-        low_grads[:, columns:],
         ADAPTER_SCALE * contract_rows(cotangent, down_low),
-        feed_grads,
         contract_rows(joined_back, half_low),
         contract_rows(normed_one, joined_low_back),
     ]
-    sums = [((at, devices), orders) for at in range(len(totals))]
-    blocks = len(first_pieces)
-    feed_grads = feed_grads.reshape(2, blocks, half_shard, -1).transpose(1, 0, 2, 3)
-    totals[5] = feed_grads.reshape(2 * blocks * half_shard, -1)
-    sums[5] = ((5, {mask: at for at, mask in enumerate(span(distant))}), (tuple(distant[::-1]),))
-    reduced = reduce_rows(totals, sums, 8)
-    early, late = reduced[:6], (reduced[6], reduced[7])
-    feed_rows = early[5]
+    d_exit, f_exit, f_entry = reduce_rows(
+        totals, [((at, devices), orders) for at in range(len(totals))], 8
+    )
+    feed_rows = jnp.concatenate(early[:2], axis=0)
+    o_entry, o_exit, g_entry, u_entry = early[2:]
     return (
         layer_output,
         grad_tokens,
-        late[1],
-        late[0],
-        early[0],
-        early[1],
-        early[2],
+        f_entry,
+        f_exit,
+        o_entry,
+        o_exit,
+        g_entry,
         feed_rows[:, :columns],
-        early[3],
+        u_entry,
         feed_rows[:, columns : 2 * columns],
         feed_rows[:, 2 * columns :],
-        early[4],
+        d_exit,
     )
 
 

time: 761 us -> 749 us (0.984)
  local copies, waits for them, and re-layouts: 24.9 us -> 13.3 us
    pallas_call x2, Pallas kernels: 236 us -> 212 us  [gather_rows(): pl.pallas_call(functools.partial(gather_kernel, parts, slots, bits_moved,...]
    pallas_call x2 -> x3, Pallas kernels: 175 us -> 198 us  [the longest x1 115 us: context_back(): pl.pallas_call(functools.partial(context_back_kernel, devices, parts, (le...]
    ppermute x4 -> x6, waiting for transfers between devices: 25.9 us -> 21.9 us  [swapped(): lax.ppermute(value, AXIS, [(source, source ^ bit) for source in range(cou...]
    dot_general x6 -> x7, matrix products: 31.1 us -> 30.6 us  [product(): return jnp.dot(left, right, preferred_element_type=jnp.float32)]
    dot_general x5 -> x6, matrix products: 17 us -> 17.2 us  [project(): lax.dot_general(left, right, (((1,), (1,)), ((), ())), preferred_element_...]
  transfers between devices with their start and end apart: 4 -> 6, of which waited for: 1 -> 1; matrix products, arithmetic and copies ran while one was open for 3% -> 4% of each run, Pallas kernels for 15% -> 26%
where the time goes in v3:
time: 749 us; the launch traced here: 741 us
  Pallas kernels  611 us (82%)
  matrix products  62 us (8%)
  other arithmetic  24.8 us (3%)
  waiting for transfers between devices  21.9 us (3%)
  local copies, waits for them, and re-layouts  13.3 us (2%)
    pallas_call x2, Pallas kernels, gather_rows(): pl.pallas_call(functools.partial(gather_kernel, parts, slots, bits_moved,...  212 us
    pallas_call x1, Pallas kernels, context_back(): pl.pallas_call(functools.partial(context_back_kernel, devices, parts, (le...  115 us
    pallas_call x2, Pallas kernels, reduce_rows(): pl.pallas_call(functools.partial(reduce_kernel, parts, (len(values), len(...  94 us
    pallas_call x2, Pallas kernels, feed(): pl.pallas_call(functools.partial(feed_kernel, pieces, hid // height, len(...  83.5 us
    pallas_call x1, Pallas kernels, context_of(): pl.pallas_call(functools.partial(context_kernel, devices), out_shape=jax....  50.1 us
    dot_general x7, matrix products, product(): return jnp.dot(left, right, preferred_element_type=jnp.float32)  30.6 us
    pallas_call x1, Pallas kernels, attend_back(): pl.pallas_call(functools.partial(attend_back_kernel, blocks), out_shape=[...  26.7 us
    ppermute x6, waiting for transfers between devices, swapped(): lax.ppermute(value, AXIS, [(source, source ^ bit) for source in range(cou...  21.9 us
  transfers between devices with their start and end apart: 6, of which 1 were waited for; matrix products, arithmetic and copies ran while one was open for 4% of the time, Pallas kernels for 26%

profile of v3, /device:TPU:0, one launch (start us, length us, event | category | flops | bytes accessed | tf_op | source)
XLA Modules:
  0.0 741.5 jit_solution(5415876008375497101)
XLA Ops:
  7.4 2.0 pad_maximum_fusion.5.refs_0_
  9.4 1.7 pad_maximum_fusion.6.refs_2_
  11.1 5.3 maximum_maximum_fusion
  16.4 143.3 %gather_rows.2 = (bf16[4096,2176]{1,0:T(8,128)(2,1)}, bf16[2048,128]{1,0:T(8,128)(2,1)}, bf16[2048,2176]{1,0:T(8,128)(2,1)}, bf16[2048,128]{1,0:T(8,128)(2,1)}, ...) custom-call(bf16[128,2176]{1,0:T(8,128)(2,1)} %pad_maximum_fusion.5., ...), custom_call_target="tpu_custom_call" | custom-call | bytes 234881024 | tf_op jit(solution)/shard_map/gather_rows/pallas_call | solution.py:262
  159.7 1.6 fusion.20
  163.9 1.5 collective-permute-start.1
  170.5 13.3 %joined_heads.1 = (bf16[256,2048]{1,0:T(8,128)(2,1)}, bf16[256,2048]{1,0:T(8,128)(2,1)}) custom-call(bf16[256,2176]{1,0:T(8,128)(2,1)} %pad_maximum_fusion.1.x_ref, bf16[4096,2176]{1,0:T(8,128)(2,1)} %get-tuple-element.56.w_ref, f32[256,128]{1,0:T(8,128)} %pad_maximum_fusion.7.cos_ref.refs_14_, f32[256,128]{1,0:T(8,128)} %pad_maximum_fusion.8.sin_ref.refs_15_), custom_call_target="tpu_custom_call" | custom-call | flops 4563402752 | bytes 20054016 | tf_op jit(solution)/shard_map/joined_heads/pallas_call | solution.py:698
  183.8 50.1 %context.1.refs_1_.refs_2_.refs_3_.refs_4_.refs_6_.refs_7_.refs_8_.refs_9_.refs_5_.refs_10_ = bf16[4,256,2048]{2,1,0:T(8,128)(2,1)} custom-call(bf16[256,2048]{1,0:T(8,128)(2,1)} %get-tuple-element.58.pair_ref.refs_5_.refs_10_.refs_6_.refs_11_), custom_call_target="tpu_custom_call" | custom-call | bytes 33554432 | tf_op jit(solution)/shard_map/context/pallas_call | solution.py:546
  235.5 16.7 %attend.1 = bf16[256,2048]{1,0:T(8,128)(2,1)} custom-call(bf16[256,2048]{1,0:T(8,128)(2,1)} %get-tuple-element.57.refs_0_, bf16[4,256,2048]{2,1,0:T(8,128)(2,1)} %context.1.refs_1_.refs_2_.refs_3_.refs_4_.refs_6_.refs_7_.refs_8_.refs_9_.refs_5_.refs_10_, ...), custom_call_target="tpu_custom_call" | custom-call | flops 2684354560 | bytes 7340032 | tf_op jit(solution)/shard_map/attend/pallas_call | solution.py:774
  252.2 1.7 broadcast_multiply_fusion
  253.8 6.8 multiply_reduce_fusion.1
  263.7 1.5 collective-permute-start.3
  265.2 68.8 %gather_rows.3 = (bf16[2048,2048]{1,0:T(8,128)(2,1)}, bf16[2048,2176]{1,0:T(8,128)(2,1)}) custom-call(bf16[256,2048]{1,0:T(8,128)(2,1)} %multiply_convert_fusion.refs_0_, bf16[256,2176]{1,0:T(8,128)(2,1)} %pad_maximum_fusion.2.refs_1_, bf16[256,2176]{1,0:T(8,128)(2,1)} %collective-permute-done.refs_2_, bf16[256,2176]{1,0:T(8,128)(2,1)} %collective-permute-done.1.refs_3_), custom_call_target="tpu_custom_call" | custom-call | bytes 67108864 | tf_op jit(solution)/shard_map/gather_rows/pallas_call | solution.py:262
  334.0 6.8 fusion.8.refs_3_
  340.8 3.2 fusion.9.refs_2_
  344.2 41.2 %feed.2 = (bf16[2048,2176]{1,0:T(8,128)(2,1)}, bf16[2048,2304]{1,0:T(8,128)(2,1)}, f32[512,384]{1,0:T(8,128)}) custom-call(bf16[2048,2048]{1,0:T(8,128)(2,1)} %get-tuple-element.65.refs_0_, bf16[2048,2176]{1,0:T(8,128)(2,1)} %get-tuple-element.66.refs_1_, bf16[2048,128]{1,0:T(8,128)(2,1)} %fusion.9.refs_2_, bf16[2048,128]{1,0:T(8,128)(2,1)} %fusion.8.refs_3_, ...), custom_call_target="tpu_custom_call" | custom-call | flops 27380416512 | bytes 65404928 | tf_op jit(solution)/shard_map/feed/pallas_call | solution.py:948
  385.5 21.9 %collective-permute-done.4.refs_7_ = bf16[384,2176]{1,0:T(8,128)(2,1)} collective-permute-done((bf16[384,2176]{1,0:T(8,128)(2,1)}, bf16[384,2176]{1,0:T(8,128)(2,1)}, u32[]{:S(2)}, u32[]{:S(2)}) %collective-permute-start.4) | collective-permute-done | bytes 1671200 | tf_op jit(solution)/shard_map/ppermute | solution.py:29
  407.4 42.3 %feed.3 = (bf16[2048,2176]{1,0:T(8,128)(2,1)}, bf16[2048,2304]{1,0:T(8,128)(2,1)}, f32[512,384]{1,0:T(8,128)}) custom-call(bf16[2048,2048]{1,0:T(8,128)(2,1)} %get-tuple-element.65.refs_0_, bf16[2048,2176]{1,0:T(8,128)(2,1)} %get-tuple-element.66.refs_1_, bf16[2048,128]{1,0:T(8,128)(2,1)} %fusion.9.refs_2_, bf16[2048,128]{1,0:T(8,128)(2,1)} %fusion.8.refs_3_, ...), custom_call_target="tpu_custom_call" | custom-call | flops 27380416512 | bytes 65404928 | tf_op jit(solution)/shard_map/feed/pallas_call | solution.py:948
  449.7 63.3 %reduce_rows.2 = f32[256,2304]{1,0:T(8,128)} custom-call(bf16[2048,2304]{1,0:T(8,128)(2,1)} %get-tuple-element.74.refs_0_), custom_call_target="tpu_custom_call" | custom-call | bytes 150994944 | tf_op jit(solution)/shard_map/reduce_rows/pallas_call | solution.py:402
  513.0 2.8 fusion.45.refs_6_
  515.8 2.4 fusion.43.refs_5_
  519.6 2.5 multiply_reduce_fusion
  522.6 6.9 fusion.30
  533.9 26.7 %attend_back.1 = (bf16[256,2048]{1,0:T(8,128)(2,1)}, f32[2,256,1024]{2,1,0:T(8,128)}, bf16[4,2,256,1024]{3,2,1,0:T(8,128)(2,1)}) custom-call(bf16[256,2048]{1,0:T(8,128)(2,1)} %get-tuple-element.57.refs_0_, bf16[256,2048]{1,0:T(8,128)(2,1)} %fusion.4.refs_1_, ...), custom_call_target="tpu_custom_call" | custom-call | flops 6710886400 | bytes 24117248 | tf_op jit(solution)/shard_map/attend_back/pallas_call | solution.py:847
  560.7 114.7 %context_back.1 = (f32[2,256,1024]{2,1,0:T(8,128)}, f32[256,2176]{1,0:T(8,128)}, f32[128,384]{1,0:T(8,128)}, f32[128,384]{1,0:T(8,128)}, f32[64,128]{1,0:T(8,128...) custom-call(bf16[4,2,256,1024]{3,2,1,0:T(8,128)(2,1)} %get-tuple-element.75.away, ...), custom_call_target="tpu_custom_call" | custom-call | bytes 33554432 | tf_op jit(solution)/shard_map/context_back/pallas_call | solution.py:647
  680.2 2.1 fusion.26.refs_1_
  682.3 10.0 %fusion.27 = f32[256,2176]{1,0:T(8,128)S(1)} fusion(bf16[4096,2176]{1,0:T(8,128)(2,1)} %get-tuple-element.56.w_ref, bf16[256,1024]{1,0:T(8,128)(2,1)S(1)} %fusion.28, bf16[256,1024]{1,0:T(8,128)(2,1)S(1)} %fusion.25, bf16[256,2048]{1,0:T(8,128)(2,1)S(1)} %copy-done.55), kind=kOutput, calls=%fused_computation.56 | convolution fusion | flops 4569694208 | bytes 22151168 | tf_op jit(solution)/shard_map/dot_general | solution.py:39
  693.9 1.9 fusion.11
  695.8 2.6 fusion.5.refs_0_
  698.4 3.2 add_convert_fusion
  702.4 30.7 %reduce_rows.3 = (f32[64,128]{1,0:T(8,128)}, f32[128,128]{1,0:T(8,128)}, f32[64,128]{1,0:T(8,128)}) custom-call(f32[2048,128]{1,0:T(8,128)} %fusion.5.refs_0_, f32[4096,128]{1,0:T(8,128)} %fusion.26.refs_1_, f32[2048,128]{1,0:T(8,128)} %fusion.50.refs_2_), custom_call_target="tpu_custom_call" | custom-call | bytes 33554432 | tf_op jit(solution)/shard_map/reduce_rows/pallas_call | solution.py:402
  733.2 3.4 fusion.14
  (179 shorter events, 36.7 us)
Async XLA Ops:
  0.7 5.0 copy-start.46
  7.4 523.7 %copy-start.18 = (pred[2048,128]{1,0:T(32,128)(4,1)}, pred[2048,128]{1,0:T(32,128)(4,1)S(1)}, u32[]{:S(2)}) copy-start(pred[2048,128]{1,0:T(32,128)(4,1)S(1)} %broadcast_compare_fusion) | copy-start | bytes 786436
  16.4 143.3 %copy-start.4 = (bf16[256,2048]{1,0:T(8,128)(2,1)S(1)}, bf16[256,2048]{1,0:T(8,128)(2,1)}, u32[]{:S(2)}) copy-start(bf16[256,2048]{1,0:T(8,128)(2,1)} %param.41) | copy-start | bytes 3145732
  159.7 5.7 copy-start.10
  159.7 6.0 copy-start.44
  162.4 102.8 %collective-permute-start = (bf16[256,2176]{1,0:T(8,128)(2,1)}, bf16[256,2176]{1,0:T(8,128)(2,1)}, u32[]{:S(2)}, u32[]{:S(2)}) collective-permute-start(bf16[256,2176]{1,0:T(8,128)(2,1)} %pad_maximum_fusion.2.refs_1_), channel_id=1, source_target_pairs={{0,2},{1,3},{2,0},{3,1},{4,6},{5,7},{6,4},{7,5},{8,10},{9,11},{10,... | collective-permute-start | bytes 3342344 | tf_op jit(solution)/shard_map/ppermute | solution.py:29
  163.9 101.3 %collective-permute-start.1 = (bf16[256,2176]{1,0:T(8,128)(2,1)}, bf16[256,2176]{1,0:T(8,128)(2,1)}, u32[]{:S(2)}, u32[]{:S(2)}) collective-permute-start(bf16[256,2176]{1,0:T(8,128)(2,1)} %pad_maximum_fusion.2.refs_1_), channel_id=1, source_target_pairs={{0,4},{1,5},{2,6},{3,7},{4,0},{5,1},{6,2},{7,3},{8,12},{9,13},{10,... | collective-permute-start | bytes 3342344 | tf_op jit(solution)/shard_map/ppermute | solution.py:29
  166.5 17.2 %copy-start.26 = (bf16[256,128]{1,0:T(8,128)(2,1)}, bf16[256,128]{1,0:T(8,128)(2,1)S(1)}, u32[]{:S(2)}) copy-start(bf16[256,128]{1,0:T(8,128)(2,1)S(1)} %fusion.21) | copy-start | bytes 196612
  183.8 51.0 %copy-start.47 = (s32[15]{0:T(128)S(1)}, s32[15]{0:T(128)}, u32[]{:S(2)}) copy-start(s32[15]{0:T(128)} %copy-done.46) | copy-start | bytes 184
  183.8 51.0 %copy-start.49 = (s32[15,1]{0,1:T(1,128)S(1)}, s32[15,1]{0,1:T(1,128)}, u32[]{:S(2)}) copy-start(s32[15,1]{0,1:T(1,128)} %copy-done.48) | copy-start | bytes 184
  183.8 51.0 %copy-start.51 = (s32[15]{0:T(128)S(1)}, s32[15]{0:T(128)}, u32[]{:S(2)}) copy-start(s32[15]{0:T(128)} %copy-done.50) | copy-start | bytes 184
  183.8 51.7 %copy-start.45 = (bf16[2048]{0:T(1024)(128)(2,1)S(1)}, bf16[2048]{0:T(1024)(128)(2,1)}, u32[]{:S(2)}) copy-start(bf16[2048]{0:T(1024)(128)(2,1)} %param.23) | copy-start | bytes 12292
  235.5 16.7 %copy-start.15 = (bf16[2048,128]{1,0:T(8,128)(2,1)S(1)}, bf16[2048,128]{1,0:T(8,128)(2,1)}, u32[]{:S(2)}) copy-start(bf16[2048,128]{1,0:T(8,128)(2,1)} %get-tuple-element.60) | copy-start | bytes 1572868
  260.6 261.5 %copy-start = (f32[256,2048]{1,0:T(8,128)}, f32[256,2048]{1,0:T(8,128)S(1)}, u32[]{:S(2)}) copy-start(f32[256,2048]{1,0:T(8,128)S(1)} %get-tuple-element.118) | copy-start | bytes 6291460
  262.1 71.9 %copy-start.53 = (s32[128]{0:T(128)S(1)}, s32[128]{0:T(128)}, u32[]{:S(2)}) copy-start(s32[128]{0:T(128)} %and_select_fusion) | copy-start | bytes 1540
  262.1 82.0 %collective-permute-start.2 = (bf16[384,2176]{1,0:T(8,128)(2,1)}, bf16[384,2176]{1,0:T(8,128)(2,1)}, u32[]{:S(2)}, u32[]{:S(2)}) collective-permute-start(bf16[384,2176]{1,0:T(8,128)(2,1)} %get-tuple-element.69.refs_4_), channel_id=1, source_target_pairs={{0,16},{1,17},{2,18},{3,19},{4,20},{5,21},{6,22},{7,23},{8,24},{9,... | collective-permute-start | bytes 5013512 | tf_op jit(solution)/shard_map/ppermute | solution.py:29
  263.2 81.1 %collective-permute-start.5 = (bf16[384,2176]{1,0:T(8,128)(2,1)}, bf16[384,2176]{1,0:T(8,128)(2,1)}, u32[]{:S(2)}, u32[]{:S(2)}) collective-permute-start(bf16[384,2176]{1,0:T(8,128)(2,1)} %get-tuple-element.70.refs_5_), channel_id=1, source_target_pairs={{0,8},{1,9},{2,10},{3,11},{4,12},{5,13},{6,14},{7,15},{8,0},{9,1},... | collective-permute-start | bytes 5013512 | tf_op jit(solution)/shard_map/ppermute | solution.py:29
  263.7 121.8 %collective-permute-start.3 = (bf16[384,2176]{1,0:T(8,128)(2,1)}, bf16[384,2176]{1,0:T(8,128)(2,1)}, u32[]{:S(2)}, u32[]{:S(2)}) collective-permute-start(bf16[384,2176]{1,0:T(8,128)(2,1)} %get-tuple-element.69.refs_4_), channel_id=1, source_target_pairs={{0,8},{1,9},{2,10},{3,11},{4,12},{5,13},{6,14},{7,15},{8,0},{9,1},... | collective-permute-start | bytes 5013512 | tf_op jit(solution)/shard_map/ppermute | solution.py:29
  334.0 6.8 copy-start.24
  334.0 6.8 copy-start.54
  344.0 63.4 %collective-permute-start.4 = (bf16[384,2176]{1,0:T(8,128)(2,1)}, bf16[384,2176]{1,0:T(8,128)(2,1)}, u32[]{:S(2)}, u32[]{:S(2)}) collective-permute-start(bf16[384,2176]{1,0:T(8,128)(2,1)} %collective-permute-done.2.refs_5_), channel_id=1, source_target_pairs={{0,8},{1,9},{2,10},{3,11},{4,12},{5,13},{6,14},{7,15},{8,0},{9,1},... | collective-permute-start | bytes 5013512 | tf_op jit(solution)/shard_map/ppermute | solution.py:29
  522.6 9.8 %copy-start.2 = (f32[256,2048]{1,0:T(8,128)}, f32[256,2048]{1,0:T(8,128)S(1)}, u32[]{:S(2)}) copy-start(f32[256,2048]{1,0:T(8,128)S(1)} %multiply_add_fusion) | copy-start | bytes 6291460
  522.6 6.9 copy-start.9
  682.3 10.0 %copy-start.7 = (bf16[256,2048]{1,0:T(8,128)(2,1)S(1)}, bf16[256,2048]{1,0:T(8,128)(2,1)}, u32[]{:S(2)}) copy-start(bf16[256,2048]{1,0:T(8,128)(2,1)} %copy-done.6) | copy-start | bytes 3145732
  682.3 10.0 %copy-start.19 = (pred[2048,128]{1,0:T(32,128)(4,1)S(1)}, pred[2048,128]{1,0:T(32,128)(4,1)}, u32[]{:S(2)}) copy-start(pred[2048,128]{1,0:T(32,128)(4,1)} %copy-done.18) | copy-start | bytes 786436
  693.9 4.5 copy-start.17
  702.4 30.8 %copy-start.3 = (f32[256,2048]{1,0:T(8,128)S(1)}, f32[256,2048]{1,0:T(8,128)}, u32[]{:S(2)}) copy-start(f32[256,2048]{1,0:T(8,128)} %copy-done.2) | copy-start | bytes 6291460
  733.2 4.7 copy-start.39
  733.2 5.4 copy-start.38
  733.2 6.0 copy-start.37
  733.2 6.6 copy-start.36
  733.2 7.2 copy-start.40
  (30 other events, 64.6 us)

commit v4 on v3

--- a/solution.py
+++ b/solution.py
@@ -289,10 +289,10 @@
         self.levels = max(len(part[4]) for part in parts)
 
     def given(self, p, mask):
-        _, block, first, rows, _, places = self.parts[p]
+        _, block, first, rows, _, places, base, _ = self.parts[p]
         a, place = places
         if isinstance(place, int):
-            at = peer_of(self.me, mask) % place
+            at = peer_of(self.me, mask + base) % place
         else:
             at = dict(place)[mask]
         return self.ins[a].at[pl.ds(pl.multiple_of(at * block + first, 8), rows)]
@@ -303,21 +303,20 @@
     def launch(self, p, level):
         order = self.parts[p][4]
         bit, half = order[level], 1 << (len(order) - 1 - level)
-        copies = []
+        region, copies = pl.ds(half - 1, half), []
         if level:
-            self.outgoing[p][half : 2 * half] = self.totals[p][half : 2 * half].astype(jnp.bfloat16)
-            copies.append((self.outgoing[p].at[pl.ds(half, half)], half, half))
+            self.outgoing[p][region] = self.totals[p][half : 2 * half].astype(jnp.bfloat16)
+            copies.append((self.outgoing[p].at[region], region, half))
         else:
             for at, mask in enumerate(self.masks(p)):
                 source = self.given(p, mask + bit)
                 if source.dtype == jnp.bfloat16:
-                    copies.append((source, half + at, None))
+                    copies.append((source, half - 1 + at, half + at))
                 else:
-                    self.outgoing[p][half + at] = source[...].astype(jnp.bfloat16)
+                    self.outgoing[p][half - 1 + at] = source[...].astype(jnp.bfloat16)
             if not copies:
-                copies.append((self.outgoing[p].at[pl.ds(half, half)], half, half))
-        for source, at, number in copies:
-            there = at if number is None else pl.ds(at, number)
+                copies.append((self.outgoing[p].at[region], region, half))
+        for source, there, at in copies:
             copy = pltpu.make_async_remote_copy(
                 src_ref=source,
                 dst_ref=self.incoming[p].at[there],
@@ -335,27 +334,29 @@
             self.launch(p, 0)
 
     def advance(self, level):
-        for p in range(len(self.parts)):
-            order = self.parts[p][4]
+        for p, (a, _, _, rows, order, _, _, row) in enumerate(self.parts):
             if level >= len(order):
                 continue
             half, wide = 1 << (len(order) - 1 - level), jnp.float32
             arrived, self.pending[p] = self.pending[p], []
             for copy in arrived:
                 copy.wait_recv()
-            if level:
-                came = self.incoming[p][half : 2 * half].astype(wide)
+            last = level + 1 == len(order)
+            if last:
+                held = self.totals[p][0] if level else self.given(p, 0)[...].astype(wide)
+                total = held + self.incoming[p][0].astype(wide)
+                self.outs[a][row : row + rows, :] = total.astype(self.outs[a].dtype)
+            elif level:
+                came = self.incoming[p][half - 1 : 2 * half - 1].astype(wide)
                 self.totals[p][:half] = self.totals[p][:half] + came
             else:
                 for at, mask in enumerate(self.masks(p)):
-                    came = self.incoming[p][half + at].astype(wide)
+                    came = self.incoming[p][half - 1 + at].astype(wide)
                     self.totals[p][at] = self.given(p, mask)[...].astype(wide) + came
-            if level + 1 < len(order):
+            if not last:
                 self.launch(p, level + 1)
 
     def finish(self):
-        for p, (a, _, first, rows, _, _) in enumerate(self.parts):
-            self.outs[a][first : first + rows, :] = self.totals[p][0]
         for copy in self.every:
             copy.wait_send()
 
@@ -375,38 +376,50 @@
     halving.finish()
 
 
-def reduce_plan(values, sums):
+def reduce_plan(values, sums, steps=()):
     parts, shapes, scratch = [], [], []
+
+    def add(part, columns, given):
+        members, rows = 1 << len(part[4]), part[3]
+        held = members // 2 if given == jnp.bfloat16 else members
+        sizes = (members // 2 if members > 2 else 0, held - 1, members - 1)
+        parts.append(part)
+        scratch.append([(n, rows, columns) if n else (1, 8, 128) for n in sizes])
+
     for a, (places, orders) in enumerate(sums):
-        members = 1 << len(orders[0])
-        source = places[0]
-        block = values[source].shape[0] // members
-        columns = values[source].shape[1]
+        value = values[places[0]]
+        block, columns = value.shape[0] >> len(orders[0]), value.shape[1]
         shapes.append(jax.ShapeDtypeStruct((block, columns), jnp.float32))
         pieces = len(orders) if block % (64 * len(orders)) == 0 else 1
         rows = block // pieces
         for i in range(pieces):
-            parts.append((a, block, i * rows, rows, orders[(a + i) % len(orders)], places))
-            out = members // 2 if values[source].dtype == jnp.bfloat16 else members
-            scratch.append([(n, rows, columns) for n in (members // 2, out, members)])
-    most = max(s[2][0] for s in scratch)
+            order = orders[(a + i) % len(orders)]
+            add((a, block, i * rows, rows, order, places, 0, i * rows), columns, value.dtype)
+    for places, bit, members, first, rows, bases, kind in steps:
+        value = values[places[0]]
+        block, columns = value.shape[0] // members, value.shape[1]
+        for i, base in enumerate(bases):
+            part = (len(shapes), block, first, rows, (bit,), places, base, i * rows)
+            add(part, columns, value.dtype)
+        shapes.append(jax.ShapeDtypeStruct((len(bases) * rows, columns), kind))
+    most = max(1 << len(part[4]) for part in parts)
     kinds = (jnp.float32, jnp.bfloat16, jnp.bfloat16)
     buffers = [pltpu.VMEM(s[i], kinds[i]) for i in range(3) for s in scratch]
     buffers += [pltpu.SemaphoreType.DMA((len(parts), most))] * 2
     return tuple(parts), shapes, buffers
 
 
-def reduce_rows(values, sums, collective_id):
-    parts, shapes, buffers = reduce_plan(values, sums)
+def reduce_rows(values, sums, collective_id, steps=()):
+    parts, shapes, buffers = reduce_plan(values, sums, steps)
     sent = 2 * sum(value.size for value in values)
     return pl.pallas_call(
-        functools.partial(reduce_kernel, parts, (len(values), len(sums))),
+        functools.partial(reduce_kernel, parts, (len(values), len(shapes))),
         out_shape=shapes,
         in_specs=[pl.BlockSpec(memory_space=pltpu.VMEM)] * len(values),
-        out_specs=[pl.BlockSpec(memory_space=pltpu.VMEM)] * len(sums),
+        out_specs=[pl.BlockSpec(memory_space=pltpu.VMEM)] * len(shapes),
         scratch_shapes=buffers,
         compiler_params=pltpu.CompilerParams(
-            collective_id=collective_id, has_side_effects=True, vmem_limit_bytes=VMEM_LIMIT
+            collective_id=collective_id, has_side_effects=True, vmem_limit_bytes=67043328
         ),
         cost_estimate=pl.CostEstimate(flops=0, bytes_accessed=16 * sent, transcendentals=0),
         name="reduce_rows",
@@ -597,6 +610,7 @@
         for i, slot in enumerate((3, 1)):
             shared.append(copy(i, c, away.at[slot, h, rows], beside.at[i, h, rows], partner))
             shared[-1].start()
+    halving.begin()
     out_ref[...] = own[...]
     far = []
     for h, rows, c in chunks:
@@ -619,7 +633,6 @@
             def _(move=move):
                 move.start()
 
-    halving.begin()
     for level in range(halving.levels):
         halving.advance(level)
     for i, h, rows, step, move in far:
@@ -690,7 +703,7 @@
 
 def joined_heads(x, weight, cosine, sine):
     number, depth = x.shape
-    tile = 512
+    tile = 1024
     steps = weight.shape[0] // tile
     half = steps // 2
     turned = (HEADS + KV_HEADS) * HEAD_WIDTH // tile
@@ -1137,7 +1150,22 @@
     *begun, first_grads = feed(*feeding, first_pieces)
     mixed_parts, back_parts, second_grads = feed(*feeding, second_pieces, begun)
     up_sum, down_sum = (core, side, line), (core, line, side)
-    (back_sum,) = reduce_rows([back_parts], [((0, members), (up_sum, down_sum) * 2)], 6)
+    step = lambda first, bases, kind: (
+        (1, members), core, members, first, half_rows, bases, kind
+    )
+    back_sum, keep_up, send_up, keep_down, send_down = reduce_rows(
+        [back_parts, mixed_parts],
+        [((0, members), (up_sum, down_sum) * 2)],
+        6,
+        (
+            step(0, (0, line), jnp.float32),
+            step(0, (side, side + line), jnp.bfloat16),
+            step(half_rows, (0, side), jnp.float32),
+            step(half_rows, (line, side + line), jnp.bfloat16),
+        ),
+    )
+    came_up = swapped(send_up, side)
+    came_down = swapped(send_down, line)
     gate_low_back = masked(ADAPTER_SCALE * back_sum[:, width : width + columns], select)
     up_low_back = masked(ADAPTER_SCALE * back_sum[:, width + columns :], select)
     normed_two_back = (
@@ -1160,11 +1188,14 @@
     )
     orders = ((core,) + tuple(middle) + head[::-1], (core,) + tuple(middle[::-1]) + head[::-1])
     places = tuple((mask, at) for at, mask in enumerate(span(distant)))
-    pair_back, mixed_sum, *early = context_back(
+    mixed_up = keep_up + came_up.astype(jnp.float32)
+    mixed_down = keep_down + came_down.astype(jnp.float32)
+    pair_back, mixed_up, mixed_down, *early = context_back(
         away,
         own_back,
         [
-            mixed_parts,
+            mixed_up,
+            mixed_down,
             first_grads,
             second_grads,
             contract_rows(attended, output_low_back),
@@ -1172,11 +1203,12 @@
             contract_rows(normed_two, gate_low_back),
             contract_rows(normed_two, up_low_back),
         ],
-        [((0, members), (up_sum, down_sum))]
-        + [((at, places), (tuple(distant[::-1]),)) for at in (1, 2)]
-        + [((at, devices), orders) for at in (3, 4, 5, 6)],
+        [((0, ((0, 0), (line, 1))), ((line,),)), ((1, ((0, 0), (side, 1))), ((side,),))]
+        + [((at, places), (tuple(distant[::-1]),)) for at in (2, 3)]
+        + [((at, devices), orders) for at in (4, 5, 6, 7)],
         7,
     )
+    mixed_sum = jnp.concatenate([mixed_up, mixed_down], axis=0)
     down_low = masked(mixed_sum[:, width:], select)
     mixed = mixed_sum[:, :width] + ADAPTER_SCALE * project(down_low, full_d_exit)
     layer_output = (hidden_one + mixed).astype(jnp.bfloat16)

time: 749 us -> 737 us (0.984)
  Pallas kernels: 611 us -> 586 us
    pallas_call x1, Pallas kernels: 115 us -> 89.3 us  [context_back(): pl.pallas_call(functools.partial(context_back_kernel, devices, parts, (le...]
    ppermute x6 -> x8, waiting for transfers between devices: 21.9 us -> 23.8 us  [swapped(): lax.ppermute(value, AXIS, [(source, source ^ bit) for source in range(cou...]
  transfers between devices with their start and end apart: 6 -> 8, of which waited for: 1 -> 1; matrix products, arithmetic and copies ran while one was open for 4% -> 4% of each run, Pallas kernels for 26% -> 29%
where the time goes in v4:
time: 737 us; the launch traced here: 729 us
  Pallas kernels  586 us (80%)
  matrix products  60.8 us (8%)
  other arithmetic  28.5 us (4%)
  waiting for transfers between devices  23.8 us (3%)
  local copies, waits for them, and re-layouts  17.8 us (2%)
  starting transfers between devices  10.2 us (1%)
    pallas_call x2, Pallas kernels, gather_rows(): pl.pallas_call(functools.partial(gather_kernel, parts, slots, bits_moved,...  210 us
    pallas_call x2, Pallas kernels, reduce_rows(): pl.pallas_call(functools.partial(reduce_kernel, parts, (len(values), len(...  96.2 us
    pallas_call x1, Pallas kernels, context_back(): pl.pallas_call(functools.partial(context_back_kernel, devices, parts, (le...  89.3 us
    pallas_call x2, Pallas kernels, feed(): pl.pallas_call(functools.partial(feed_kernel, pieces, hid // height, len(...  83.5 us
    pallas_call x1, Pallas kernels, context_of(): pl.pallas_call(functools.partial(context_kernel, devices), out_shape=jax....  52.2 us
    dot_general x7, matrix products, product(): return jnp.dot(left, right, preferred_element_type=jnp.float32)  31.2 us
    pallas_call x1, Pallas kernels, attend_back(): pl.pallas_call(functools.partial(attend_back_kernel, blocks), out_shape=[...  26.8 us
    ppermute x8, waiting for transfers between devices, swapped(): lax.ppermute(value, AXIS, [(source, source ^ bit) for source in range(cou...  23.8 us
  transfers between devices with their start and end apart: 8, of which 1 were waited for; matrix products, arithmetic and copies ran while one was open for 4% of the time, Pallas kernels for 29%

profile of v4, /device:TPU:0, one launch (start us, length us, event | category | flops | bytes accessed | tf_op | source)
XLA Modules:
  0.0 728.9 jit_solution(986910414504580154)
XLA Ops:
  7.4 2.0 pad_maximum_fusion.5.refs_0_
  9.4 1.7 pad_maximum_fusion.6.refs_2_
  11.1 5.3 maximum_maximum_fusion
  16.4 143.3 %gather_rows.2 = (bf16[4096,2176]{1,0:T(8,128)(2,1)}, bf16[2048,128]{1,0:T(8,128)(2,1)}, bf16[2048,2176]{1,0:T(8,128)(2,1)}, bf16[2048,128]{1,0:T(8,128)(2,1)}, ...) custom-call(bf16[128,2176]{1,0:T(8,128)(2,1)} %pad_maximum_fusion.5., ...), custom_call_target="tpu_custom_call" | custom-call | bytes 234881024 | tf_op jit(solution)/shard_map/gather_rows/pallas_call | solution.py:262
  169.6 11.0 %joined_heads.1 = (bf16[256,2048]{1,0:T(8,128)(2,1)}, bf16[256,2048]{1,0:T(8,128)(2,1)}) custom-call(bf16[256,2176]{1,0:T(8,128)(2,1)} %pad_maximum_fusion.1.x_ref, bf16[4096,2176]{1,0:T(8,128)(2,1)} %get-tuple-element.62.w_ref, f32[256,128]{1,0:T(8,128)} %pad_maximum_fusion.7.cos_ref.refs_14_, f32[256,128]{1,0:T(8,128)} %pad_maximum_fusion.8.sin_ref.refs_15_), custom_call_target="tpu_custom_call" | custom-call | flops 4563402752 | bytes 20054016 | tf_op jit(solution)/shard_map/joined_heads/pallas_call | solution.py:711
  180.6 52.2 %context.1.refs_1_.refs_2_.refs_3_.refs_4_.refs_6_.refs_7_.refs_8_.refs_9_.refs_5_.refs_10_ = bf16[4,256,2048]{2,1,0:T(8,128)(2,1)} custom-call(bf16[256,2048]{1,0:T(8,128)(2,1)} %get-tuple-element.64.pair_ref.refs_5_.refs_10_.refs_6_.refs_11_), custom_call_target="tpu_custom_call" | custom-call | bytes 33554432 | tf_op jit(solution)/shard_map/context/pallas_call | solution.py:559
  234.3 16.7 %attend.1 = bf16[256,2048]{1,0:T(8,128)(2,1)} custom-call(bf16[256,2048]{1,0:T(8,128)(2,1)} %get-tuple-element.63.refs_0_, bf16[4,256,2048]{2,1,0:T(8,128)(2,1)} %context.1.refs_1_.refs_2_.refs_3_.refs_4_.refs_6_.refs_7_.refs_8_.refs_9_.refs_5_.refs_10_, ...), custom_call_target="tpu_custom_call" | custom-call | flops 2684354560 | bytes 7340032 | tf_op jit(solution)/shard_map/attend/pallas_call | solution.py:787
  251.1 2.3 broadcast_multiply_fusion
  253.4 5.6 multiply_reduce_fusion.1
  264.7 66.7 %gather_rows.3 = (bf16[2048,2048]{1,0:T(8,128)(2,1)}, bf16[2048,2176]{1,0:T(8,128)(2,1)}) custom-call(bf16[256,2048]{1,0:T(8,128)(2,1)} %multiply_convert_fusion.refs_0_, bf16[256,2176]{1,0:T(8,128)(2,1)} %copy-done.13, bf16[256,2176]{1,0:T(8,128)(2,1)} %collective-permute-done.refs_2_, bf16[256,2176]{1,0:T(8,128)(2,1)} %collective-permute-done.1.refs_3_), custom_call_target="tpu_custom_call" | custom-call | bytes 67108864 | tf_op jit(solution)/shard_map/gather_rows/pallas_call | solution.py:262
  331.4 6.7 fusion.12.refs_3_
  338.2 3.2 fusion.13.refs_2_
  341.6 41.2 %feed.2 = (bf16[2048,2176]{1,0:T(8,128)(2,1)}, bf16[2048,2304]{1,0:T(8,128)(2,1)}, f32[512,384]{1,0:T(8,128)}) custom-call(bf16[2048,2048]{1,0:T(8,128)(2,1)} %get-tuple-element.71.refs_0_, bf16[2048,2176]{1,0:T(8,128)(2,1)} %get-tuple-element.72.refs_1_, bf16[2048,128]{1,0:T(8,128)(2,1)} %fusion.13.refs_2_, bf16[2048,128]{1,0:T(8,128)(2,1)} %fusion.12.refs_3_, ...), custom_call_target="tpu_custom_call" | custom-call | flops 27380416512 | bytes 65404928 | tf_op jit(solution)/shard_map/feed/pallas_call | solution.py:961
  382.9 23.8 %collective-permute-done.4.refs_7_ = bf16[384,2176]{1,0:T(8,128)(2,1)S(1)} collective-permute-done((bf16[384,2176]{1,0:T(8,128)(2,1)}, bf16[384,2176]{1,0:T(8,128)(2,1)S(1)}, u32[]{:S(2)}, u32[]{:S(2)}) %collective-permute-start.4) | collective-permute-done | bytes 1671200 | tf_op jit(solution)/shard_map/ppermute | solution.py:29
  407.9 42.3 %feed.3 = (bf16[2048,2176]{1,0:T(8,128)(2,1)}, bf16[2048,2304]{1,0:T(8,128)(2,1)}, f32[512,384]{1,0:T(8,128)}) custom-call(bf16[2048,2048]{1,0:T(8,128)(2,1)} %get-tuple-element.71.refs_0_, bf16[2048,2176]{1,0:T(8,128)(2,1)} %get-tuple-element.72.refs_1_, bf16[2048,128]{1,0:T(8,128)(2,1)} %fusion.13.refs_2_, bf16[2048,128]{1,0:T(8,128)(2,1)} %fusion.12.refs_3_, ...), custom_call_target="tpu_custom_call" | custom-call | flops 27380416512 | bytes 65404928 | tf_op jit(solution)/shard_map/feed/pallas_call | solution.py:961
  450.2 66.9 %reduce_rows.2 = (f32[256,2304]{1,0:T(8,128)}, f32[256,2176]{1,0:T(8,128)}, bf16[256,2176]{1,0:T(8,128)(2,1)}, f32[256,2176]{1,0:T(8,128)}, bf16[256,2176]{1,0:T(8,128)(2,1)}) custom-call(bf16[2048,2304]{1,0:T(8,128)(2,1)} %get-tuple-element.80.refs_0_, bf16[2048,2176]{1,0:T(8,128)(2,1)} %get-tuple-element.81.refs_1_), custom_call_target="tpu_custom_call" | custom-call | bytes 293601280 | tf_op jit(solution)/shard_map/reduce_rows/pallas_call | solution.py:415
  517.2 2.9 fusion.52.refs_7_
  520.1 2.5 fusion.50.refs_6_
  524.1 2.7 multiply_reduce_fusion
  527.3 6.9 fusion.34
  537.3 2.2 collective-permute-start.6
  541.0 26.8 %attend_back.1 = (bf16[256,2048]{1,0:T(8,128)(2,1)}, f32[2,256,1024]{2,1,0:T(8,128)}, bf16[4,2,256,1024]{3,2,1,0:T(8,128)(2,1)}) custom-call(bf16[256,2048]{1,0:T(8,128)(2,1)} %get-tuple-element.63.refs_0_, bf16[256,2048]{1,0:T(8,128)(2,1)} %fusion.7.refs_1_, ...), custom_call_target="tpu_custom_call" | custom-call | flops 6710886400 | bytes 24117248 | tf_op jit(solution)/shard_map/attend_back/pallas_call | solution.py:860
  567.7 2.5 fusion.53.refs_4_
  570.3 1.7 convert_add_fusion.1.refs_1_
  572.7 1.7 convert_add_fusion.2.refs_0_
  574.4 89.3 %context_back.1 = (f32[2,256,1024]{2,1,0:T(8,128)}, f32[128,2176]{1,0:T(8,128)}, f32[128,2176]{1,0:T(8,128)}, f32[128,384]{1,0:T(8,128)}, f32[128,384]{1,0:T(8,1...) custom-call(bf16[4,2,256,1024]{3,2,1,0:T(8,128)(2,1)} %get-tuple-element.83.away, ...), custom_call_target="tpu_custom_call" | custom-call | bytes 33554432 | tf_op jit(solution)/shard_map/context_back/pallas_call | solution.py:660
  668.5 2.1 fusion.30.refs_1_
  670.5 10.0 %fusion.31 = f32[256,2176]{1,0:T(8,128)S(1)} fusion(bf16[4096,2176]{1,0:T(8,128)(2,1)} %get-tuple-element.62.w_ref, bf16[256,1024]{1,0:T(8,128)(2,1)S(1)} %fusion.32, bf16[256,1024]{1,0:T(8,128)(2,1)S(1)} %fusion.29, bf16[256,2048]{1,0:T(8,128)(2,1)S(1)} %copy-done.71), kind=kOutput, calls=%fused_computation.61 | convolution fusion | flops 4569694208 | bytes 22151168 | tf_op jit(solution)/shard_map/dot_general | solution.py:39
  682.1 2.5 fusion.15
  685.9 1.6 fusion.9.refs_0_
  689.7 29.3 %reduce_rows.3 = (f32[64,128]{1,0:T(8,128)}, f32[128,128]{1,0:T(8,128)}, f32[64,128]{1,0:T(8,128)}) custom-call(f32[2048,128]{1,0:T(8,128)} %fusion.9.refs_0_, f32[4096,128]{1,0:T(8,128)} %fusion.30.refs_1_, f32[2048,128]{1,0:T(8,128)} %fusion.56.refs_2_), custom_call_target="tpu_custom_call" | custom-call | bytes 33554432 | tf_op jit(solution)/shard_map/reduce_rows/pallas_call | solution.py:415
  719.7 4.4 fusion.18
  (219 shorter events, 46.8 us)
Async XLA Ops:
  7.4 243.7 %copy-start.23 = (pred[2048,128]{1,0:T(32,128)(4,1)}, pred[2048,128]{1,0:T(32,128)(4,1)S(1)}, u32[]{:S(2)}) copy-start(pred[2048,128]{1,0:T(32,128)(4,1)S(1)} %broadcast_compare_fusion) | copy-start | bytes 786436
  16.4 143.3 %copy-start.4 = (bf16[256,2048]{1,0:T(8,128)(2,1)S(1)}, bf16[256,2048]{1,0:T(8,128)(2,1)}, u32[]{:S(2)}) copy-start(bf16[256,2048]{1,0:T(8,128)(2,1)} %param.41) | copy-start | bytes 3145732
  161.4 103.3 %collective-permute-start = (bf16[256,2176]{1,0:T(8,128)(2,1)S(1)}, bf16[256,2176]{1,0:T(8,128)(2,1)}, u32[]{:S(2)}, u32[]{:S(2)}) collective-permute-start(bf16[256,2176]{1,0:T(8,128)(2,1)S(1)} %pad_maximum_fusion.2.refs_1_), channel_id=1, source_target_pairs={{0,2},{1,3},{2,0},{3,1},{4,6},{5,7},{6,4},{7,5},{8,10},{9,11},{10,... | collective-permute-start | bytes 3342344 | tf_op jit(solution)/shard_map/ppermute | solution.py:29
  163.0 101.7 %collective-permute-start.1 = (bf16[256,2176]{1,0:T(8,128)(2,1)S(1)}, bf16[256,2176]{1,0:T(8,128)(2,1)}, u32[]{:S(2)}, u32[]{:S(2)}) collective-permute-start(bf16[256,2176]{1,0:T(8,128)(2,1)S(1)} %pad_maximum_fusion.2.refs_1_), channel_id=1, source_target_pairs={{0,4},{1,5},{2,6},{3,7},{4,0},{5,1},{6,2},{7,3},{8,12},{9,13},{10,... | collective-permute-start | bytes 3342344 | tf_op jit(solution)/shard_map/ppermute | solution.py:29
  165.6 14.9 %copy-start.35 = (bf16[256,128]{1,0:T(8,128)(2,1)}, bf16[256,128]{1,0:T(8,128)(2,1)S(1)}, u32[]{:S(2)}) copy-start(bf16[256,128]{1,0:T(8,128)(2,1)S(1)} %fusion.25) | copy-start | bytes 196612
  180.5 53.1 %copy-start.62 = (s32[15]{0:T(128)S(1)}, s32[15]{0:T(128)}, u32[]{:S(2)}) copy-start(s32[15]{0:T(128)} %copy-done.61) | copy-start | bytes 184
  180.5 53.1 %copy-start.64 = (s32[15,1]{0,1:T(1,128)S(1)}, s32[15,1]{0,1:T(1,128)}, u32[]{:S(2)}) copy-start(s32[15,1]{0,1:T(1,128)} %copy-done.63) | copy-start | bytes 184
  180.6 53.0 %copy-start.66 = (s32[15]{0:T(128)S(1)}, s32[15]{0:T(128)}, u32[]{:S(2)}) copy-start(s32[15]{0:T(128)} %copy-done.65) | copy-start | bytes 184
  180.6 53.8 %copy-start.60 = (bf16[2048]{0:T(1024)(128)(2,1)S(1)}, bf16[2048]{0:T(1024)(128)(2,1)}, u32[]{:S(2)}) copy-start(bf16[2048]{0:T(1024)(128)(2,1)} %param.23) | copy-start | bytes 12292
  234.3 24.7 %copy-start.40 = (f32[2048]{0:T(1024)}, f32[2048]{0:T(1024)S(1)}, u32[]{:S(2)}) copy-start(f32[2048]{0:T(1024)S(1)} %convert_element_type.80) | copy-start | bytes 24580
  234.3 16.7 %copy-start.19 = (bf16[2048,128]{1,0:T(8,128)(2,1)S(1)}, bf16[2048,128]{1,0:T(8,128)(2,1)}, u32[]{:S(2)}) copy-start(bf16[2048,128]{1,0:T(8,128)(2,1)} %get-tuple-element.66) | copy-start | bytes 1572868
  259.0 5.7 copy-start.55
  261.5 69.9 %copy-start.68 = (s32[128]{0:T(128)S(1)}, s32[128]{0:T(128)}, u32[]{:S(2)}) copy-start(s32[128]{0:T(128)} %and_select_fusion) | copy-start | bytes 1540
  261.5 79.9 %collective-permute-start.2 = (bf16[384,2176]{1,0:T(8,128)(2,1)S(1)}, bf16[384,2176]{1,0:T(8,128)(2,1)}, u32[]{:S(2)}, u32[]{:S(2)}) collective-permute-start(bf16[384,2176]{1,0:T(8,128)(2,1)S(1)} %copy-done.22), channel_id=1, source_target_pairs={{0,16},{1,17},{2,18},{3,19},{4,20},{5,21},{6,22},{7,23},{8,24},{9,... | collective-permute-start | bytes 5013512 | tf_op jit(solution)/shard_map/ppermute | solution.py:29
  262.6 79.0 %collective-permute-start.5 = (bf16[384,2176]{1,0:T(8,128)(2,1)}, bf16[384,2176]{1,0:T(8,128)(2,1)}, u32[]{:S(2)}, u32[]{:S(2)}) collective-permute-start(bf16[384,2176]{1,0:T(8,128)(2,1)} %get-tuple-element.76.refs_5_), channel_id=1, source_target_pairs={{0,8},{1,9},{2,10},{3,11},{4,12},{5,13},{6,14},{7,15},{8,0},{9,1},... | collective-permute-start | bytes 5013512 | tf_op jit(solution)/shard_map/ppermute | solution.py:29
  263.2 119.7 %collective-permute-start.3 = (bf16[384,2176]{1,0:T(8,128)(2,1)S(1)}, bf16[384,2176]{1,0:T(8,128)(2,1)}, u32[]{:S(2)}, u32[]{:S(2)}) collective-permute-start(bf16[384,2176]{1,0:T(8,128)(2,1)S(1)} %copy-done.22), channel_id=1, source_target_pairs={{0,8},{1,9},{2,10},{3,11},{4,12},{5,13},{6,14},{7,15},{8,0},{9,1},... | collective-permute-start | bytes 5013512 | tf_op jit(solution)/shard_map/ppermute | solution.py:29
  331.4 6.8 copy-start.32
  331.4 6.8 copy-start.69
  341.4 65.3 %collective-permute-start.4 = (bf16[384,2176]{1,0:T(8,128)(2,1)}, bf16[384,2176]{1,0:T(8,128)(2,1)S(1)}, u32[]{:S(2)}, u32[]{:S(2)}) collective-permute-start(bf16[384,2176]{1,0:T(8,128)(2,1)} %collective-permute-done.2.refs_5_), channel_id=1, source_target_pairs={{0,8},{1,9},{2,10},{3,11},{4,12},{5,13},{6,14},{7,15},{8,0},{9,1},... | collective-permute-start | bytes 5013512 | tf_op jit(solution)/shard_map/ppermute | solution.py:29
  517.2 5.5 copy-start.33
  527.2 7.0 copy-start.3
  527.3 7.0 copy-start.37
  535.8 34.5 %collective-permute-start.7 = (bf16[256,2176]{1,0:T(8,128)(2,1)}, bf16[256,2176]{1,0:T(8,128)(2,1)S(1)}, u32[]{:S(2)}, u32[]{:S(2)}) collective-permute-start(bf16[256,2176]{1,0:T(8,128)(2,1)} %get-tuple-element.88), channel_id=1, source_target_pairs={{0,4},{1,5},{2,6},{3,7},{4,0},{5,1},{6,2},{7,3},{8,12},{9,13},{10,... | collective-permute-start | bytes 3342344 | tf_op jit(solution)/shard_map/ppermute | solution.py:29
  537.3 34.7 %collective-permute-start.6 = (bf16[256,2176]{1,0:T(8,128)(2,1)}, bf16[256,2176]{1,0:T(8,128)(2,1)S(1)}, u32[]{:S(2)}, u32[]{:S(2)}) collective-permute-start(bf16[256,2176]{1,0:T(8,128)(2,1)} %get-tuple-element.86), channel_id=1, source_target_pairs={{0,2},{1,3},{2,0},{3,1},{4,6},{5,7},{6,4},{7,5},{8,10},{9,11},{10,... | collective-permute-start | bytes 3342344 | tf_op jit(solution)/shard_map/ppermute | solution.py:29
  541.0 26.8 %copy-start.10 = (bf16[256,2048]{1,0:T(8,128)(2,1)S(1)}, bf16[256,2048]{1,0:T(8,128)(2,1)}, u32[]{:S(2)}) copy-start(bf16[256,2048]{1,0:T(8,128)(2,1)} %attend.1) | copy-start | bytes 3145732
  670.5 10.0 %copy-start.8 = (bf16[256,2048]{1,0:T(8,128)(2,1)S(1)}, bf16[256,2048]{1,0:T(8,128)(2,1)}, u32[]{:S(2)}) copy-start(bf16[256,2048]{1,0:T(8,128)(2,1)} %copy-done.7) | copy-start | bytes 3145732
  670.5 10.0 %copy-start.25 = (pred[2048,128]{1,0:T(32,128)(4,1)S(1)}, pred[2048,128]{1,0:T(32,128)(4,1)}, u32[]{:S(2)}) copy-start(pred[2048,128]{1,0:T(32,128)(4,1)} %copy-done.23) | copy-start | bytes 786436
  719.7 5.6 copy-start.51
  719.7 6.3 copy-start.50
  719.7 6.9 copy-start.49
  719.7 7.5 %copy-start.48 = (f32[64,128]{1,0:T(8,128)S(1)}, f32[64,128]{1,0:T(8,128)}, u32[]{:S(2)}) copy-start(f32[64,128]{1,0:T(8,128)} %get-tuple-element.159) | copy-start | bytes 98308
  719.7 8.1 %copy-start.52 = (f32[64,128]{1,0:T(8,128)S(1)}, f32[64,128]{1,0:T(8,128)}, u32[]{:S(2)}) copy-start(f32[64,128]{1,0:T(8,128)} %get-tuple-element.162) | copy-start | bytes 98308
  (48 other events, 126.1 us)
